TPU v7x, 16 devices: a whole 2x2x2 slice. The times are simulated.
16 devices in a mesh: z: 2 (over z), y: 2 (over y), x: 4 (over x, core).
Axes of the slice: x: 2, y: 2, z: 2, core: 2. Of those that a mesh axis runs over, the one named last changes fastest.
Arguments:
- atom_pos: float32 [11664, 3], P(('z', 'y', 'x'))
- atom_vel: float32 [11664, 3], P(('z', 'y', 'x'))
- atom_frc: float32 [11664, 3], P(('z', 'y', 'x'))
- atom_id: int32 [11664], P(('z', 'y', 'x'))
- atom_ok: int32 [11664], P(('z', 'y', 'x'))
- brick_side: float32 [], replicated
Outputs:
- output 1: float32 [11664, 3], P(('z', 'y', 'x'))
- output 2: float32 [11664, 3], P(('z', 'y', 'x'))
- output 3: float32 [11664, 3], P(('z', 'y', 'x'))
- output 4: int32 [11664], P(('z', 'y', 'x'))
- output 5: int32 [11664], P(('z', 'y', 'x'))
- output 6: float32 [], replicated
All inputs are finite; a program needn't handle non-finite values.
Results may differ from a plain program's by a relative error of at most 0.001.
Values sent between devices are 32-bit elements.
A program may use at most 1 GiB of HBM per device.

v0:
```python
import jax
import jax.numpy as jnp
from jax import lax
from jax.experimental import pallas as pl
from jax.experimental.pallas import tpu as pltpu
from jax.sharding import PartitionSpec as P

DT = 0.005
RC = 2.5
UPC = -48.0 * RC ** -13 + 24.0 * RC ** -7
MESH_AXES = ("z", "y", "x")
MESH = pl.DeviceIdType.MESH
NZ, NY, NX = 2, 2, 4
CAP = 729
LANES = 128
BLOCKS = 6
WIDE = BLOCKS * LANES
MOVE_CAP = CAP // 100
FAR_OWN = 1.0e4
FAR_OTHER = -1.0e4
NOWHERE = 1.0e9
PEERS = [(dz, dy, dx) for dz in range(NZ) for dy in range(NY) for dx in range(NX)][1:]
GROUPS = [(1, 1, 1), (-1, 1, 1), (1, 1, 0), (-1, 1, 0), (1, 0, 1), (-1, 0, 1), (1, 0, 0), (-1, 0, 0), (0, 1, 1), (0, 1, 0), (0, 0, 1)]
N_GROUPS = len(GROUPS)
DISTANT = [(2, 1, 1), (2, 1, 0), (2, 0, 1), (2, 0, 0)]
N_PACKETS = N_GROUPS + len(DISTANT)


def lane_plan():
    starts, base = [], {}
    block, lane = 0, 0
    for index, (gx, gy, gz) in enumerate(GROUPS):
        if index == 8:
            block, lane = 1, 0
        dirs = [(gx, sy, sz) for sz in ((-1, 1) if gz else (0,)) for sy in ((-1, 1) if gy else (0,))]
        starts.append((block, lane, lane + MOVE_CAP * len(dirs)))
        for dx, dy, dz in dirs:
            base[(dz + 1) * 9 + (dy + 1) * 3 + dx + 1] = block * LANES + lane
            lane += MOVE_CAP
    return starts, base


LANE_STARTS, LANE_BASE = lane_plan()
STAY = 13


def split3(values):
    hi = values.astype(jnp.bfloat16).astype(jnp.float32)
    rest = values - hi
    mid = rest.astype(jnp.bfloat16).astype(jnp.float32)
    return jnp.concatenate([hi, mid, rest - mid], axis=0).astype(jnp.bfloat16)


def join3(parts):
    rows = parts.shape[0] // 3
    return (parts[0:rows] + parts[rows:2 * rows]) + parts[2 * rows:3 * rows]


def dot_nt(a, b):
    return lax.dot_general(a, b, (((1,), (1,)), ((), ())), preferred_element_type=jnp.float32)


def dot_nn(a, b):
    return lax.dot_general(a, b, (((1,), (0,)), ((), ())), preferred_element_type=jnp.float32)


def my_coords():
    return lax.axis_index("z"), lax.axis_index("y"), lax.axis_index("x")


def peer_id(coords, offset):
    mz, my, mx = coords
    return (lax.rem(mz + offset[0], NZ), lax.rem(my + offset[1], NY), lax.rem(mx + offset[2] + NX, NX))


def entry_signals(coords):
    barrier = pltpu.get_barrier_semaphore()
    for offset in PEERS:
        pl.semaphore_signal(barrier, inc=1, device_id=peer_id(coords, offset), device_id_type=MESH)
    return barrier


def exchange_kernel(brick_ref, pos_ref, vel_ref, frc_ref, id_ref, ok_ref, gat_ref, pkt_ref, own_ref, raw, ids_in, oks_in, pad_ref, int_ref, send_pos, send_pkt, in_sem, pos_send_sem, pos_recv_sem, pkt_send_sem, pkt_recv_sem):
    coords = my_coords()
    fetches = [pltpu.make_async_copy(src, dst, in_sem.at[index]) for index, (src, dst) in enumerate(((pos_ref, raw.at[0]), (vel_ref, raw.at[1]), (frc_ref, raw.at[2]), (id_ref, ids_in), (ok_ref, oks_in)))]
    for fetch in fetches:
        fetch.start()
    barrier = entry_signals(coords)
    brick = brick_ref[0]
    tail = slice(WIDE - LANES, WIDE)
    pad_ref[:, :, tail] = jnp.zeros((3, 4, LANES), jnp.float32)
    int_ref[:, tail] = jnp.zeros((2, LANES), jnp.int32)
    for fetch in fetches:
        fetch.wait()
    for index in range(3):
        pad_ref[index, 0:3, 0:CAP] = raw[index]
    int_ref[0:1, 0:CAP] = ids_in[...].reshape(1, CAP)
    int_ref[1:2, 0:CAP] = oks_in[...].reshape(1, CAP)
    owned = int_ref[1:2, :] > 0
    moved, half, code = [], [], jnp.zeros((1, WIDE), jnp.int32)
    for axis, (mine, size, weight) in enumerate(((coords[2], NX, 1), (coords[1], NY, 3), (coords[0], NZ, 9))):
        box = brick * float(size)
        low = mine.astype(jnp.float32) * brick
        high = (mine + 1).astype(jnp.float32) * brick
        half_v = pad_ref[1, axis:axis + 1, :] + (0.5 * DT) * pad_ref[2, axis:axis + 1, :]
        drift = pad_ref[0, axis:axis + 1, :] + DT * half_v
        step = jnp.where(drift >= high, 2, jnp.where(drift < low, 0, 1))
        code = code + step * weight
        wrapped = jnp.where(drift < 0.0, drift + box, jnp.where(drift >= box, drift - box, drift))
        moved.append(wrapped)
        half.append(half_v)
    code = jnp.where(owned, code, -1)
    for axis in range(3):
        for block in range(8):
            if block < BLOCKS:
                lanes = slice(block * LANES, (block + 1) * LANES)
                send_pos[axis, block:block + 1, :] = jnp.where(owned[:, lanes], moved[axis][:, lanes], NOWHERE)
            else:
                send_pos[axis, block:block + 1, :] = jnp.full((1, LANES), NOWHERE, jnp.float32)
    ids = int_ref[0:1, :]
    id_hi = (lax.shift_right_logical(ids, 16) + 1).astype(jnp.float32)
    id_lo = (ids & 65535).astype(jnp.float32)
    data = jnp.concatenate(moved + half + [id_hi, id_lo], axis=0)
    member = (jnp.broadcast_to(code, (32, WIDE)) == lax.broadcasted_iota(jnp.int32, (32, WIDE), 0)).astype(jnp.float32)
    tri = (lax.broadcasted_iota(jnp.int32, (LANES, LANES), 0) < lax.broadcasted_iota(jnp.int32, (LANES, LANES), 1)).astype(jnp.bfloat16)
    codes = lax.broadcasted_iota(jnp.int32, (32, LANES), 0)
    running = jnp.zeros((32, LANES), jnp.float32)
    for move, first in LANE_BASE.items():
        running = jnp.where(codes == move, float(first), running)
    slots = []
    for block in range(BLOCKS):
        part = member[:, block * LANES:(block + 1) * LANES]
        before = dot_nn(part.astype(jnp.bfloat16), tri)
        slots.append(jnp.sum(part * (before + running), axis=0, keepdims=True))
        running = running + jnp.sum(part, axis=1, keepdims=True)
    slot = jnp.concatenate(slots, axis=1)
    stay = code == STAY
    mover_slot = jnp.where(owned & jnp.logical_not(stay), slot, -1.0).astype(jnp.int32)
    pick = (lax.broadcasted_iota(jnp.int32, (2 * LANES, WIDE), 0) == mover_slot).astype(jnp.float32).astype(jnp.bfloat16)
    packet = join3(dot_nt(split3(data), pick))
    send_pkt[0] = packet[:, 0:LANES]
    send_pkt[1] = packet[:, LANES:2 * LANES]
    own_ref[0:8, :] = data
    own_ref[8:16, :] = jnp.concatenate([jnp.where(stay, slot, -1.0), jnp.zeros((7, WIDE), jnp.float32)], axis=0)
    pl.semaphore_wait(barrier, len(PEERS))
    copies = []
    for index, (gx, gy, gz) in enumerate(GROUPS + DISTANT):
        peer = peer_id(coords, (gz, gy, gx))
        if index < N_GROUPS:
            copies.append(pltpu.make_async_remote_copy(src_ref=send_pos, dst_ref=gat_ref.at[index], send_sem=pos_send_sem.at[index], recv_sem=pos_recv_sem.at[index], device_id=peer, device_id_type=MESH))
            copies[-1].start()
        block = LANE_STARTS[index][0] if index < N_GROUPS else 0
        copies.append(pltpu.make_async_remote_copy(src_ref=send_pkt.at[block], dst_ref=pkt_ref.at[index], send_sem=pkt_send_sem.at[index], recv_sem=pkt_recv_sem.at[index], device_id=peer, device_id_type=MESH))
        copies[-1].start()
    gat_ref[N_GROUPS] = send_pos[...]
    for copy in copies:
        copy.wait()


CAND_ROWS = 8 * (N_GROUPS + 1) + 8
MAX_ROWS = BLOCKS + CAND_ROWS
QUAD = 4


def force_kernel(brick_ref, gat_ref, pkt_ref, own_ref, pos_out, vel_out, frc_out, id_out, ok_out, eng_out, others, mine, acc, sorted_ref):
    mz, my, mx = my_coords()
    brick = brick_ref[0]
    half_l = 0.5 * brick
    reach = half_l + RC
    sizes = (NX, NY, NZ)
    centre = [(index.astype(jnp.float32) + 0.5) * brick for index in (mx, my, mz)]
    box = [brick * float(size) for size in sizes]
    lane_1 = lax.broadcasted_iota(jnp.int32, (1, LANES), 1)

    arrived = []
    for block in range(2):
        total = jnp.zeros((8, LANES), jnp.float32)
        for index in range(N_GROUPS):
            where_block, first, last = LANE_STARTS[index]
            if where_block == block:
                total = total + jnp.where((lane_1 >= first) & (lane_1 < last), pkt_ref[index], 0.0)
        arrived.append(total)
    arr = jnp.concatenate(arrived, axis=1)
    data = jnp.concatenate([own_ref[0:8, :], arr], axis=1)
    int_max = 2147483647
    ids = lax.shift_left(data[6:7].astype(jnp.int32) - 1, 16) + data[7:8].astype(jnp.int32)
    stay_rank = own_ref[8:9, :]
    stay = stay_rank >= 0.0
    arr_ok = arr[6:7] > 0.5
    arr_id = jnp.where(arr_ok, ids[:, WIDE:], int_max)
    own_id = jnp.where(stay, ids[:, :WIDE], int_max)
    arr_col = jnp.transpose(jnp.broadcast_to(arr_id, (8, 2 * LANES)), (1, 0))[:, 0:1]
    own_col = jnp.transpose(jnp.broadcast_to(own_id, (8, WIDE)), (1, 0))[:, 0:1]
    all_id = jnp.concatenate([own_id, arr_id], axis=1)
    arr_before = jnp.sum((arr_col < all_id).astype(jnp.float32), axis=0, keepdims=True)
    stay_before = jnp.sum((own_col < arr_id).astype(jnp.float32), axis=0, keepdims=True)
    rank = jnp.concatenate([jnp.where(stay, stay_rank + arr_before[:, :WIDE], -1.0), jnp.where(arr_ok, stay_before + arr_before[:, WIDE:], -1.0)], axis=1).astype(jnp.int32)
    n_own = jnp.sum((rank >= 0).astype(jnp.float32)).astype(jnp.int32)
    parts = split3(data)
    for block in range(BLOCKS):
        pick = (lax.broadcasted_iota(jnp.int32, (LANES, WIDE + 2 * LANES), 0) + block * LANES == rank).astype(jnp.float32).astype(jnp.bfloat16)
        sorted_ref[block] = join3(dot_nt(parts, pick))
    for block in range(BLOCKS):
        valid = lane_1 + block * LANES < n_own
        for axis in range(3):
            rel = sorted_ref[block, axis:axis + 1, :] - centre[axis]
            others[axis, block] = jnp.broadcast_to(jnp.where(valid, rel, FAR_OTHER), (8, LANES))
            column = jnp.transpose(jnp.broadcast_to(jnp.where(valid, rel, FAR_OWN), (8, LANES)), (1, 0))[:, 0:1]
            mine[axis, pl.ds(block * 16, 16)] = jnp.broadcast_to(column, (LANES, LANES)).reshape(16, 8, LANES)
    own_rows = lax.div(n_own + (LANES - 1), LANES)

    rel = []
    for axis in range(3):
        distant = [jnp.where(pkt_ref[N_GROUPS + k, 6:7, :] > 0.5, pkt_ref[N_GROUPS + k, axis:axis + 1, :], NOWHERE) for k in range(len(DISTANT))]
        values = jnp.concatenate([gat_ref[:, axis].reshape(8 * (N_GROUPS + 1), LANES)] + distant + [jnp.full((4, LANES), NOWHERE, jnp.float32)], axis=0) - centre[axis]
        values = jnp.where(values > 0.5 * box[axis], values - box[axis], jnp.where(values < -0.5 * box[axis], values + box[axis], values))
        rel.append(values)
    near = (jnp.abs(rel[0]) < reach) & (jnp.abs(rel[1]) < reach) & (jnp.abs(rel[2]) < reach)
    inside = (jnp.abs(rel[0]) < half_l) & (jnp.abs(rel[1]) < half_l) & (jnp.abs(rel[2]) < half_l)
    ghost = (near & jnp.logical_not(inside)).astype(jnp.float32).astype(jnp.bfloat16)
    row_i = lax.broadcasted_iota(jnp.int32, (LANES, LANES), 0)
    col_i = lax.broadcasted_iota(jnp.int32, (LANES, LANES), 1)
    cum = dot_nn(ghost, (row_i <= col_i).astype(jnp.bfloat16)).astype(jnp.int32)
    count = dot_nn(ghost, jnp.ones((LANES, LANES), jnp.bfloat16))
    base = dot_nn((col_i < row_i).astype(jnp.bfloat16)[:CAND_ROWS, :CAND_ROWS], count.astype(jnp.bfloat16)).astype(jnp.int32)
    count = count.astype(jnp.int32)
    n_ghost = jnp.max(base[CAND_ROWS - 8:] + count[CAND_ROWS - 8:])
    lane_c = lax.broadcasted_iota(jnp.int32, (CAND_ROWS, LANES), 1)
    place = (lane_c - base) & (LANES - 1)
    source = jnp.zeros((CAND_ROWS, LANES), jnp.int32)
    for step in (64, 32, 16, 8, 4, 2, 1):
        probe = jnp.take_along_axis(cum, source + (step - 1), axis=1)
        source = jnp.where(probe <= place, source + step, source)
    target = jnp.where(place < count, lax.shift_right_logical(base + place, 7), -1)
    packed = [jnp.take_along_axis(values, source, axis=1) for values in rel]
    ghost_rows = lax.div(n_ghost + (LANES - 1), LANES)

    def pack_row(row, carry):
        hit = target == row
        filled = lane_1 + row * LANES < n_ghost
        for axis in range(3):
            values = jnp.sum(jnp.where(hit, packed[axis], 0.0), axis=0, keepdims=True)
            others[axis, own_rows + row] = jnp.broadcast_to(jnp.where(filled, values, FAR_OTHER), (8, LANES))
        return carry

    lax.fori_loop(0, ghost_rows, pack_row, 0)
    rows = own_rows + ghost_rows

    rc2 = jnp.full((8, LANES), RC * RC + 0.0 * brick, jnp.float32)
    kappa = UPC / 48.0

    def radial(dist_sq):
        inv_r = lax.rsqrt(dist_sq)
        inv_2 = inv_r * inv_r
        inv_4 = inv_2 * inv_2
        term = inv_4 * inv_2 - 0.5
        tail = kappa * inv_r
        return term * (inv_4 * inv_4) + tail, term * term, tail * dist_sq

    cut_f, cut_a, cut_h = radial(rc2)
    own_minus_lane = lax.broadcasted_iota(jnp.int32, (8, LANES), 0) - lax.broadcasted_iota(jnp.int32, (8, LANES), 1)
    zero = jnp.zeros((8, LANES), jnp.float32)

    def pair_loops(wrap):
        inv_box = [1.0 / (brick * float(size)) for size in sizes]

        def quad(index, energy):
            first = index * QUAD
            own = [[mine[axis, first + k] for axis in range(3)] for k in range(QUAD)]
            self_row = lax.div(first, 16)

            def one_row(row, sums, with_self):
                other = [others[axis, row] for axis in range(3)]
                force, sum_a, sum_h = list(sums[:-2]), sums[-2], sums[-1]
                for k in range(QUAD):
                    delta = [own[k][axis] - other[axis] for axis in range(3)]
                    if wrap:
                        for axis in (1, 2):
                            delta[axis] = delta[axis] - box[axis] * jnp.floor(delta[axis] * inv_box[axis] + 0.5)
                    dist_sq = delta[0] * delta[0] + delta[1] * delta[1] + delta[2] * delta[2]
                    if with_self:
                        dist_sq = jnp.where(own_minus_lane == row * LANES - (first + k) * 8, rc2, dist_sq)
                    dist_sq = jnp.minimum(dist_sq, rc2)
                    scale, a, h = radial(dist_sq)
                    scale = scale - cut_f
                    for axis in range(3):
                        force[3 * k + axis] = force[3 * k + axis] + scale * delta[axis]
                    sum_a, sum_h = sum_a + a, sum_h + h
                return tuple(force) + (sum_a, sum_h)

            def other_row(count, sums):
                return one_row(count + (count >= self_row).astype(jnp.int32), sums, False)

            def two_rows(count, sums):
                return other_row(2 * count + 1, other_row(2 * count, sums))

            sums = one_row(self_row, (zero,) * (3 * QUAD + 2), True)
            twos = lax.div(rows - 1, 2)
            sums = lax.fori_loop(0, twos, two_rows, sums)
            sums = lax.fori_loop(2 * twos, rows - 1, other_row, sums)
            for k in range(QUAD):
                for axis in range(3):
                    acc[axis, first + k] = sums[3 * k + axis]
            n = QUAD * rows.astype(jnp.float32)
            return energy + (sums[-2] - n * cut_a) - 12.0 * (sums[-1] - n * cut_h)

        quads = lax.div(n_own + (8 * QUAD - 1), 8 * QUAD)
        energy = lax.fori_loop(0, quads, quad, zero)
        eng_out[...] = jnp.full((8, LANES), 2.0 * jnp.sum(energy), jnp.float32)

    pl.when(brick >= 2.0 * RC)(lambda: pair_loops(False))
    pl.when(brick < 2.0 * RC)(lambda: pair_loops(True))

    for block in range(BLOCKS):
        width = min(LANES, CAP - block * LANES)
        lanes = slice(block * LANES, block * LANES + width)
        valid = lane_1 + block * LANES < n_own
        rows_s = sorted_ref[block]
        for axis in range(3):
            turned = jnp.transpose(acc[axis, pl.ds(block * 16, 16)].reshape(LANES, LANES), (1, 0))
            force = jnp.where(valid, 48.0 * jnp.sum(turned, axis=0, keepdims=True), 0.0)
            frc_out[axis:axis + 1, lanes] = force[:, :width]
            vel_out[axis:axis + 1, lanes] = (rows_s[3 + axis:4 + axis] + (0.5 * DT) * force)[:, :width]
            pos_out[axis:axis + 1, lanes] = rows_s[axis:axis + 1, :width]
        new_id = lax.shift_left(rows_s[6:7].astype(jnp.int32) - 1, 16) + rows_s[7:8].astype(jnp.int32)
        id_out[lanes] = jnp.where(valid, new_id, 0)[:, :width].reshape(width)
        ok_out[lanes] = valid.astype(jnp.int32)[:, :width].reshape(width)


def energy_kernel(eng_ref, out_ref, slots, send_sem, recv_sem):
    coords = my_coords()
    mz, my, mx = coords
    barrier = entry_signals(coords)
    pl.semaphore_wait(barrier, len(PEERS))
    place = (mz * NY + my) * NX + mx
    copies = []
    for index, offset in enumerate(PEERS):
        copies.append(pltpu.make_async_remote_copy(src_ref=eng_ref, dst_ref=slots.at[place], send_sem=send_sem.at[index], recv_sem=recv_sem.at[index], device_id=peer_id(coords, offset), device_id_type=MESH))
        copies[-1].start()
    slots[place] = eng_ref[...]
    for copy in copies:
        copy.wait()
    total = slots[0]
    for index in range(1, NZ * NY * NX):
        total = total + slots[index]
    out_ref[0, 0] = jnp.max(total)


VMEM_SPEC = pl.BlockSpec(memory_space=pltpu.VMEM)
HBM_SPEC = pl.BlockSpec(memory_space=pltpu.HBM)
VMEM_LIMIT = 8 * 1024 * 1024
SMEM_SPEC = pl.BlockSpec(memory_space=pltpu.SMEM)


def solution(mesh):
    def local_step(atom_pos, atom_vel, atom_frc, atom_id, atom_ok, brick_side):
        f32 = jnp.float32
        brick = brick_side.reshape(1)
        n_dev = NZ * NY * NX
        gat, pkt, own = pl.pallas_call(
            exchange_kernel,
            out_shape=(jax.ShapeDtypeStruct((N_GROUPS + 1, 3, 8, LANES), f32), jax.ShapeDtypeStruct((N_PACKETS, 8, LANES), f32), jax.ShapeDtypeStruct((16, WIDE), f32)),
            in_specs=[SMEM_SPEC] + [HBM_SPEC] * 5,
            out_specs=(VMEM_SPEC,) * 3,
            scratch_shapes=[
                pltpu.VMEM((3, 3, CAP), f32),
                pltpu.VMEM((CAP,), jnp.int32),
                pltpu.VMEM((CAP,), jnp.int32),
                pltpu.VMEM((3, 4, WIDE), f32),
                pltpu.VMEM((2, WIDE), jnp.int32),
                pltpu.VMEM((3, 8, LANES), f32),
                pltpu.VMEM((2, 8, LANES), f32),
                pltpu.SemaphoreType.DMA((5,)),
                pltpu.SemaphoreType.DMA((N_GROUPS,)),
                pltpu.SemaphoreType.DMA((N_GROUPS,)),
                pltpu.SemaphoreType.DMA((N_PACKETS,)),
                pltpu.SemaphoreType.DMA((N_PACKETS,)),
            ],
            compiler_params=pltpu.CompilerParams(collective_id=0, has_side_effects=True, vmem_limit_bytes=VMEM_LIMIT),
            name="exchange",
        )(brick, *(pltpu.with_memory_space_constraint(value, pltpu.HBM) for value in (atom_pos.T, atom_vel.T, atom_frc.T, atom_id, atom_ok)))
        pos, vel, frc, ids, oks, eng = pl.pallas_call(
            force_kernel,
            out_shape=(jax.ShapeDtypeStruct((3, CAP), f32),) * 3 + (jax.ShapeDtypeStruct((CAP,), jnp.int32),) * 2 + (jax.ShapeDtypeStruct((8, LANES), f32),),
            in_specs=[SMEM_SPEC] + [VMEM_SPEC] * 3,
            out_specs=(VMEM_SPEC,) * 6,
            scratch_shapes=[
                pltpu.VMEM((3, MAX_ROWS, 8, LANES), f32),
                pltpu.VMEM((3, BLOCKS * 16, 8, LANES), f32),
                pltpu.VMEM((3, BLOCKS * 16, 8, LANES), f32),
                pltpu.VMEM((BLOCKS, 8, LANES), f32),
            ],
            compiler_params=pltpu.CompilerParams(vmem_limit_bytes=VMEM_LIMIT),
            name="forces",
        )(brick, gat, pkt, own)
        total = pl.pallas_call(
            energy_kernel,
            out_shape=jax.ShapeDtypeStruct((1, 1), f32),
            in_specs=[VMEM_SPEC],
            out_specs=SMEM_SPEC,
            scratch_shapes=[pltpu.VMEM((n_dev, 8, LANES), f32), pltpu.SemaphoreType.DMA((n_dev - 1,)), pltpu.SemaphoreType.DMA((n_dev - 1,))],
            compiler_params=pltpu.CompilerParams(collective_id=1, has_side_effects=True, vmem_limit_bytes=VMEM_LIMIT),
            name="energy",
        )(eng)
        return pos.T, vel.T, frc.T, ids, oks, total.reshape(())

    row_spec = P(MESH_AXES, None)
    id_spec = P(MESH_AXES)
    return jax.shard_map(local_step, mesh=mesh, in_specs=(row_spec, row_spec, row_spec, id_spec, id_spec, P()), out_specs=(row_spec, row_spec, row_spec, id_spec, id_spec, P()), check_vma=False)
```

profile of v0, /device:TPU:0, one launch (start us, length us, event | category | flops | bytes accessed | tf_op | source)
XLA Modules:
  0.0 27.6 jit_solution(868823263497696684)
XLA Ops:
  1.3 9.8 %exchange.1 = (f32[12,3,8,128]{3,2,1,0:T(8,128)S(1)}, f32[15,8,128]{2,1,0:T(8,128)S(1)}, f32[16,768]{1,0:T(8,128)S(1)}) custom-call(f32[1]{0:T(128)} %bitcast.8.brick_ref, f32[3,729]{1,0:T(4,128)} %bitcast.10, f32[3,729]{1,0:T(4,128)} %bitcast.11, f32[3,729]{1,0:T(4,128)} %bitcast.12, s32[729]{0:T(1024)} %id_ref.1, s32[729]{0:T(1024)} %ok_ref.1), custom_call_target="tpu_custom_call" | custom-call | tf_op jit(solution)/shard_map/exchange/pallas_call | solution.py:360
  11.1 6.4 %forces.1 = (f32[3,729]{1,0:T(4,128)}, f32[3,729]{1,0:T(4,128)}, f32[3,729]{1,0:T(4,128)}, s32[729]{0:T(1024)}, s32[729]{0:T(1024)}, /*index=5*/f32[8,128]{1,0:T(8,128)S(1)}) custom-call(f32[1]{0:T(128)} %bitcast.9.brick_ref, f32[12,3,8,128]{3,2,1,0:T(8,128)S(1)} %get-tuple-element.15.gat_ref, f32[15,8,128]{2,1,0:T(8,128)S(1)} %get-tuple-element.16.pkt_ref, ...), custom_call_target="tpu_custom_call" | custom-call | tf_op jit(solution)/shard_map/forces/pallas_call | solution.py:382
  17.5 8.4 %energy.1 = f32[1,1]{1,0:T(1,128)} custom-call(f32[8,128]{1,0:T(8,128)S(1)} %get-tuple-element.23.eng_ref), custom_call_target="tpu_custom_call" | custom-call | tf_op jit(solution)/shard_map/energy/pallas_call | solution.py:396
where the time goes:
time: 27.6 us
  Pallas kernels  24.6 us (89%)
  between operations  3.05 us (11%)
    pallas_call x1, Pallas kernels, local_step(): pl.pallas_call(exchange_kernel, out_shape=(jax.ShapeDtypeStruct((N_GROUPS...  9.82 us
    pallas_call x1, Pallas kernels, local_step(): pl.pallas_call(energy_kernel, out_shape=jax.ShapeDtypeStruct((1, 1), f32)...  8.39 us
    pallas_call x1, Pallas kernels, local_step(): pl.pallas_call(force_kernel, out_shape=(jax.ShapeDtypeStruct((3, CAP), f3...  6.38 us

commit v1 on v0

--- a/solution.py
+++ b/solution.py
@@ -159,10 +159,54 @@
 
 CAND_ROWS = 8 * (N_GROUPS + 1) + 8
 MAX_ROWS = BLOCKS + CAND_ROWS
+GROUPS_OWN = BLOCKS * 16
 QUAD = 4
-
-
-def force_kernel(brick_ref, gat_ref, pkt_ref, own_ref, pos_out, vel_out, frc_out, id_out, ok_out, eng_out, others, mine, acc, sorted_ref):
+FIXED_QUADS = 15
+FIXED_ROWS = 12
+
+
+def pair_tools(mine, others, rc2, wrap_box):
+    kappa = UPC / 48.0
+
+    def radial(dist_sq):
+        inv_r = lax.rsqrt(dist_sq)
+        inv_2 = inv_r * inv_r
+        inv_4 = inv_2 * inv_2
+        term = inv_4 * inv_2 - 0.5
+        tail = kappa * inv_r
+        return term * (inv_4 * inv_4) + tail, term * term, tail * dist_sq
+
+    cut_f, cut_a, cut_h = radial(rc2)
+    own_minus_lane = lax.broadcasted_iota(jnp.int32, (8, LANES), 0) - lax.broadcasted_iota(jnp.int32, (8, LANES), 1)
+
+    def load_own(first):
+        return [[mine[axis, first + k] for axis in range(3)] for k in range(QUAD)]
+
+    def one_row(own, first, row, sums, with_self):
+        other = [others[axis, row] for axis in range(3)]
+        force, sum_a, sum_h = list(sums[:-2]), sums[-2], sums[-1]
+        for k in range(QUAD):
+            delta = [own[k][axis] - other[axis] for axis in range(3)]
+            for axis, box, inv_box in wrap_box:
+                delta[axis] = delta[axis] - box * jnp.floor(delta[axis] * inv_box + 0.5)
+            dist_sq = delta[0] * delta[0] + delta[1] * delta[1] + delta[2] * delta[2]
+            if with_self:
+                dist_sq = jnp.where(own_minus_lane == row * LANES - (first + k) * 8, rc2, dist_sq)
+            dist_sq = jnp.minimum(dist_sq, rc2)
+            scale, a, h = radial(dist_sq)
+            scale = scale - cut_f
+            for axis in range(3):
+                force[3 * k + axis] = force[3 * k + axis] + scale * delta[axis]
+            sum_a, sum_h = sum_a + a, sum_h + h
+        return tuple(force) + (sum_a, sum_h)
+
+    def energy_of(sums, n_rows):
+        return (sums[-2] - (QUAD * n_rows) * cut_a) - 12.0 * (sums[-1] - (QUAD * n_rows) * cut_h)
+
+    return load_own, one_row, energy_of
+
+
+def prepare_kernel(brick_ref, gat_ref, pkt_ref, own_ref, sorted_ref, mine, others, acc, eng_ref):
     mz, my, mx = my_coords()
     brick = brick_ref[0]
     half_l = 0.5 * brick
@@ -199,15 +243,14 @@
     parts = split3(data)
     for block in range(BLOCKS):
         pick = (lax.broadcasted_iota(jnp.int32, (LANES, WIDE + 2 * LANES), 0) + block * LANES == rank).astype(jnp.float32).astype(jnp.bfloat16)
-        sorted_ref[block] = join3(dot_nt(parts, pick))
-    for block in range(BLOCKS):
+        rows_s = join3(jnp.transpose(dot_nt(pick, parts), (1, 0)))
+        sorted_ref[block] = rows_s
         valid = lane_1 + block * LANES < n_own
-        for axis in range(3):
-            rel = sorted_ref[block, axis:axis + 1, :] - centre[axis]
-            others[axis, block] = jnp.broadcast_to(jnp.where(valid, rel, FAR_OTHER), (8, LANES))
-            column = jnp.transpose(jnp.broadcast_to(jnp.where(valid, rel, FAR_OWN), (8, LANES)), (1, 0))[:, 0:1]
-            mine[axis, pl.ds(block * 16, 16)] = jnp.broadcast_to(column, (LANES, LANES)).reshape(16, 8, LANES)
-    own_rows = lax.div(n_own + (LANES - 1), LANES)
+        rel = jnp.concatenate([rows_s[axis:axis + 1] - centre[axis] for axis in range(3)] + [rows_s[3:8]], axis=0)
+        columns = jnp.transpose(jnp.where(valid, rel, FAR_OWN), (1, 0))
+        for axis in range(3):
+            others[axis, block] = jnp.broadcast_to(jnp.where(valid, rel[axis:axis + 1], 0.0), (8, LANES))
+            mine[axis, pl.ds(block * 16, 16)] = jnp.broadcast_to(columns[:, axis:axis + 1], (LANES, LANES)).reshape(16, 8, LANES)
 
     rel = []
     for axis in range(3):
@@ -222,9 +265,9 @@
     col_i = lax.broadcasted_iota(jnp.int32, (LANES, LANES), 1)
     cum = dot_nn(ghost, (row_i <= col_i).astype(jnp.bfloat16)).astype(jnp.int32)
     count = dot_nn(ghost, jnp.ones((LANES, LANES), jnp.bfloat16))
-    base = dot_nn((col_i < row_i).astype(jnp.bfloat16)[:CAND_ROWS, :CAND_ROWS], count.astype(jnp.bfloat16)).astype(jnp.int32)
+    base = dot_nn((col_i < row_i).astype(jnp.bfloat16)[:CAND_ROWS, :CAND_ROWS], count.astype(jnp.bfloat16)).astype(jnp.int32) + n_own
     count = count.astype(jnp.int32)
-    n_ghost = jnp.max(base[CAND_ROWS - 8:] + count[CAND_ROWS - 8:])
+    n_all = jnp.max(base[CAND_ROWS - 8:] + count[CAND_ROWS - 8:])
     lane_c = lax.broadcasted_iota(jnp.int32, (CAND_ROWS, LANES), 1)
     place = (lane_c - base) & (LANES - 1)
     source = jnp.zeros((CAND_ROWS, LANES), jnp.int32)
@@ -233,117 +276,122 @@
         source = jnp.where(probe <= place, source + step, source)
     target = jnp.where(place < count, lax.shift_right_logical(base + place, 7), -1)
     packed = [jnp.take_along_axis(values, source, axis=1) for values in rel]
-    ghost_rows = lax.div(n_ghost + (LANES - 1), LANES)
+    rows = lax.div(n_all + (LANES - 1), LANES)
+    own_rows = lax.div(n_own + (LANES - 1), LANES)
 
     def pack_row(row, carry):
         hit = target == row
-        filled = lane_1 + row * LANES < n_ghost
-        for axis in range(3):
+        filled = lane_1 + row * LANES < n_all
+        for axis in range(3):
+            own_part = jnp.where(row < own_rows, others[axis, row], 0.0)
             values = jnp.sum(jnp.where(hit, packed[axis], 0.0), axis=0, keepdims=True)
-            others[axis, own_rows + row] = jnp.broadcast_to(jnp.where(filled, values, FAR_OTHER), (8, LANES))
+            others[axis, row] = jnp.where(filled, own_part + values, FAR_OTHER)
         return carry
 
-    lax.fori_loop(0, ghost_rows, pack_row, 0)
-    rows = own_rows + ghost_rows
+    lax.fori_loop(lax.div(n_own, LANES), rows, pack_row, 0)
 
     rc2 = jnp.full((8, LANES), RC * RC + 0.0 * brick, jnp.float32)
-    kappa = UPC / 48.0
-
-    def radial(dist_sq):
-        inv_r = lax.rsqrt(dist_sq)
-        inv_2 = inv_r * inv_r
-        inv_4 = inv_2 * inv_2
-        term = inv_4 * inv_2 - 0.5
-        tail = kappa * inv_r
-        return term * (inv_4 * inv_4) + tail, term * term, tail * dist_sq
-
-    cut_f, cut_a, cut_h = radial(rc2)
-    own_minus_lane = lax.broadcasted_iota(jnp.int32, (8, LANES), 0) - lax.broadcasted_iota(jnp.int32, (8, LANES), 1)
     zero = jnp.zeros((8, LANES), jnp.float32)
-
-    def pair_loops(wrap):
-        inv_box = [1.0 / (brick * float(size)) for size in sizes]
-
-        def quad(index, energy):
+    acc[...] = jnp.zeros_like(acc)
+    quads = lax.div(n_own + (8 * QUAD - 1), 8 * QUAD)
+    far = jnp.full((8, LANES), FAR_OTHER, jnp.float32)
+
+    def set_far(row, carry):
+        for axis in range(3):
+            others[axis, row] = far
+        return carry
+
+    def excess(first_quad, last_quad, first_row, wrap_box, energy):
+        load_own, one_row, energy_of = pair_tools(mine, others, rc2, wrap_box)
+
+        def quad(index, total):
             first = index * QUAD
-            own = [[mine[axis, first + k] for axis in range(3)] for k in range(QUAD)]
-            self_row = lax.div(first, 16)
-
-            def one_row(row, sums, with_self):
-                other = [others[axis, row] for axis in range(3)]
-                force, sum_a, sum_h = list(sums[:-2]), sums[-2], sums[-1]
-                for k in range(QUAD):
-                    delta = [own[k][axis] - other[axis] for axis in range(3)]
-                    if wrap:
-                        for axis in (1, 2):
-                            delta[axis] = delta[axis] - box[axis] * jnp.floor(delta[axis] * inv_box[axis] + 0.5)
-                    dist_sq = delta[0] * delta[0] + delta[1] * delta[1] + delta[2] * delta[2]
-                    if with_self:
-                        dist_sq = jnp.where(own_minus_lane == row * LANES - (first + k) * 8, rc2, dist_sq)
-                    dist_sq = jnp.minimum(dist_sq, rc2)
-                    scale, a, h = radial(dist_sq)
-                    scale = scale - cut_f
-                    for axis in range(3):
-                        force[3 * k + axis] = force[3 * k + axis] + scale * delta[axis]
-                    sum_a, sum_h = sum_a + a, sum_h + h
-                return tuple(force) + (sum_a, sum_h)
-
-            def other_row(count, sums):
-                return one_row(count + (count >= self_row).astype(jnp.int32), sums, False)
-
-            def two_rows(count, sums):
-                return other_row(2 * count + 1, other_row(2 * count, sums))
-
-            sums = one_row(self_row, (zero,) * (3 * QUAD + 2), True)
-            twos = lax.div(rows - 1, 2)
-            sums = lax.fori_loop(0, twos, two_rows, sums)
-            sums = lax.fori_loop(2 * twos, rows - 1, other_row, sums)
+            own = load_own(first)
+            sums = (zero,) * (3 * QUAD + 2)
+            sums = lax.fori_loop(first_row, rows, lambda row, part: one_row(own, first, row, part, True), sums)
             for k in range(QUAD):
                 for axis in range(3):
                     acc[axis, first + k] = sums[3 * k + axis]
-            n = QUAD * rows.astype(jnp.float32)
-            return energy + (sums[-2] - n * cut_a) - 12.0 * (sums[-1] - n * cut_h)
-
-        quads = lax.div(n_own + (8 * QUAD - 1), 8 * QUAD)
-        energy = lax.fori_loop(0, quads, quad, zero)
-        eng_out[...] = jnp.full((8, LANES), 2.0 * jnp.sum(energy), jnp.float32)
-
-    pl.when(brick >= 2.0 * RC)(lambda: pair_loops(False))
-    pl.when(brick < 2.0 * RC)(lambda: pair_loops(True))
-
+            return total + energy_of(sums, (rows - first_row).astype(jnp.float32))
+
+        return lax.fori_loop(first_quad, last_quad, quad, energy)
+
+    def plain():
+        short = jnp.where(rows > FIXED_ROWS, jnp.minimum(quads, FIXED_QUADS), 0)
+        energy = excess(0, short, FIXED_ROWS, [], zero)
+        eng_ref[...] = excess(FIXED_QUADS, quads, 0, [], energy)
+        lax.fori_loop(rows, FIXED_ROWS, set_far, 0)
+
+    def wrapped():
+        wrap_box = [(axis, box[axis], 1.0 / box[axis]) for axis in (1, 2)]
+        eng_ref[...] = excess(0, quads, 0, wrap_box, zero)
+        lax.fori_loop(0, FIXED_ROWS, set_far, 0)
+
+    pl.when(brick >= 2.0 * RC)(plain)
+    pl.when(brick < 2.0 * RC)(wrapped)
+
+
+def tile_kernel(brick_ref, mine, others, part, eng_ref, frc_ref, out_ref, acc, eng, slots, send_sem, recv_sem):
+    coords = my_coords()
+    mz, my, mx = coords
+    barrier = entry_signals(coords)
+    brick = brick_ref[0]
+    rc2 = jnp.full((8, LANES), RC * RC + 0.0 * brick, jnp.float32)
+    load_own, one_row, energy_of = pair_tools(mine, others, rc2, [])
+
+    def quad(index, energy):
+        first = index * QUAD
+        own = load_own(first)
+        self_row = lax.div(first, 16)
+        zero = jnp.zeros((8, LANES), jnp.float32)
+        sums = tuple(part[axis, first + k] for k in range(QUAD) for axis in range(3)) + (zero, zero)
+        sums = one_row(own, first, self_row, sums, True)
+        for count in range(FIXED_ROWS - 1):
+            sums = one_row(own, first, count + (count >= self_row).astype(jnp.int32), sums, False)
+        for k in range(QUAD):
+            for axis in range(3):
+                acc[axis, first + k] = sums[3 * k + axis]
+        return energy + energy_of(sums, float(FIXED_ROWS))
+
+    energy = lax.fori_loop(0, FIXED_QUADS, quad, eng_ref[...])
+    eng[...] = jnp.full((8, LANES), 2.0 * jnp.sum(energy), jnp.float32)
+    for group in range(FIXED_QUADS * QUAD, 16 * (FIXED_QUADS * QUAD // 16 + 1)):
+        for axis in range(3):
+            acc[axis, group] = part[axis, group]
+    pl.semaphore_wait(barrier, len(PEERS))
+    place = (mz * NY + my) * NX + mx
+    copies = []
+    for index, offset in enumerate(PEERS):
+        copies.append(pltpu.make_async_remote_copy(src_ref=eng, dst_ref=slots.at[place], send_sem=send_sem.at[index], recv_sem=recv_sem.at[index], device_id=peer_id(coords, offset), device_id_type=MESH))
+        copies[-1].start()
+    slots[place] = eng[...]
+    for block in range(BLOCKS):
+        held = acc if block <= FIXED_QUADS * QUAD // 16 else part
+        for axis in range(3):
+            turned = jnp.transpose(held[axis, pl.ds(block * 16, 16)].reshape(LANES, LANES), (1, 0))
+            frc_ref[axis:axis + 1, block * LANES:(block + 1) * LANES] = 48.0 * jnp.sum(turned, axis=0, keepdims=True)
+    for copy in copies:
+        copy.wait()
+    total = slots[0]
+    for index in range(1, NZ * NY * NX):
+        total = total + slots[index]
+    out_ref[0, 0] = jnp.max(total)
+
+
+def finish_kernel(sorted_ref, frc_ref, pos_out, vel_out, frc_out, id_out, ok_out):
     for block in range(BLOCKS):
         width = min(LANES, CAP - block * LANES)
         lanes = slice(block * LANES, block * LANES + width)
-        valid = lane_1 + block * LANES < n_own
         rows_s = sorted_ref[block]
-        for axis in range(3):
-            turned = jnp.transpose(acc[axis, pl.ds(block * 16, 16)].reshape(LANES, LANES), (1, 0))
-            force = jnp.where(valid, 48.0 * jnp.sum(turned, axis=0, keepdims=True), 0.0)
+        valid = rows_s[6:7] > 0.5
+        for axis in range(3):
+            force = jnp.where(valid, frc_ref[axis:axis + 1, block * LANES:(block + 1) * LANES], 0.0)
             frc_out[axis:axis + 1, lanes] = force[:, :width]
             vel_out[axis:axis + 1, lanes] = (rows_s[3 + axis:4 + axis] + (0.5 * DT) * force)[:, :width]
             pos_out[axis:axis + 1, lanes] = rows_s[axis:axis + 1, :width]
         new_id = lax.shift_left(rows_s[6:7].astype(jnp.int32) - 1, 16) + rows_s[7:8].astype(jnp.int32)
         id_out[lanes] = jnp.where(valid, new_id, 0)[:, :width].reshape(width)
         ok_out[lanes] = valid.astype(jnp.int32)[:, :width].reshape(width)
-
-
-def energy_kernel(eng_ref, out_ref, slots, send_sem, recv_sem):
-    coords = my_coords()
-    mz, my, mx = coords
-    barrier = entry_signals(coords)
-    pl.semaphore_wait(barrier, len(PEERS))
-    place = (mz * NY + my) * NX + mx
-    copies = []
-    for index, offset in enumerate(PEERS):
-        copies.append(pltpu.make_async_remote_copy(src_ref=eng_ref, dst_ref=slots.at[place], send_sem=send_sem.at[index], recv_sem=recv_sem.at[index], device_id=peer_id(coords, offset), device_id_type=MESH))
-        copies[-1].start()
-    slots[place] = eng_ref[...]
-    for copy in copies:
-        copy.wait()
-    total = slots[0]
-    for index in range(1, NZ * NY * NX):
-        total = total + slots[index]
-    out_ref[0, 0] = jnp.max(total)
 
 
 VMEM_SPEC = pl.BlockSpec(memory_space=pltpu.VMEM)
@@ -379,29 +427,32 @@
             compiler_params=pltpu.CompilerParams(collective_id=0, has_side_effects=True, vmem_limit_bytes=VMEM_LIMIT),
             name="exchange",
         )(brick, *(pltpu.with_memory_space_constraint(value, pltpu.HBM) for value in (atom_pos.T, atom_vel.T, atom_frc.T, atom_id, atom_ok)))
-        pos, vel, frc, ids, oks, eng = pl.pallas_call(
-            force_kernel,
-            out_shape=(jax.ShapeDtypeStruct((3, CAP), f32),) * 3 + (jax.ShapeDtypeStruct((CAP,), jnp.int32),) * 2 + (jax.ShapeDtypeStruct((8, LANES), f32),),
+        own_tiles = jax.ShapeDtypeStruct((3, GROUPS_OWN, 8, LANES), f32)
+        placed, mine, others, part, eng = pl.pallas_call(
+            prepare_kernel,
+            out_shape=(jax.ShapeDtypeStruct((BLOCKS, 8, LANES), f32), own_tiles, jax.ShapeDtypeStruct((3, MAX_ROWS, 8, LANES), f32), own_tiles, jax.ShapeDtypeStruct((8, LANES), f32)),
             in_specs=[SMEM_SPEC] + [VMEM_SPEC] * 3,
-            out_specs=(VMEM_SPEC,) * 6,
-            scratch_shapes=[
-                pltpu.VMEM((3, MAX_ROWS, 8, LANES), f32),
-                pltpu.VMEM((3, BLOCKS * 16, 8, LANES), f32),
-                pltpu.VMEM((3, BLOCKS * 16, 8, LANES), f32),
-                pltpu.VMEM((BLOCKS, 8, LANES), f32),
-            ],
+            out_specs=(VMEM_SPEC,) * 5,
             compiler_params=pltpu.CompilerParams(vmem_limit_bytes=VMEM_LIMIT),
-            name="forces",
+            name="prepare",
         )(brick, gat, pkt, own)
-        total = pl.pallas_call(
-            energy_kernel,
-            out_shape=jax.ShapeDtypeStruct((1, 1), f32),
-            in_specs=[VMEM_SPEC],
-            out_specs=SMEM_SPEC,
-            scratch_shapes=[pltpu.VMEM((n_dev, 8, LANES), f32), pltpu.SemaphoreType.DMA((n_dev - 1,)), pltpu.SemaphoreType.DMA((n_dev - 1,))],
+        frc_rows, total = pl.pallas_call(
+            tile_kernel,
+            out_shape=(jax.ShapeDtypeStruct((8, WIDE), f32), jax.ShapeDtypeStruct((1, 1), f32)),
+            in_specs=[SMEM_SPEC] + [VMEM_SPEC] * 4,
+            out_specs=(VMEM_SPEC, SMEM_SPEC),
+            scratch_shapes=[pltpu.VMEM((3, GROUPS_OWN, 8, LANES), f32), pltpu.VMEM((8, LANES), f32), pltpu.VMEM((n_dev, 8, LANES), f32), pltpu.SemaphoreType.DMA((n_dev - 1,)), pltpu.SemaphoreType.DMA((n_dev - 1,))],
             compiler_params=pltpu.CompilerParams(collective_id=1, has_side_effects=True, vmem_limit_bytes=VMEM_LIMIT),
-            name="energy",
-        )(eng)
+            name="tile",
+        )(brick, mine, others, part, eng)
+        pos, vel, frc, ids, oks = pl.pallas_call(
+            finish_kernel,
+            out_shape=(jax.ShapeDtypeStruct((3, CAP), f32),) * 3 + (jax.ShapeDtypeStruct((CAP,), jnp.int32),) * 2,
+            in_specs=[VMEM_SPEC] * 2,
+            out_specs=(VMEM_SPEC,) * 5,
+            compiler_params=pltpu.CompilerParams(vmem_limit_bytes=VMEM_LIMIT),
+            name="finish",
+        )(placed, frc_rows)
         return pos.T, vel.T, frc.T, ids, oks, total.reshape(())
 
     row_spec = P(MESH_AXES, None)

time: 27.6 us -> 24.8 us (0.90)
  Pallas kernels: 24.6 us -> 21.5 us
    pallas_call x2 -> x3, Pallas kernels: 14.8 us -> 11.7 us  [the longest x1 8.46 us: local_step(): pl.pallas_call(tile_kernel, out_shape=(jax.ShapeDtypeStruct((8, WIDE), f3...]
where the time goes in v1:
time: 24.8 us; the launch traced here: 24.6 us
  Pallas kernels  21.5 us (87%)
  between operations  3.04 us (12%)
    pallas_call x1, Pallas kernels, local_step(): pl.pallas_call(exchange_kernel, out_shape=(jax.ShapeDtypeStruct((N_GROUPS...  9.82 us
    pallas_call x1, Pallas kernels, local_step(): pl.pallas_call(tile_kernel, out_shape=(jax.ShapeDtypeStruct((8, WIDE), f3...  8.46 us
    pallas_call x1, Pallas kernels, local_step(): pl.pallas_call(prepare_kernel, out_shape=(jax.ShapeDtypeStruct((BLOCKS, 8...  2.61 us
    pallas_call x1, Pallas kernels, local_step(): pl.pallas_call(finish_kernel, out_shape=(jax.ShapeDtypeStruct((3, CAP), f...  0.64 us

profile of v1, /device:TPU:0, one launch (start us, length us, event | category | flops | bytes accessed | tf_op | source)
XLA Modules:
  0.0 24.6 jit_solution(5981179057929173158)
XLA Ops:
  1.3 9.8 %exchange.1 = (f32[12,3,8,128]{3,2,1,0:T(8,128)S(1)}, f32[15,8,128]{2,1,0:T(8,128)S(1)}, f32[16,768]{1,0:T(8,128)S(1)}) custom-call(f32[1]{0:T(128)} %bitcast.8.brick_ref, f32[3,729]{1,0:T(4,128)} %bitcast.11, f32[3,729]{1,0:T(4,128)} %bitcast.12, f32[3,729]{1,0:T(4,128)} %bitcast.13, s32[729]{0:T(1024)} %id_ref.1, s32[729]{0:T(1024)} %ok_ref.1), custom_call_target="tpu_custom_call" | custom-call | tf_op jit(solution)/shard_map/exchange/pallas_call | solution.py:408
  11.1 2.6 %prepare.1 = (f32[6,8,128]{2,1,0:T(8,128)S(1)}, f32[3,96,8,128]{3,2,1,0:T(8,128)S(1)}, f32[3,110,8,128]{3,2,1,0:T(8,128)S(1)}, f32[3,96,8,128]{3,2,1,0:T(8,128)S(1)}, f32[8,128]{1,0:T(8,128)S(1)}) custom-call(f32[1]{0:T(128)} %bitcast.9.brick_ref, f32[12,3,8,128]{3,2,1,0:T(8,128)S(1)} %get-tuple-element.21.gat_ref, ...), custom_call_target="tpu_custom_call" | custom-call | tf_op jit(solution)/shard_map/prepare/pallas_call | solution.py:431
  13.7 8.5 %tile.1 = (f32[8,768]{1,0:T(8,128)S(1)}, f32[1,1]{1,0:T(1,128)}) custom-call(f32[1]{0:T(128)} %bitcast.10.brick_ref, f32[3,96,8,128]{3,2,1,0:T(8,128)S(1)} %get-tuple-element.25.mine, f32[3,110,8,128]{3,2,1,0:T(8,128)S(1)} %get-tuple-element.26.others, f32[3,96,8,128]{3,2,1,0:T(8,128)S(1)} %get-tuple-element.27.part, f32[8,128]{1,0:T(8,128)S(1)} %get-tuple-element.28.eng_ref), custom_call_target="tpu_custom_call" | custom-call | tf_op jit(solution)/shard_map/tile/pallas_call | solution.py:439
  22.2 0.6 %finish.1 = (f32[3,729]{1,0:T(4,128)}, f32[3,729]{1,0:T(4,128)}, f32[3,729]{1,0:T(4,128)}, s32[729]{0:T(1024)}, s32[729]{0:T(1024)}) custom-call(f32[6,8,128]{2,1,0:T(8,128)S(1)} %get-tuple-element.24.sorted_ref, f32[8,768]{1,0:T(8,128)S(1)} %get-tuple-element.29.frc_ref), custom_call_target="tpu_custom_call" | custom-call | tf_op jit(solution)/shard_map/finish/pallas_call | solution.py:448

commit v2 on v1

--- a/solution.py
+++ b/solution.py
@@ -19,6 +19,7 @@
 FAR_OWN = 1.0e4
 FAR_OTHER = -1.0e4
 NOWHERE = 1.0e9
+GHOST_SQ = RC * RC + 0.01
 PEERS = [(dz, dy, dx) for dz in range(NZ) for dy in range(NY) for dx in range(NX)][1:]
 GROUPS = [(1, 1, 1), (-1, 1, 1), (1, 1, 0), (-1, 1, 0), (1, 0, 1), (-1, 0, 1), (1, 0, 0), (-1, 0, 0), (0, 1, 1), (0, 1, 0), (0, 0, 1)]
 N_GROUPS = len(GROUPS)
@@ -86,12 +87,12 @@
     for fetch in fetches:
         fetch.start()
     barrier = entry_signals(coords)
-    brick = brick_ref[0]
     tail = slice(WIDE - LANES, WIDE)
     pad_ref[:, :, tail] = jnp.zeros((3, 4, LANES), jnp.float32)
     int_ref[:, tail] = jnp.zeros((2, LANES), jnp.int32)
     for fetch in fetches:
         fetch.wait()
+    brick = brick_ref[...]
     for index in range(3):
         pad_ref[index, 0:3, 0:CAP] = raw[index]
     int_ref[0:1, 0:CAP] = ids_in[...].reshape(1, CAP)
@@ -141,7 +142,7 @@
     send_pkt[0] = packet[:, 0:LANES]
     send_pkt[1] = packet[:, LANES:2 * LANES]
     own_ref[0:8, :] = data
-    own_ref[8:16, :] = jnp.concatenate([jnp.where(stay, slot, -1.0), jnp.zeros((7, WIDE), jnp.float32)], axis=0)
+    own_ref[8:16, :] = jnp.concatenate([jnp.where(stay, slot, -1.0), jnp.full((7, WIDE), brick, jnp.float32)], axis=0)
     pl.semaphore_wait(barrier, len(PEERS))
     copies = []
     for index, (gx, gy, gz) in enumerate(GROUPS + DISTANT):
@@ -161,8 +162,8 @@
 MAX_ROWS = BLOCKS + CAND_ROWS
 GROUPS_OWN = BLOCKS * 16
 QUAD = 4
-FIXED_QUADS = 15
-FIXED_ROWS = 12
+FIXED_QUADS = 16
+FIXED_ROWS = 11
 
 
 def pair_tools(mine, others, rc2, wrap_box):
@@ -176,7 +177,11 @@
         tail = kappa * inv_r
         return term * (inv_4 * inv_4) + tail, term * term, tail * dist_sq
 
+    def quad_energy(a, h):
+        return ((a[0] + a[1]) + (a[2] + a[3])) - 12.0 * ((h[0] + h[1]) + (h[2] + h[3]))
+
     cut_f, cut_a, cut_h = radial(rc2)
+    cut_energy = quad_energy([cut_a] * QUAD, [cut_h] * QUAD)
     own_minus_lane = lax.broadcasted_iota(jnp.int32, (8, LANES), 0) - lax.broadcasted_iota(jnp.int32, (8, LANES), 1)
 
     def load_own(first):
@@ -184,7 +189,7 @@
 
     def one_row(own, first, row, sums, with_self):
         other = [others[axis, row] for axis in range(3)]
-        force, sum_a, sum_h = list(sums[:-2]), sums[-2], sums[-1]
+        force, energy, parts_a, parts_h = list(sums[:-1]), sums[-1], [], []
         for k in range(QUAD):
             delta = [own[k][axis] - other[axis] for axis in range(3)]
             for axis, box, inv_box in wrap_box:
@@ -197,20 +202,17 @@
             scale = scale - cut_f
             for axis in range(3):
                 force[3 * k + axis] = force[3 * k + axis] + scale * delta[axis]
-            sum_a, sum_h = sum_a + a, sum_h + h
-        return tuple(force) + (sum_a, sum_h)
-
-    def energy_of(sums, n_rows):
-        return (sums[-2] - (QUAD * n_rows) * cut_a) - 12.0 * (sums[-1] - (QUAD * n_rows) * cut_h)
-
-    return load_own, one_row, energy_of
-
-
-def prepare_kernel(brick_ref, gat_ref, pkt_ref, own_ref, sorted_ref, mine, others, acc, eng_ref):
+            parts_a.append(a)
+            parts_h.append(h)
+        return tuple(force) + (energy + (quad_energy(parts_a, parts_h) - cut_energy),)
+
+    return load_own, one_row
+
+
+def prepare_kernel(gat_ref, pkt_ref, own_ref, sorted_ref, mine, others, acc, eng_ref):
     mz, my, mx = my_coords()
-    brick = brick_ref[0]
+    brick = own_ref[9:10, 0:LANES]
     half_l = 0.5 * brick
-    reach = half_l + RC
     sizes = (NX, NY, NZ)
     centre = [(index.astype(jnp.float32) + 0.5) * brick for index in (mx, my, mz)]
     box = [brick * float(size) for size in sizes]
@@ -233,24 +235,8 @@
     arr_ok = arr[6:7] > 0.5
     arr_id = jnp.where(arr_ok, ids[:, WIDE:], int_max)
     own_id = jnp.where(stay, ids[:, :WIDE], int_max)
-    arr_col = jnp.transpose(jnp.broadcast_to(arr_id, (8, 2 * LANES)), (1, 0))[:, 0:1]
-    own_col = jnp.transpose(jnp.broadcast_to(own_id, (8, WIDE)), (1, 0))[:, 0:1]
-    all_id = jnp.concatenate([own_id, arr_id], axis=1)
-    arr_before = jnp.sum((arr_col < all_id).astype(jnp.float32), axis=0, keepdims=True)
-    stay_before = jnp.sum((own_col < arr_id).astype(jnp.float32), axis=0, keepdims=True)
-    rank = jnp.concatenate([jnp.where(stay, stay_rank + arr_before[:, :WIDE], -1.0), jnp.where(arr_ok, stay_before + arr_before[:, WIDE:], -1.0)], axis=1).astype(jnp.int32)
-    n_own = jnp.sum((rank >= 0).astype(jnp.float32)).astype(jnp.int32)
-    parts = split3(data)
-    for block in range(BLOCKS):
-        pick = (lax.broadcasted_iota(jnp.int32, (LANES, WIDE + 2 * LANES), 0) + block * LANES == rank).astype(jnp.float32).astype(jnp.bfloat16)
-        rows_s = join3(jnp.transpose(dot_nt(pick, parts), (1, 0)))
-        sorted_ref[block] = rows_s
-        valid = lane_1 + block * LANES < n_own
-        rel = jnp.concatenate([rows_s[axis:axis + 1] - centre[axis] for axis in range(3)] + [rows_s[3:8]], axis=0)
-        columns = jnp.transpose(jnp.where(valid, rel, FAR_OWN), (1, 0))
-        for axis in range(3):
-            others[axis, block] = jnp.broadcast_to(jnp.where(valid, rel[axis:axis + 1], 0.0), (8, LANES))
-            mine[axis, pl.ds(block * 16, 16)] = jnp.broadcast_to(columns[:, axis:axis + 1], (LANES, LANES)).reshape(16, 8, LANES)
+    n_vec = jnp.sum(stay.astype(jnp.float32), axis=1, keepdims=True) + jnp.sum(arr_ok.astype(jnp.float32), axis=1, keepdims=True)
+    n_own = jnp.max(n_vec).astype(jnp.int32)
 
     rel = []
     for axis in range(3):
@@ -258,14 +244,14 @@
         values = jnp.concatenate([gat_ref[:, axis].reshape(8 * (N_GROUPS + 1), LANES)] + distant + [jnp.full((4, LANES), NOWHERE, jnp.float32)], axis=0) - centre[axis]
         values = jnp.where(values > 0.5 * box[axis], values - box[axis], jnp.where(values < -0.5 * box[axis], values + box[axis], values))
         rel.append(values)
-    near = (jnp.abs(rel[0]) < reach) & (jnp.abs(rel[1]) < reach) & (jnp.abs(rel[2]) < reach)
-    inside = (jnp.abs(rel[0]) < half_l) & (jnp.abs(rel[1]) < half_l) & (jnp.abs(rel[2]) < half_l)
-    ghost = (near & jnp.logical_not(inside)).astype(jnp.float32).astype(jnp.bfloat16)
+    over = [jnp.maximum(jnp.abs(values) - half_l, 0.0) for values in rel]
+    gap_sq = over[0] * over[0] + over[1] * over[1] + over[2] * over[2]
+    ghost = ((gap_sq > 0.0) & (gap_sq < GHOST_SQ)).astype(jnp.float32).astype(jnp.bfloat16)
     row_i = lax.broadcasted_iota(jnp.int32, (LANES, LANES), 0)
     col_i = lax.broadcasted_iota(jnp.int32, (LANES, LANES), 1)
     cum = dot_nn(ghost, (row_i <= col_i).astype(jnp.bfloat16)).astype(jnp.int32)
     count = dot_nn(ghost, jnp.ones((LANES, LANES), jnp.bfloat16))
-    base = dot_nn((col_i < row_i).astype(jnp.bfloat16)[:CAND_ROWS, :CAND_ROWS], count.astype(jnp.bfloat16)).astype(jnp.int32) + n_own
+    base = dot_nn((col_i < row_i).astype(jnp.bfloat16)[:CAND_ROWS, :CAND_ROWS], count.astype(jnp.bfloat16)).astype(jnp.int32) + n_vec.astype(jnp.int32)
     count = count.astype(jnp.int32)
     n_all = jnp.max(base[CAND_ROWS - 8:] + count[CAND_ROWS - 8:])
     lane_c = lax.broadcasted_iota(jnp.int32, (CAND_ROWS, LANES), 1)
@@ -276,6 +262,24 @@
         source = jnp.where(probe <= place, source + step, source)
     target = jnp.where(place < count, lax.shift_right_logical(base + place, 7), -1)
     packed = [jnp.take_along_axis(values, source, axis=1) for values in rel]
+    arr_col = jnp.transpose(jnp.broadcast_to(arr_id, (8, 2 * LANES)), (1, 0))[:, 0:1]
+    own_col = jnp.transpose(jnp.broadcast_to(own_id, (8, WIDE)), (1, 0))[:, 0:1]
+    all_id = jnp.concatenate([own_id, arr_id], axis=1)
+    arr_before = jnp.sum((arr_col < all_id).astype(jnp.float32), axis=0, keepdims=True)
+    stay_before = jnp.sum((own_col < arr_id).astype(jnp.float32), axis=0, keepdims=True)
+    rank = jnp.concatenate([jnp.where(stay, stay_rank + arr_before[:, :WIDE], -1.0), jnp.where(arr_ok, stay_before + arr_before[:, WIDE:], -1.0)], axis=1).astype(jnp.int32)
+    parts = split3(data)
+    for block in range(BLOCKS):
+        pick = (lax.broadcasted_iota(jnp.int32, (LANES, WIDE + 2 * LANES), 0) + block * LANES == rank).astype(jnp.float32).astype(jnp.bfloat16)
+        rows_s = join3(jnp.transpose(dot_nt(pick, parts), (1, 0)))
+        sorted_ref[block] = rows_s
+        valid = lane_1 + block * LANES < n_vec.astype(jnp.int32)
+        own_rel = jnp.concatenate([rows_s[axis:axis + 1] - centre[axis] for axis in range(3)] + [rows_s[3:8]], axis=0)
+        columns = jnp.transpose(jnp.where(valid, own_rel, FAR_OWN), (1, 0))
+        for axis in range(3):
+            others[axis, block] = jnp.broadcast_to(jnp.where(valid, own_rel[axis:axis + 1], 0.0), (8, LANES))
+            mine[axis, pl.ds(block * 16, 16)] = jnp.broadcast_to(columns[:, axis:axis + 1], (LANES, LANES)).reshape(16, 8, LANES)
+
     rows = lax.div(n_all + (LANES - 1), LANES)
     own_rows = lax.div(n_own + (LANES - 1), LANES)
 
@@ -290,7 +294,7 @@
 
     lax.fori_loop(lax.div(n_own, LANES), rows, pack_row, 0)
 
-    rc2 = jnp.full((8, LANES), RC * RC + 0.0 * brick, jnp.float32)
+    rc2 = RC * RC + 0.0 * own_ref[8:16, 0:LANES]
     zero = jnp.zeros((8, LANES), jnp.float32)
     acc[...] = jnp.zeros_like(acc)
     quads = lax.div(n_own + (8 * QUAD - 1), 8 * QUAD)
@@ -302,17 +306,17 @@
         return carry
 
     def excess(first_quad, last_quad, first_row, wrap_box, energy):
-        load_own, one_row, energy_of = pair_tools(mine, others, rc2, wrap_box)
+        load_own, one_row = pair_tools(mine, others, rc2, wrap_box)
 
         def quad(index, total):
             first = index * QUAD
             own = load_own(first)
-            sums = (zero,) * (3 * QUAD + 2)
+            sums = (zero,) * (3 * QUAD) + (total,)
             sums = lax.fori_loop(first_row, rows, lambda row, part: one_row(own, first, row, part, True), sums)
             for k in range(QUAD):
                 for axis in range(3):
                     acc[axis, first + k] = sums[3 * k + axis]
-            return total + energy_of(sums, (rows - first_row).astype(jnp.float32))
+            return sums[-1]
 
         return lax.fori_loop(first_quad, last_quad, quad, energy)
 
@@ -327,37 +331,33 @@
         eng_ref[...] = excess(0, quads, 0, wrap_box, zero)
         lax.fori_loop(0, FIXED_ROWS, set_far, 0)
 
-    pl.when(brick >= 2.0 * RC)(plain)
-    pl.when(brick < 2.0 * RC)(wrapped)
-
-
-def tile_kernel(brick_ref, mine, others, part, eng_ref, frc_ref, out_ref, acc, eng, slots, send_sem, recv_sem):
+    wide = jnp.max(brick) >= 2.0 * RC
+    pl.when(wide)(plain)
+    pl.when(jnp.logical_not(wide))(wrapped)
+
+
+def tile_kernel(mine, others, part, eng_ref, frc_ref, out_ref, acc, eng, slots, send_sem, recv_sem):
     coords = my_coords()
     mz, my, mx = coords
     barrier = entry_signals(coords)
-    brick = brick_ref[0]
-    rc2 = jnp.full((8, LANES), RC * RC + 0.0 * brick, jnp.float32)
-    load_own, one_row, energy_of = pair_tools(mine, others, rc2, [])
+    rc2 = RC * RC + 0.0 * mine[0, 0]
+    load_own, one_row = pair_tools(mine, others, rc2, [])
 
     def quad(index, energy):
         first = index * QUAD
         own = load_own(first)
         self_row = lax.div(first, 16)
-        zero = jnp.zeros((8, LANES), jnp.float32)
-        sums = tuple(part[axis, first + k] for k in range(QUAD) for axis in range(3)) + (zero, zero)
+        sums = tuple(part[axis, first + k] for k in range(QUAD) for axis in range(3)) + (energy,)
         sums = one_row(own, first, self_row, sums, True)
         for count in range(FIXED_ROWS - 1):
             sums = one_row(own, first, count + (count >= self_row).astype(jnp.int32), sums, False)
         for k in range(QUAD):
             for axis in range(3):
                 acc[axis, first + k] = sums[3 * k + axis]
-        return energy + energy_of(sums, float(FIXED_ROWS))
+        return sums[-1]
 
     energy = lax.fori_loop(0, FIXED_QUADS, quad, eng_ref[...])
     eng[...] = jnp.full((8, LANES), 2.0 * jnp.sum(energy), jnp.float32)
-    for group in range(FIXED_QUADS * QUAD, 16 * (FIXED_QUADS * QUAD // 16 + 1)):
-        for axis in range(3):
-            acc[axis, group] = part[axis, group]
     pl.semaphore_wait(barrier, len(PEERS))
     place = (mz * NY + my) * NX + mx
     copies = []
@@ -366,7 +366,7 @@
         copies[-1].start()
     slots[place] = eng[...]
     for block in range(BLOCKS):
-        held = acc if block <= FIXED_QUADS * QUAD // 16 else part
+        held = acc if block < FIXED_QUADS * QUAD // 16 else part
         for axis in range(3):
             turned = jnp.transpose(held[axis, pl.ds(block * 16, 16)].reshape(LANES, LANES), (1, 0))
             frc_ref[axis:axis + 1, block * LANES:(block + 1) * LANES] = 48.0 * jnp.sum(turned, axis=0, keepdims=True)
@@ -375,10 +375,11 @@
     total = slots[0]
     for index in range(1, NZ * NY * NX):
         total = total + slots[index]
-    out_ref[0, 0] = jnp.max(total)
-
-
-def finish_kernel(sorted_ref, frc_ref, pos_out, vel_out, frc_out, id_out, ok_out):
+    out_ref[...] = total
+
+
+def finish_kernel(sorted_ref, frc_ref, total_ref, pos_out, vel_out, frc_out, id_out, ok_out, eng_out):
+    eng_out[...] = jnp.max(total_ref[...])
     for block in range(BLOCKS):
         width = min(LANES, CAP - block * LANES)
         lanes = slice(block * LANES, block * LANES + width)
@@ -403,7 +404,6 @@
 def solution(mesh):
     def local_step(atom_pos, atom_vel, atom_frc, atom_id, atom_ok, brick_side):
         f32 = jnp.float32
-        brick = brick_side.reshape(1)
         n_dev = NZ * NY * NX
         gat, pkt, own = pl.pallas_call(
             exchange_kernel,
@@ -426,34 +426,34 @@
             ],
             compiler_params=pltpu.CompilerParams(collective_id=0, has_side_effects=True, vmem_limit_bytes=VMEM_LIMIT),
             name="exchange",
-        )(brick, *(pltpu.with_memory_space_constraint(value, pltpu.HBM) for value in (atom_pos.T, atom_vel.T, atom_frc.T, atom_id, atom_ok)))
+        )(brick_side, *(pltpu.with_memory_space_constraint(value, pltpu.HBM) for value in (atom_pos.T, atom_vel.T, atom_frc.T, atom_id, atom_ok)))
         own_tiles = jax.ShapeDtypeStruct((3, GROUPS_OWN, 8, LANES), f32)
         placed, mine, others, part, eng = pl.pallas_call(
             prepare_kernel,
             out_shape=(jax.ShapeDtypeStruct((BLOCKS, 8, LANES), f32), own_tiles, jax.ShapeDtypeStruct((3, MAX_ROWS, 8, LANES), f32), own_tiles, jax.ShapeDtypeStruct((8, LANES), f32)),
-            in_specs=[SMEM_SPEC] + [VMEM_SPEC] * 3,
+            in_specs=[VMEM_SPEC] * 3,
             out_specs=(VMEM_SPEC,) * 5,
             compiler_params=pltpu.CompilerParams(vmem_limit_bytes=VMEM_LIMIT),
             name="prepare",
-        )(brick, gat, pkt, own)
+        )(gat, pkt, own)
         frc_rows, total = pl.pallas_call(
             tile_kernel,
-            out_shape=(jax.ShapeDtypeStruct((8, WIDE), f32), jax.ShapeDtypeStruct((1, 1), f32)),
-            in_specs=[SMEM_SPEC] + [VMEM_SPEC] * 4,
-            out_specs=(VMEM_SPEC, SMEM_SPEC),
+            out_shape=(jax.ShapeDtypeStruct((8, WIDE), f32), jax.ShapeDtypeStruct((8, LANES), f32)),
+            in_specs=[VMEM_SPEC] * 4,
+            out_specs=(VMEM_SPEC,) * 2,
             scratch_shapes=[pltpu.VMEM((3, GROUPS_OWN, 8, LANES), f32), pltpu.VMEM((8, LANES), f32), pltpu.VMEM((n_dev, 8, LANES), f32), pltpu.SemaphoreType.DMA((n_dev - 1,)), pltpu.SemaphoreType.DMA((n_dev - 1,))],
             compiler_params=pltpu.CompilerParams(collective_id=1, has_side_effects=True, vmem_limit_bytes=VMEM_LIMIT),
             name="tile",
-        )(brick, mine, others, part, eng)
-        pos, vel, frc, ids, oks = pl.pallas_call(
+        )(mine, others, part, eng)
+        pos, vel, frc, ids, oks, energy = pl.pallas_call(
             finish_kernel,
-            out_shape=(jax.ShapeDtypeStruct((3, CAP), f32),) * 3 + (jax.ShapeDtypeStruct((CAP,), jnp.int32),) * 2,
-            in_specs=[VMEM_SPEC] * 2,
-            out_specs=(VMEM_SPEC,) * 5,
+            out_shape=(jax.ShapeDtypeStruct((3, CAP), f32),) * 3 + (jax.ShapeDtypeStruct((CAP,), jnp.int32),) * 2 + (jax.ShapeDtypeStruct((), f32),),
+            in_specs=[VMEM_SPEC] * 3,
+            out_specs=(VMEM_SPEC,) * 5 + (SMEM_SPEC,),
             compiler_params=pltpu.CompilerParams(vmem_limit_bytes=VMEM_LIMIT),
             name="finish",
-        )(placed, frc_rows)
-        return pos.T, vel.T, frc.T, ids, oks, total.reshape(())
+        )(placed, frc_rows, total)
+        return pos.T, vel.T, frc.T, ids, oks, energy
 
     row_spec = P(MESH_AXES, None)
     id_spec = P(MESH_AXES)

time: 24.8 us -> 22.1 us (0.89)
  between operations: 3.04 us -> 1.3 us
  Pallas kernels: 21.5 us -> 20.5 us
    pallas_call x1, Pallas kernels: 8.46 us -> 7.68 us  [local_step(): pl.pallas_call(tile_kernel, out_shape=(jax.ShapeDtypeStruct((8, WIDE), f3...]
where the time goes in v2:
time: 22.1 us; the launch traced here: 21.8 us
  Pallas kernels  20.5 us (93%)
  between operations  1.3 us (6%)
    pallas_call x1, Pallas kernels, local_step(): pl.pallas_call(exchange_kernel, out_shape=(jax.ShapeDtypeStruct((N_GROUPS...  9.82 us
    pallas_call x1, Pallas kernels, local_step(): pl.pallas_call(tile_kernel, out_shape=(jax.ShapeDtypeStruct((8, WIDE), f3...  7.68 us
    pallas_call x1, Pallas kernels, local_step(): pl.pallas_call(prepare_kernel, out_shape=(jax.ShapeDtypeStruct((BLOCKS, 8...  2.38 us
    pallas_call x1, Pallas kernels, local_step(): pl.pallas_call(finish_kernel, out_shape=(jax.ShapeDtypeStruct((3, CAP), f...  0.65 us

profile of v2, /device:TPU:0, one launch (start us, length us, event | category | flops | bytes accessed | tf_op | source)
XLA Modules:
  0.0 21.8 jit_solution(2707097105378141035)
XLA Ops:
  1.3 9.8 %exchange.1 = (f32[12,3,8,128]{3,2,1,0:T(8,128)S(1)}, f32[15,8,128]{2,1,0:T(8,128)S(1)}, f32[16,768]{1,0:T(8,128)S(1)}) custom-call(f32[]{:T(128)S(6)} %copy.12.brick_ref, f32[3,729]{1,0:T(4,128)} %bitcast.6, f32[3,729]{1,0:T(4,128)} %bitcast.7, f32[3,729]{1,0:T(4,128)} %bitcast.8, s32[729]{0:T(1024)} %id_ref.1, s32[729]{0:T(1024)} %ok_ref.1), custom_call_target="tpu_custom_call" | custom-call | tf_op jit(solution)/shard_map/exchange/pallas_call | solution.py:408
  11.1 2.4 %prepare.1 = (f32[6,8,128]{2,1,0:T(8,128)S(1)}, f32[3,96,8,128]{3,2,1,0:T(8,128)S(1)}, f32[3,110,8,128]{3,2,1,0:T(8,128)S(1)}, f32[3,96,8,128]{3,2,1,0:T(8,128)S(1)}, f32[8,128]{1,0:T(8,128)S(1)}) custom-call(f32[12,3,8,128]{3,2,1,0:T(8,128)S(1)} %get-tuple-element.22.gat_ref, f32[15,8,128]{2,1,0:T(8,128)S(1)} %get-tuple-element.23.pkt_ref, ...), custom_call_target="tpu_custom_call" | custom-call | tf_op jit(solution)/shard_map/prepare/pallas_call | solution.py:431
  13.5 7.7 %tile.1 = (f32[8,768]{1,0:T(8,128)S(1)}, f32[8,128]{1,0:T(8,128)S(1)}) custom-call(f32[3,96,8,128]{3,2,1,0:T(8,128)S(1)} %get-tuple-element.26.mine, f32[3,110,8,128]{3,2,1,0:T(8,128)S(1)} %get-tuple-element.27.others, f32[3,96,8,128]{3,2,1,0:T(8,128)S(1)} %get-tuple-element.28.part, f32[8,128]{1,0:T(8,128)S(1)} %get-tuple-element.29.eng_ref), custom_call_target="tpu_custom_call" | custom-call | tf_op jit(solution)/shard_map/tile/pallas_call | solution.py:439
  21.2 0.7 %finish.1 = (f32[3,729]{1,0:T(4,128)}, f32[3,729]{1,0:T(4,128)}, f32[3,729]{1,0:T(4,128)}, s32[729]{0:T(1024)}, s32[729]{0:T(1024)}, /*index=5*/f32[]{:T(128)}) custom-call(f32[6,8,128]{2,1,0:T(8,128)S(1)} %get-tuple-element.25.sorted_ref, f32[8,768]{1,0:T(8,128)S(1)} %get-tuple-element.30.frc_ref, f32[8,128]{1,0:T(8,128)S(1)} %get-tuple-element.31.total_ref), custom_call_target="tpu_custom_call" | custom-call | tf_op jit(solution)/shard_map/finish/pallas_call | solution.py:448

commit v3 on v2

--- a/solution.py
+++ b/solution.py
@@ -21,9 +21,10 @@
 NOWHERE = 1.0e9
 GHOST_SQ = RC * RC + 0.01
 PEERS = [(dz, dy, dx) for dz in range(NZ) for dy in range(NY) for dx in range(NX)][1:]
-GROUPS = [(1, 1, 1), (-1, 1, 1), (1, 1, 0), (-1, 1, 0), (1, 0, 1), (-1, 0, 1), (1, 0, 0), (-1, 0, 0), (0, 1, 1), (0, 1, 0), (0, 0, 1)]
+SIDES = [(1, 1), (1, 0), (0, 1), (0, 0)]
+GROUPS = [(gx, *side) for side in SIDES for gx in (1, -1)] + [(0, *side) for side in SIDES[:3]]
 N_GROUPS = len(GROUPS)
-DISTANT = [(2, 1, 1), (2, 1, 0), (2, 0, 1), (2, 0, 0)]
+DISTANT = [(2, *side) for side in SIDES]
 N_PACKETS = N_GROUPS + len(DISTANT)
 
 
@@ -43,6 +44,8 @@
 
 LANE_STARTS, LANE_BASE = lane_plan()
 STAY = 13
+NT_DIMS = (((1,), (1,)), ((), ()))
+NN_DIMS = (((1,), (0,)), ((), ()))
 
 
 def split3(values):
@@ -58,11 +61,11 @@
 
 
 def dot_nt(a, b):
-    return lax.dot_general(a, b, (((1,), (1,)), ((), ())), preferred_element_type=jnp.float32)
+    return lax.dot_general(a, b, NT_DIMS, preferred_element_type=jnp.float32)
 
 
 def dot_nn(a, b):
-    return lax.dot_general(a, b, (((1,), (0,)), ((), ())), preferred_element_type=jnp.float32)
+    return lax.dot_general(a, b, NN_DIMS, preferred_element_type=jnp.float32)
 
 
 def my_coords():
@@ -162,34 +165,44 @@
 MAX_ROWS = BLOCKS + CAND_ROWS
 GROUPS_OWN = BLOCKS * 16
 QUAD = 4
-FIXED_QUADS = 16
+FIXED_BLOCKS = 4
+FIXED_QUADS = FIXED_BLOCKS * 16 // QUAD
 FIXED_ROWS = 11
 
 
 def pair_tools(mine, others, rc2, wrap_box):
-    kappa = UPC / 48.0
-
-    def radial(dist_sq):
+    def powers(dist_sq):
         inv_r = lax.rsqrt(dist_sq)
         inv_2 = inv_r * inv_r
         inv_4 = inv_2 * inv_2
         term = inv_4 * inv_2 - 0.5
+        return inv_r, term, term * (inv_4 * inv_4)
+
+    cut_inv_r, cut_term, cut_core = powers(rc2)
+    kappa = -RC * cut_core
+    for ulps in (-3, -2, -1, 1, 2, 3):
+        trial = ulps * 2.0 ** -34 - RC * cut_core
+        kappa = jnp.where(trial * cut_inv_r == -cut_core, trial, kappa)
+
+    def radial(dist_sq):
+        inv_r, term, core = powers(dist_sq)
         tail = kappa * inv_r
-        return term * (inv_4 * inv_4) + tail, term * term, tail * dist_sq
+        return core + tail, term * term, tail * dist_sq
 
     def quad_energy(a, h):
         return ((a[0] + a[1]) + (a[2] + a[3])) - 12.0 * ((h[0] + h[1]) + (h[2] + h[3]))
 
     cut_f, cut_a, cut_h = radial(rc2)
+    del cut_f
     cut_energy = quad_energy([cut_a] * QUAD, [cut_h] * QUAD)
     own_minus_lane = lax.broadcasted_iota(jnp.int32, (8, LANES), 0) - lax.broadcasted_iota(jnp.int32, (8, LANES), 1)
 
     def load_own(first):
         return [[mine[axis, first + k] for axis in range(3)] for k in range(QUAD)]
 
-    def one_row(own, first, row, sums, with_self):
+    def one_row(own, first, row, sums, with_self, react=None, weight=None):
         other = [others[axis, row] for axis in range(3)]
-        force, energy, parts_a, parts_h = list(sums[:-1]), sums[-1], [], []
+        force, energy, parts_a, parts_h, pulls = list(sums[:-1]), sums[-1], [], [], []
         for k in range(QUAD):
             delta = [own[k][axis] - other[axis] for axis in range(3)]
             for axis, box, inv_box in wrap_box:
@@ -199,12 +212,17 @@
                 dist_sq = jnp.where(own_minus_lane == row * LANES - (first + k) * 8, rc2, dist_sq)
             dist_sq = jnp.minimum(dist_sq, rc2)
             scale, a, h = radial(dist_sq)
-            scale = scale - cut_f
+            pulls.append([scale * delta[axis] for axis in range(3)])
             for axis in range(3):
-                force[3 * k + axis] = force[3 * k + axis] + scale * delta[axis]
+                force[3 * k + axis] = force[3 * k + axis] + pulls[k][axis]
             parts_a.append(a)
             parts_h.append(h)
-        return tuple(force) + (energy + (quad_energy(parts_a, parts_h) - cut_energy),)
+        gain = quad_energy(parts_a, parts_h) - cut_energy
+        if react is not None:
+            gain = gain * weight
+            for axis in range(3):
+                react[axis, row] = react[axis, row] + ((pulls[0][axis] + pulls[1][axis]) + (pulls[2][axis] + pulls[3][axis]))
+        return tuple(force) + (energy + gain,)
 
     return load_own, one_row
 
@@ -217,6 +235,7 @@
     centre = [(index.astype(jnp.float32) + 0.5) * brick for index in (mx, my, mz)]
     box = [brick * float(size) for size in sizes]
     lane_1 = lax.broadcasted_iota(jnp.int32, (1, LANES), 1)
+    acc[:, pl.ds(0, FIXED_QUADS * QUAD)] = jnp.zeros((3, FIXED_QUADS * QUAD, 8, LANES), jnp.float32)
 
     arrived = []
     for block in range(2):
@@ -227,136 +246,170 @@
                 total = total + jnp.where((lane_1 >= first) & (lane_1 < last), pkt_ref[index], 0.0)
         arrived.append(total)
     arr = jnp.concatenate(arrived, axis=1)
-    data = jnp.concatenate([own_ref[0:8, :], arr], axis=1)
+    arr_ok = arr[6:7] > 0.5
+    stay_all = own_ref[8:9, :] >= 0.0
+    n_vec = jnp.sum(stay_all.astype(jnp.float32), axis=1, keepdims=True) + jnp.sum(arr_ok.astype(jnp.float32), axis=1, keepdims=True)
+    n_own = jnp.max(n_vec).astype(jnp.int32)
+    n_int = n_vec.astype(jnp.int32)
+    quads = lax.div(n_own + (8 * QUAD - 1), 8 * QUAD)
+    own_rows = lax.div(n_own + (LANES - 1), LANES)
+    beyond = gat_ref[0, 0, 4:6, :]
+    for slot in range(1, N_GROUPS + 1):
+        beyond = jnp.minimum(beyond, gat_ref[slot, 0, 4:6, :])
+    small = (jnp.min(beyond) > 0.5 * NOWHERE) & (n_own <= FIXED_BLOCKS * LANES)
+    eng_ref[1] = jnp.broadcast_to(n_vec, (8, LANES))
+    wide = jnp.max(brick) >= 2.0 * RC
     int_max = 2147483647
-    ids = lax.shift_left(data[6:7].astype(jnp.int32) - 1, 16) + data[7:8].astype(jnp.int32)
-    stay_rank = own_ref[8:9, :]
-    stay = stay_rank >= 0.0
-    arr_ok = arr[6:7] > 0.5
-    arr_id = jnp.where(arr_ok, ids[:, WIDE:], int_max)
-    own_id = jnp.where(stay, ids[:, :WIDE], int_max)
-    n_vec = jnp.sum(stay.astype(jnp.float32), axis=1, keepdims=True) + jnp.sum(arr_ok.astype(jnp.float32), axis=1, keepdims=True)
-    n_own = jnp.max(n_vec).astype(jnp.int32)
-
-    rel = []
-    for axis in range(3):
-        distant = [jnp.where(pkt_ref[N_GROUPS + k, 6:7, :] > 0.5, pkt_ref[N_GROUPS + k, axis:axis + 1, :], NOWHERE) for k in range(len(DISTANT))]
-        values = jnp.concatenate([gat_ref[:, axis].reshape(8 * (N_GROUPS + 1), LANES)] + distant + [jnp.full((4, LANES), NOWHERE, jnp.float32)], axis=0) - centre[axis]
-        values = jnp.where(values > 0.5 * box[axis], values - box[axis], jnp.where(values < -0.5 * box[axis], values + box[axis], values))
-        rel.append(values)
-    over = [jnp.maximum(jnp.abs(values) - half_l, 0.0) for values in rel]
-    gap_sq = over[0] * over[0] + over[1] * over[1] + over[2] * over[2]
-    ghost = ((gap_sq > 0.0) & (gap_sq < GHOST_SQ)).astype(jnp.float32).astype(jnp.bfloat16)
-    row_i = lax.broadcasted_iota(jnp.int32, (LANES, LANES), 0)
-    col_i = lax.broadcasted_iota(jnp.int32, (LANES, LANES), 1)
-    cum = dot_nn(ghost, (row_i <= col_i).astype(jnp.bfloat16)).astype(jnp.int32)
-    count = dot_nn(ghost, jnp.ones((LANES, LANES), jnp.bfloat16))
-    base = dot_nn((col_i < row_i).astype(jnp.bfloat16)[:CAND_ROWS, :CAND_ROWS], count.astype(jnp.bfloat16)).astype(jnp.int32) + n_vec.astype(jnp.int32)
-    count = count.astype(jnp.int32)
-    n_all = jnp.max(base[CAND_ROWS - 8:] + count[CAND_ROWS - 8:])
-    lane_c = lax.broadcasted_iota(jnp.int32, (CAND_ROWS, LANES), 1)
-    place = (lane_c - base) & (LANES - 1)
-    source = jnp.zeros((CAND_ROWS, LANES), jnp.int32)
-    for step in (64, 32, 16, 8, 4, 2, 1):
-        probe = jnp.take_along_axis(cum, source + (step - 1), axis=1)
-        source = jnp.where(probe <= place, source + step, source)
-    target = jnp.where(place < count, lax.shift_right_logical(base + place, 7), -1)
-    packed = [jnp.take_along_axis(values, source, axis=1) for values in rel]
-    arr_col = jnp.transpose(jnp.broadcast_to(arr_id, (8, 2 * LANES)), (1, 0))[:, 0:1]
-    own_col = jnp.transpose(jnp.broadcast_to(own_id, (8, WIDE)), (1, 0))[:, 0:1]
-    all_id = jnp.concatenate([own_id, arr_id], axis=1)
-    arr_before = jnp.sum((arr_col < all_id).astype(jnp.float32), axis=0, keepdims=True)
-    stay_before = jnp.sum((own_col < arr_id).astype(jnp.float32), axis=0, keepdims=True)
-    rank = jnp.concatenate([jnp.where(stay, stay_rank + arr_before[:, :WIDE], -1.0), jnp.where(arr_ok, stay_before + arr_before[:, WIDE:], -1.0)], axis=1).astype(jnp.int32)
-    parts = split3(data)
-    for block in range(BLOCKS):
-        pick = (lax.broadcasted_iota(jnp.int32, (LANES, WIDE + 2 * LANES), 0) + block * LANES == rank).astype(jnp.float32).astype(jnp.bfloat16)
-        rows_s = join3(jnp.transpose(dot_nt(pick, parts), (1, 0)))
-        sorted_ref[block] = rows_s
-        valid = lane_1 + block * LANES < n_vec.astype(jnp.int32)
-        own_rel = jnp.concatenate([rows_s[axis:axis + 1] - centre[axis] for axis in range(3)] + [rows_s[3:8]], axis=0)
-        columns = jnp.transpose(jnp.where(valid, own_rel, FAR_OWN), (1, 0))
-        for axis in range(3):
-            others[axis, block] = jnp.broadcast_to(jnp.where(valid, own_rel[axis:axis + 1], 0.0), (8, LANES))
-            mine[axis, pl.ds(block * 16, 16)] = jnp.broadcast_to(columns[:, axis:axis + 1], (LANES, LANES)).reshape(16, 8, LANES)
-
-    rows = lax.div(n_all + (LANES - 1), LANES)
-    own_rows = lax.div(n_own + (LANES - 1), LANES)
-
-    def pack_row(row, carry):
-        hit = target == row
-        filled = lane_1 + row * LANES < n_all
-        for axis in range(3):
-            own_part = jnp.where(row < own_rows, others[axis, row], 0.0)
-            values = jnp.sum(jnp.where(hit, packed[axis], 0.0), axis=0, keepdims=True)
-            others[axis, row] = jnp.where(filled, own_part + values, FAR_OTHER)
-        return carry
-
-    lax.fori_loop(lax.div(n_own, LANES), rows, pack_row, 0)
-
     rc2 = RC * RC + 0.0 * own_ref[8:16, 0:LANES]
     zero = jnp.zeros((8, LANES), jnp.float32)
-    acc[...] = jnp.zeros_like(acc)
-    quads = lax.div(n_own + (8 * QUAD - 1), 8 * QUAD)
     far = jnp.full((8, LANES), FAR_OTHER, jnp.float32)
 
-    def set_far(row, carry):
+    def build(blocks, tile_rows):
+        span = blocks * LANES
+        data = jnp.concatenate([own_ref[0:8, 0:span], arr], axis=1)
+        ids = lax.shift_left(data[6:7].astype(jnp.int32) - 1, 16) + data[7:8].astype(jnp.int32)
+        stay_rank = own_ref[8:9, 0:span]
+        stay = stay_rank >= 0.0
+        arr_id = jnp.where(arr_ok, ids[:, span:], int_max)
+        own_id = jnp.where(stay, ids[:, :span], int_max)
+
+        count_rows = (N_GROUPS + 1) * tile_rows
+        cand = -(-(count_rows + len(DISTANT)) // 8) * 8
+        rel = []
         for axis in range(3):
-            others[axis, row] = far
-        return carry
-
-    def excess(first_quad, last_quad, first_row, wrap_box, energy):
-        load_own, one_row = pair_tools(mine, others, rc2, wrap_box)
-
-        def quad(index, total):
-            first = index * QUAD
-            own = load_own(first)
-            sums = (zero,) * (3 * QUAD) + (total,)
-            sums = lax.fori_loop(first_row, rows, lambda row, part: one_row(own, first, row, part, True), sums)
-            for k in range(QUAD):
-                for axis in range(3):
-                    acc[axis, first + k] = sums[3 * k + axis]
-            return sums[-1]
-
-        return lax.fori_loop(first_quad, last_quad, quad, energy)
-
-    def plain():
-        short = jnp.where(rows > FIXED_ROWS, jnp.minimum(quads, FIXED_QUADS), 0)
-        energy = excess(0, short, FIXED_ROWS, [], zero)
-        eng_ref[...] = excess(FIXED_QUADS, quads, 0, [], energy)
-        lax.fori_loop(rows, FIXED_ROWS, set_far, 0)
-
-    def wrapped():
-        wrap_box = [(axis, box[axis], 1.0 / box[axis]) for axis in (1, 2)]
-        eng_ref[...] = excess(0, quads, 0, wrap_box, zero)
-        lax.fori_loop(0, FIXED_ROWS, set_far, 0)
-
-    wide = jnp.max(brick) >= 2.0 * RC
-    pl.when(wide)(plain)
-    pl.when(jnp.logical_not(wide))(wrapped)
-
-
-def tile_kernel(mine, others, part, eng_ref, frc_ref, out_ref, acc, eng, slots, send_sem, recv_sem):
+            near = [gat_ref[slot, axis, 0:tile_rows, :] for slot in range(N_GROUPS + 1)]
+            distant = [jnp.where(pkt_ref[N_GROUPS + k, 6:7, :] > 0.5, pkt_ref[N_GROUPS + k, axis:axis + 1, :], NOWHERE) for k in range(len(DISTANT))]
+            values = jnp.concatenate(near + distant + [jnp.full((cand - count_rows - len(DISTANT), LANES), NOWHERE, jnp.float32)], axis=0) - centre[axis]
+            rel.append(jnp.where(values > 0.5 * box[axis], values - box[axis], jnp.where(values < -0.5 * box[axis], values + box[axis], values)))
+        over = [jnp.maximum(jnp.abs(values) - half_l, 0.0) for values in rel]
+        gap_sq = over[0] * over[0] + over[1] * over[1] + over[2] * over[2]
+        ghost = ((gap_sq > 0.0) & (gap_sq < GHOST_SQ)).astype(jnp.float32).astype(jnp.bfloat16)
+        row_i = lax.broadcasted_iota(jnp.int32, (LANES, LANES), 0)
+        col_i = lax.broadcasted_iota(jnp.int32, (LANES, LANES), 1)
+        cum = dot_nn(ghost, (row_i <= col_i).astype(jnp.bfloat16)).astype(jnp.int32)
+        count = dot_nn(ghost, jnp.ones((LANES, LANES), jnp.bfloat16))
+        arr_col = jnp.transpose(jnp.broadcast_to(arr_id, (8, 2 * LANES)), (1, 0))[:, 0:1]
+        own_col = jnp.transpose(jnp.broadcast_to(own_id, (8, span)), (1, 0))[:, 0:1]
+        all_id = jnp.concatenate([own_id, arr_id], axis=1)
+        arr_before = jnp.sum((arr_col < all_id).astype(jnp.float32), axis=0, keepdims=True)
+        stay_before = jnp.sum((own_col < arr_id).astype(jnp.float32), axis=0, keepdims=True)
+        rank = jnp.concatenate([jnp.where(stay, stay_rank + arr_before[:, :span], -1.0), jnp.where(arr_ok, stay_before + arr_before[:, span:], -1.0)], axis=1).astype(jnp.int32)
+        base = dot_nn((col_i < row_i).astype(jnp.bfloat16)[:cand, :cand], count.astype(jnp.bfloat16)).astype(jnp.int32) + n_int
+        count = count.astype(jnp.int32)
+        n_all = jnp.max(base[cand - 8:] + count[cand - 8:])
+        place = (lax.broadcasted_iota(jnp.int32, (cand, LANES), 1) - base) & (LANES - 1)
+        parts = split3(data)
+
+        def place_block(block):
+            pick = (lax.broadcasted_iota(jnp.int32, (LANES, span + 2 * LANES), 0) + block * LANES == rank).astype(jnp.float32).astype(jnp.bfloat16)
+            rows_s = join3(jnp.transpose(dot_nt(pick, parts), (1, 0)))
+            sorted_ref[block] = rows_s
+            valid = lane_1 + block * LANES < n_int
+            own_rel = jnp.concatenate([rows_s[axis:axis + 1] - centre[axis] for axis in range(3)] + [rows_s[3:8]], axis=0)
+            columns = jnp.transpose(jnp.where(valid, own_rel, FAR_OWN), (1, 0))
+            for axis in range(3):
+                others[axis, block] = jnp.broadcast_to(jnp.where(valid, own_rel[axis:axis + 1], 0.0), (8, LANES))
+                mine[axis, pl.ds(block * 16, 16)] = jnp.broadcast_to(columns[:, axis:axis + 1], (LANES, LANES)).reshape(16, 8, LANES)
+
+        wanted = lax.broadcasted_iota(jnp.int32, (cand, LANES), 1)
+        source = jnp.zeros((cand, LANES), jnp.int32)
+        waiting = list(range(blocks))
+        for stride, probes in ((16, 7), (2, 7), (1, 1)):
+            below = jnp.zeros((cand, LANES), jnp.int32)
+            for k in range(1, probes + 1):
+                probe = jnp.take_along_axis(cum, source + (stride * k - 1), axis=1)
+                below = below + (probe <= wanted).astype(jnp.int32)
+            source = source + stride * below
+            for block in waiting[:2]:
+                place_block(block)
+            waiting = waiting[2:]
+        source = jnp.take_along_axis(source & (LANES - 1), place, axis=1)
+        for block in range(blocks, BLOCKS):
+            sorted_ref[block] = zero
+        target = jnp.where(place < count, lax.shift_right_logical(base + place, 7), -1)
+        packed = [jnp.take_along_axis(values, source, axis=1) for values in rel]
+        rows = lax.div(n_all + (LANES - 1), LANES)
+
+        def pack_row(row, carry):
+            hit = target == row
+            filled = lane_1 + row * LANES < n_all
+            for axis in range(3):
+                own_part = jnp.where(row < own_rows, others[axis, row], 0.0)
+                values = jnp.sum(jnp.where(hit, packed[axis], 0.0), axis=0, keepdims=True)
+                others[axis, row] = jnp.where(filled, own_part + values, FAR_OTHER)
+            return carry
+
+        lax.fori_loop(lax.div(n_own, LANES), rows, pack_row, 0)
+
+        def set_far(row, carry):
+            for axis in range(3):
+                others[axis, row] = far
+            return carry
+
+        def excess(first_quad, last_quad, first_row, wrap_box, energy):
+            load_own, one_row = pair_tools(mine, others, rc2, wrap_box)
+
+            def quad(index, total):
+                first = index * QUAD
+                own = load_own(first)
+                sums = (zero,) * (3 * QUAD) + (total,)
+                sums = lax.fori_loop(first_row, rows, lambda row, part: one_row(own, first, row, part, True), sums)
+                for k in range(QUAD):
+                    for axis in range(3):
+                        acc[axis, first + k] = sums[3 * k + axis]
+                return sums[-1]
+
+            return lax.fori_loop(first_quad, last_quad, quad, energy)
+
+        def plain():
+            short = jnp.where(rows > FIXED_ROWS, jnp.minimum(quads, FIXED_QUADS), 0)
+            energy = excess(0, short, FIXED_ROWS, [], zero)
+            if blocks > FIXED_BLOCKS:
+                energy = excess(FIXED_QUADS, quads, 0, [], energy)
+            eng_ref[0] = energy
+            lax.fori_loop(rows, FIXED_ROWS, set_far, 0)
+
+        def wrapped():
+            wrap_box = [(axis, box[axis], 1.0 / box[axis]) for axis in (1, 2)]
+            eng_ref[0] = excess(0, quads, 0, wrap_box, zero)
+            lax.fori_loop(0, FIXED_ROWS, set_far, 0)
+
+        pl.when(wide)(plain)
+        pl.when(jnp.logical_not(wide))(wrapped)
+
+    pl.when(small)(lambda: build(FIXED_BLOCKS, 4))
+    pl.when(jnp.logical_not(small))(lambda: build(BLOCKS, 8))
+
+
+def tile_kernel(mine, others, part, eng_ref, frc_ref, out_ref, acc, react, eng, slots, send_sem, recv_sem):
     coords = my_coords()
     mz, my, mx = coords
     barrier = entry_signals(coords)
     rc2 = RC * RC + 0.0 * mine[0, 0]
     load_own, one_row = pair_tools(mine, others, rc2, [])
 
-    def quad(index, energy):
-        first = index * QUAD
-        own = load_own(first)
-        self_row = lax.div(first, 16)
-        sums = tuple(part[axis, first + k] for k in range(QUAD) for axis in range(3)) + (energy,)
-        sums = one_row(own, first, self_row, sums, True)
-        for count in range(FIXED_ROWS - 1):
-            sums = one_row(own, first, count + (count >= self_row).astype(jnp.int32), sums, False)
-        for k in range(QUAD):
-            for axis in range(3):
-                acc[axis, first + k] = sums[3 * k + axis]
-        return sums[-1]
-
-    energy = lax.fori_loop(0, FIXED_QUADS, quad, eng_ref[...])
+    lane_8 = lax.broadcasted_iota(jnp.int32, (8, LANES), 1).astype(jnp.float32)
+    weights = [jnp.where(lane_8 + float(row * LANES) < eng_ref[1], 2.0, 1.0) for row in range(FIXED_BLOCKS)]
+    react[...] = jnp.zeros_like(react)
+    energy = eng_ref[0]
+    for block in range(FIXED_BLOCKS):
+
+        def quad(index, total, block=block):
+            first = block * 16 + index * QUAD
+            own = load_own(first)
+            sums = tuple(part[axis, first + k] for k in range(QUAD) for axis in range(3)) + (total,)
+            sums = one_row(own, first, block, sums, True)
+            for row in range(block + 1, FIXED_ROWS):
+                if row < FIXED_BLOCKS:
+                    sums = one_row(own, first, row, sums, False, react, weights[row])
+                else:
+                    sums = one_row(own, first, row, sums, False)
+            for k in range(QUAD):
+                for axis in range(3):
+                    acc[axis, first + k] = sums[3 * k + axis]
+            return sums[-1]
+
+        energy = lax.fori_loop(0, 16 // QUAD, quad, energy)
     eng[...] = jnp.full((8, LANES), 2.0 * jnp.sum(energy), jnp.float32)
     pl.semaphore_wait(barrier, len(PEERS))
     place = (mz * NY + my) * NX + mx
@@ -366,10 +419,13 @@
         copies[-1].start()
     slots[place] = eng[...]
     for block in range(BLOCKS):
-        held = acc if block < FIXED_QUADS * QUAD // 16 else part
+        held = acc if block < FIXED_BLOCKS else part
         for axis in range(3):
             turned = jnp.transpose(held[axis, pl.ds(block * 16, 16)].reshape(LANES, LANES), (1, 0))
-            frc_ref[axis:axis + 1, block * LANES:(block + 1) * LANES] = 48.0 * jnp.sum(turned, axis=0, keepdims=True)
+            force = jnp.sum(turned, axis=0, keepdims=True)
+            if 0 < block < FIXED_BLOCKS:
+                force = force - jnp.sum(react[axis, block], axis=0, keepdims=True)
+            frc_ref[axis:axis + 1, block * LANES:(block + 1) * LANES] = 48.0 * force
     for copy in copies:
         copy.wait()
     total = slots[0]
@@ -430,7 +486,7 @@
         own_tiles = jax.ShapeDtypeStruct((3, GROUPS_OWN, 8, LANES), f32)
         placed, mine, others, part, eng = pl.pallas_call(
             prepare_kernel,
-            out_shape=(jax.ShapeDtypeStruct((BLOCKS, 8, LANES), f32), own_tiles, jax.ShapeDtypeStruct((3, MAX_ROWS, 8, LANES), f32), own_tiles, jax.ShapeDtypeStruct((8, LANES), f32)),
+            out_shape=(jax.ShapeDtypeStruct((BLOCKS, 8, LANES), f32), own_tiles, jax.ShapeDtypeStruct((3, MAX_ROWS, 8, LANES), f32), own_tiles, jax.ShapeDtypeStruct((2, 8, LANES), f32)),
             in_specs=[VMEM_SPEC] * 3,
             out_specs=(VMEM_SPEC,) * 5,
             compiler_params=pltpu.CompilerParams(vmem_limit_bytes=VMEM_LIMIT),
@@ -441,7 +497,7 @@
             out_shape=(jax.ShapeDtypeStruct((8, WIDE), f32), jax.ShapeDtypeStruct((8, LANES), f32)),
             in_specs=[VMEM_SPEC] * 4,
             out_specs=(VMEM_SPEC,) * 2,
-            scratch_shapes=[pltpu.VMEM((3, GROUPS_OWN, 8, LANES), f32), pltpu.VMEM((8, LANES), f32), pltpu.VMEM((n_dev, 8, LANES), f32), pltpu.SemaphoreType.DMA((n_dev - 1,)), pltpu.SemaphoreType.DMA((n_dev - 1,))],
+            scratch_shapes=[pltpu.VMEM((3, FIXED_BLOCKS * 16, 8, LANES), f32), pltpu.VMEM((3, FIXED_BLOCKS, 8, LANES), f32), pltpu.VMEM((8, LANES), f32), pltpu.VMEM((n_dev, 8, LANES), f32), pltpu.SemaphoreType.DMA((n_dev - 1,)), pltpu.SemaphoreType.DMA((n_dev - 1,))],
             compiler_params=pltpu.CompilerParams(collective_id=1, has_side_effects=True, vmem_limit_bytes=VMEM_LIMIT),
             name="tile",
         )(mine, others, part, eng)

time: 22.1 us -> 21.2 us (0.959)
  Pallas kernels: 20.5 us -> 19.6 us
    pallas_call x1, Pallas kernels: 2.38 us -> 1.81 us  [local_step(): pl.pallas_call(prepare_kernel, out_shape=(jax.ShapeDtypeStruct((BLOCKS, 8...]
    pallas_call x1, Pallas kernels: 7.68 us -> 7.36 us  [local_step(): pl.pallas_call(tile_kernel, out_shape=(jax.ShapeDtypeStruct((8, WIDE), f3...]
where the time goes in v3:
time: 21.2 us; the launch traced here: 20.9 us
  Pallas kernels  19.6 us (92%)
  between operations  1.3 us (6%)
    pallas_call x1, Pallas kernels, local_step(): pl.pallas_call(exchange_kernel, out_shape=(jax.ShapeDtypeStruct((N_GROUPS...  9.82 us
    pallas_call x1, Pallas kernels, local_step(): pl.pallas_call(tile_kernel, out_shape=(jax.ShapeDtypeStruct((8, WIDE), f3...  7.36 us
    pallas_call x1, Pallas kernels, local_step(): pl.pallas_call(prepare_kernel, out_shape=(jax.ShapeDtypeStruct((BLOCKS, 8...  1.81 us
    pallas_call x1, Pallas kernels, local_step(): pl.pallas_call(finish_kernel, out_shape=(jax.ShapeDtypeStruct((3, CAP), f...  0.65 us

profile of v3, /device:TPU:0, one launch (start us, length us, event | category | flops | bytes accessed | tf_op | source)
XLA Modules:
  0.0 20.9 jit_solution(4901505139747386610)
XLA Ops:
  1.3 9.8 %exchange.1 = (f32[12,3,8,128]{3,2,1,0:T(8,128)S(1)}, f32[15,8,128]{2,1,0:T(8,128)S(1)}, f32[16,768]{1,0:T(8,128)S(1)}) custom-call(f32[]{:T(128)S(6)} %copy.12.brick_ref, f32[3,729]{1,0:T(4,128)} %bitcast.6, f32[3,729]{1,0:T(4,128)} %bitcast.7, f32[3,729]{1,0:T(4,128)} %bitcast.8, s32[729]{0:T(1024)} %id_ref.1, s32[729]{0:T(1024)} %ok_ref.1), custom_call_target="tpu_custom_call" | custom-call | tf_op jit(solution)/shard_map/exchange/pallas_call | solution.py:464
  11.1 1.8 %prepare.1 = (f32[6,8,128]{2,1,0:T(8,128)S(1)}, f32[3,96,8,128]{3,2,1,0:T(8,128)S(1)}, f32[3,110,8,128]{3,2,1,0:T(8,128)S(1)}, f32[3,96,8,128]{3,2,1,0:T(8,128)S(1)}, f32[2,8,128]{2,1,0:T(8,128)S(1)}) custom-call(f32[12,3,8,128]{3,2,1,0:T(8,128)S(1)} %get-tuple-element.22.gat_ref, f32[15,8,128]{2,1,0:T(8,128)S(1)} %get-tuple-element.23.pkt_ref, ...), custom_call_target="tpu_custom_call" | custom-call | tf_op jit(solution)/shard_map/prepare/pallas_call | solution.py:487
  12.9 7.4 %tile.1 = (f32[8,768]{1,0:T(8,128)S(1)}, f32[8,128]{1,0:T(8,128)S(1)}) custom-call(f32[3,96,8,128]{3,2,1,0:T(8,128)S(1)} %get-tuple-element.26.mine, f32[3,110,8,128]{3,2,1,0:T(8,128)S(1)} %get-tuple-element.27.others, f32[3,96,8,128]{3,2,1,0:T(8,128)S(1)} %get-tuple-element.28.part, f32[2,8,128]{2,1,0:T(8,128)S(1)} %get-tuple-element.29.eng_ref), custom_call_target="tpu_custom_call" | custom-call | tf_op jit(solution)/shard_map/tile/pallas_call | solution.py:495
  20.3 0.7 %finish.1 = (f32[3,729]{1,0:T(4,128)}, f32[3,729]{1,0:T(4,128)}, f32[3,729]{1,0:T(4,128)}, s32[729]{0:T(1024)}, s32[729]{0:T(1024)}, /*index=5*/f32[]{:T(128)}) custom-call(f32[6,8,128]{2,1,0:T(8,128)S(1)} %get-tuple-element.25.sorted_ref, f32[8,768]{1,0:T(8,128)S(1)} %get-tuple-element.30.frc_ref, f32[8,128]{1,0:T(8,128)S(1)} %get-tuple-element.31.total_ref), custom_call_target="tpu_custom_call" | custom-call | tf_op jit(solution)/shard_map/finish/pallas_call | solution.py:504

commit v4 on v3

--- a/solution.py
+++ b/solution.py
@@ -20,7 +20,7 @@
 FAR_OTHER = -1.0e4
 NOWHERE = 1.0e9
 GHOST_SQ = RC * RC + 0.01
-PEERS = [(dz, dy, dx) for dz in range(NZ) for dy in range(NY) for dx in range(NX)][1:]
+PEERS = [(dz, dy, dx) for dz in range(NZ) for dy in range(NY) for dx in range(NX)][:0:-1]
 SIDES = [(1, 1), (1, 0), (0, 1), (0, 0)]
 GROUPS = [(gx, *side) for side in SIDES for gx in (1, -1)] + [(0, *side) for side in SIDES[:3]]
 N_GROUPS = len(GROUPS)
@@ -115,16 +115,13 @@
         half.append(half_v)
     code = jnp.where(owned, code, -1)
     for axis in range(3):
-        for block in range(8):
-            if block < BLOCKS:
-                lanes = slice(block * LANES, (block + 1) * LANES)
-                send_pos[axis, block:block + 1, :] = jnp.where(owned[:, lanes], moved[axis][:, lanes], NOWHERE)
-            else:
-                send_pos[axis, block:block + 1, :] = jnp.full((1, LANES), NOWHERE, jnp.float32)
+        for block in range(BLOCKS):
+            lanes = slice(block * LANES, (block + 1) * LANES)
+            send_pos[axis, block:block + 1, :] = jnp.where(owned[:, lanes], moved[axis][:, lanes], NOWHERE)
     ids = int_ref[0:1, :]
     id_hi = (lax.shift_right_logical(ids, 16) + 1).astype(jnp.float32)
     id_lo = (ids & 65535).astype(jnp.float32)
-    data = jnp.concatenate(moved + half + [id_hi, id_lo], axis=0)
+    data = jnp.concatenate(moved + [id_hi] + half + [id_lo], axis=0)
     member = (jnp.broadcast_to(code, (32, WIDE)) == lax.broadcasted_iota(jnp.int32, (32, WIDE), 0)).astype(jnp.float32)
     tri = (lax.broadcasted_iota(jnp.int32, (LANES, LANES), 0) < lax.broadcasted_iota(jnp.int32, (LANES, LANES), 1)).astype(jnp.bfloat16)
     codes = lax.broadcasted_iota(jnp.int32, (32, LANES), 0)
@@ -153,8 +150,10 @@
         if index < N_GROUPS:
             copies.append(pltpu.make_async_remote_copy(src_ref=send_pos, dst_ref=gat_ref.at[index], send_sem=pos_send_sem.at[index], recv_sem=pos_recv_sem.at[index], device_id=peer, device_id_type=MESH))
             copies[-1].start()
-        block = LANE_STARTS[index][0] if index < N_GROUPS else 0
-        copies.append(pltpu.make_async_remote_copy(src_ref=send_pkt.at[block], dst_ref=pkt_ref.at[index], send_sem=pkt_send_sem.at[index], recv_sem=pkt_recv_sem.at[index], device_id=peer, device_id_type=MESH))
+            source, target = send_pkt.at[LANE_STARTS[index][0]], pkt_ref.at[index]
+        else:
+            source, target = send_pkt.at[0, 0:4], pkt_ref.at[index, 0:4]
+        copies.append(pltpu.make_async_remote_copy(src_ref=source, dst_ref=target, send_sem=pkt_send_sem.at[index], recv_sem=pkt_recv_sem.at[index], device_id=peer, device_id_type=MESH))
         copies[-1].start()
     gat_ref[N_GROUPS] = send_pos[...]
     for copy in copies:
@@ -246,7 +245,7 @@
                 total = total + jnp.where((lane_1 >= first) & (lane_1 < last), pkt_ref[index], 0.0)
         arrived.append(total)
     arr = jnp.concatenate(arrived, axis=1)
-    arr_ok = arr[6:7] > 0.5
+    arr_ok = arr[3:4] > 0.5
     stay_all = own_ref[8:9, :] >= 0.0
     n_vec = jnp.sum(stay_all.astype(jnp.float32), axis=1, keepdims=True) + jnp.sum(arr_ok.astype(jnp.float32), axis=1, keepdims=True)
     n_own = jnp.max(n_vec).astype(jnp.int32)
@@ -267,7 +266,7 @@
     def build(blocks, tile_rows):
         span = blocks * LANES
         data = jnp.concatenate([own_ref[0:8, 0:span], arr], axis=1)
-        ids = lax.shift_left(data[6:7].astype(jnp.int32) - 1, 16) + data[7:8].astype(jnp.int32)
+        ids = lax.shift_left(data[3:4].astype(jnp.int32) - 1, 16) + data[7:8].astype(jnp.int32)
         stay_rank = own_ref[8:9, 0:span]
         stay = stay_rank >= 0.0
         arr_id = jnp.where(arr_ok, ids[:, span:], int_max)
@@ -278,7 +277,7 @@
         rel = []
         for axis in range(3):
             near = [gat_ref[slot, axis, 0:tile_rows, :] for slot in range(N_GROUPS + 1)]
-            distant = [jnp.where(pkt_ref[N_GROUPS + k, 6:7, :] > 0.5, pkt_ref[N_GROUPS + k, axis:axis + 1, :], NOWHERE) for k in range(len(DISTANT))]
+            distant = [jnp.where(pkt_ref[N_GROUPS + k, 3:4, :] > 0.5, pkt_ref[N_GROUPS + k, axis:axis + 1, :], NOWHERE) for k in range(len(DISTANT))]
             values = jnp.concatenate(near + distant + [jnp.full((cand - count_rows - len(DISTANT), LANES), NOWHERE, jnp.float32)], axis=0) - centre[axis]
             rel.append(jnp.where(values > 0.5 * box[axis], values - box[axis], jnp.where(values < -0.5 * box[axis], values + box[axis], values)))
         over = [jnp.maximum(jnp.abs(values) - half_l, 0.0) for values in rel]
@@ -378,7 +377,7 @@
         pl.when(jnp.logical_not(wide))(wrapped)
 
     pl.when(small)(lambda: build(FIXED_BLOCKS, 4))
-    pl.when(jnp.logical_not(small))(lambda: build(BLOCKS, 8))
+    pl.when(jnp.logical_not(small))(lambda: build(BLOCKS, BLOCKS))
 
 
 def tile_kernel(mine, others, part, eng_ref, frc_ref, out_ref, acc, react, eng, slots, send_sem, recv_sem):
@@ -410,7 +409,7 @@
             return sums[-1]
 
         energy = lax.fori_loop(0, 16 // QUAD, quad, energy)
-    eng[...] = jnp.full((8, LANES), 2.0 * jnp.sum(energy), jnp.float32)
+    eng[...] = jnp.full((1, LANES), 2.0 * jnp.sum(energy), jnp.float32)
     pl.semaphore_wait(barrier, len(PEERS))
     place = (mz * NY + my) * NX + mx
     copies = []
@@ -440,13 +439,13 @@
         width = min(LANES, CAP - block * LANES)
         lanes = slice(block * LANES, block * LANES + width)
         rows_s = sorted_ref[block]
-        valid = rows_s[6:7] > 0.5
+        valid = rows_s[3:4] > 0.5
         for axis in range(3):
             force = jnp.where(valid, frc_ref[axis:axis + 1, block * LANES:(block + 1) * LANES], 0.0)
             frc_out[axis:axis + 1, lanes] = force[:, :width]
-            vel_out[axis:axis + 1, lanes] = (rows_s[3 + axis:4 + axis] + (0.5 * DT) * force)[:, :width]
+            vel_out[axis:axis + 1, lanes] = (rows_s[4 + axis:5 + axis] + (0.5 * DT) * force)[:, :width]
             pos_out[axis:axis + 1, lanes] = rows_s[axis:axis + 1, :width]
-        new_id = lax.shift_left(rows_s[6:7].astype(jnp.int32) - 1, 16) + rows_s[7:8].astype(jnp.int32)
+        new_id = lax.shift_left(rows_s[3:4].astype(jnp.int32) - 1, 16) + rows_s[7:8].astype(jnp.int32)
         id_out[lanes] = jnp.where(valid, new_id, 0)[:, :width].reshape(width)
         ok_out[lanes] = valid.astype(jnp.int32)[:, :width].reshape(width)
 
@@ -463,7 +462,7 @@
         n_dev = NZ * NY * NX
         gat, pkt, own = pl.pallas_call(
             exchange_kernel,
-            out_shape=(jax.ShapeDtypeStruct((N_GROUPS + 1, 3, 8, LANES), f32), jax.ShapeDtypeStruct((N_PACKETS, 8, LANES), f32), jax.ShapeDtypeStruct((16, WIDE), f32)),
+            out_shape=(jax.ShapeDtypeStruct((N_GROUPS + 1, 3, BLOCKS, LANES), f32), jax.ShapeDtypeStruct((N_PACKETS, 8, LANES), f32), jax.ShapeDtypeStruct((16, WIDE), f32)),
             in_specs=[SMEM_SPEC] + [HBM_SPEC] * 5,
             out_specs=(VMEM_SPEC,) * 3,
             scratch_shapes=[
@@ -472,7 +471,7 @@
                 pltpu.VMEM((CAP,), jnp.int32),
                 pltpu.VMEM((3, 4, WIDE), f32),
                 pltpu.VMEM((2, WIDE), jnp.int32),
-                pltpu.VMEM((3, 8, LANES), f32),
+                pltpu.VMEM((3, BLOCKS, LANES), f32),
                 pltpu.VMEM((2, 8, LANES), f32),
                 pltpu.SemaphoreType.DMA((5,)),
                 pltpu.SemaphoreType.DMA((N_GROUPS,)),
@@ -494,10 +493,10 @@
         )(gat, pkt, own)
         frc_rows, total = pl.pallas_call(
             tile_kernel,
-            out_shape=(jax.ShapeDtypeStruct((8, WIDE), f32), jax.ShapeDtypeStruct((8, LANES), f32)),
+            out_shape=(jax.ShapeDtypeStruct((8, WIDE), f32), jax.ShapeDtypeStruct((1, LANES), f32)),
             in_specs=[VMEM_SPEC] * 4,
             out_specs=(VMEM_SPEC,) * 2,
-            scratch_shapes=[pltpu.VMEM((3, FIXED_BLOCKS * 16, 8, LANES), f32), pltpu.VMEM((3, FIXED_BLOCKS, 8, LANES), f32), pltpu.VMEM((8, LANES), f32), pltpu.VMEM((n_dev, 8, LANES), f32), pltpu.SemaphoreType.DMA((n_dev - 1,)), pltpu.SemaphoreType.DMA((n_dev - 1,))],
+            scratch_shapes=[pltpu.VMEM((3, FIXED_BLOCKS * 16, 8, LANES), f32), pltpu.VMEM((3, FIXED_BLOCKS, 8, LANES), f32), pltpu.VMEM((1, LANES), f32), pltpu.VMEM((n_dev, 1, LANES), f32), pltpu.SemaphoreType.DMA((n_dev - 1,)), pltpu.SemaphoreType.DMA((n_dev - 1,))],
             compiler_params=pltpu.CompilerParams(collective_id=1, has_side_effects=True, vmem_limit_bytes=VMEM_LIMIT),
             name="tile",
         )(mine, others, part, eng)

time: 21.2 us -> 20.5 us (0.967)
  Pallas kernels: 19.6 us -> 19 us
    pallas_call x1, Pallas kernels: 9.82 us -> 9.49 us  [local_step(): pl.pallas_call(exchange_kernel, out_shape=(jax.ShapeDtypeStruct((N_GROUPS...]
    pallas_call x1, Pallas kernels: 7.36 us -> 7.04 us  [local_step(): pl.pallas_call(tile_kernel, out_shape=(jax.ShapeDtypeStruct((8, WIDE), f3...]
where the time goes in v4:
time: 20.5 us; the launch traced here: 20.3 us
  Pallas kernels  19 us (93%)
  between operations  1.3 us (6%)
    pallas_call x1, Pallas kernels, local_step(): pl.pallas_call(exchange_kernel, out_shape=(jax.ShapeDtypeStruct((N_GROUPS...  9.49 us
    pallas_call x1, Pallas kernels, local_step(): pl.pallas_call(tile_kernel, out_shape=(jax.ShapeDtypeStruct((8, WIDE), f3...  7.04 us
    pallas_call x1, Pallas kernels, local_step(): pl.pallas_call(prepare_kernel, out_shape=(jax.ShapeDtypeStruct((BLOCKS, 8...  1.78 us
    pallas_call x1, Pallas kernels, local_step(): pl.pallas_call(finish_kernel, out_shape=(jax.ShapeDtypeStruct((3, CAP), f...  0.65 us

profile of v4, /device:TPU:0, one launch (start us, length us, event | category | flops | bytes accessed | tf_op | source)
XLA Modules:
  0.0 20.3 jit_solution(10184990611171348469)
XLA Ops:
  1.3 9.5 %exchange.1 = (f32[12,3,6,128]{3,2,1,0:T(8,128)S(1)}, f32[15,8,128]{2,1,0:T(8,128)S(1)}, f32[16,768]{1,0:T(8,128)S(1)}) custom-call(f32[]{:T(128)S(6)} %copy.12.brick_ref, f32[3,729]{1,0:T(4,128)} %bitcast.6, f32[3,729]{1,0:T(4,128)} %bitcast.7, f32[3,729]{1,0:T(4,128)} %bitcast.8, s32[729]{0:T(1024)} %id_ref.1, s32[729]{0:T(1024)} %ok_ref.1), custom_call_target="tpu_custom_call" | custom-call | tf_op jit(solution)/shard_map/exchange/pallas_call | solution.py:463
  10.8 1.8 %prepare.1 = (f32[6,8,128]{2,1,0:T(8,128)S(1)}, f32[3,96,8,128]{3,2,1,0:T(8,128)S(1)}, f32[3,110,8,128]{3,2,1,0:T(8,128)S(1)}, f32[3,96,8,128]{3,2,1,0:T(8,128)S(1)}, f32[2,8,128]{2,1,0:T(8,128)S(1)}) custom-call(f32[12,3,6,128]{3,2,1,0:T(8,128)S(1)} %get-tuple-element.22.gat_ref, f32[15,8,128]{2,1,0:T(8,128)S(1)} %get-tuple-element.23.pkt_ref, ...), custom_call_target="tpu_custom_call" | custom-call | tf_op jit(solution)/shard_map/prepare/pallas_call | solution.py:486
  12.6 7.0 %tile.1 = (f32[8,768]{1,0:T(8,128)S(1)}, f32[1,128]{1,0:T(1,128)S(1)}) custom-call(f32[3,96,8,128]{3,2,1,0:T(8,128)S(1)} %get-tuple-element.26.mine, f32[3,110,8,128]{3,2,1,0:T(8,128)S(1)} %get-tuple-element.27.others, f32[3,96,8,128]{3,2,1,0:T(8,128)S(1)} %get-tuple-element.28.part, f32[2,8,128]{2,1,0:T(8,128)S(1)} %get-tuple-element.29.eng_ref), custom_call_target="tpu_custom_call" | custom-call | tf_op jit(solution)/shard_map/tile/pallas_call | solution.py:494
  19.6 0.6 %finish.1 = (f32[3,729]{1,0:T(4,128)}, f32[3,729]{1,0:T(4,128)}, f32[3,729]{1,0:T(4,128)}, s32[729]{0:T(1024)}, s32[729]{0:T(1024)}, /*index=5*/f32[]{:T(128)}) custom-call(f32[6,8,128]{2,1,0:T(8,128)S(1)} %get-tuple-element.25.sorted_ref, f32[8,768]{1,0:T(8,128)S(1)} %get-tuple-element.30.frc_ref, f32[1,128]{1,0:T(1,128)S(1)} %get-tuple-element.31.total_ref), custom_call_target="tpu_custom_call" | custom-call | tf_op jit(solution)/shard_map/finish/pallas_call | solution.py:503

commit v5 on v4

--- a/solution.py
+++ b/solution.py
@@ -183,25 +183,25 @@
         trial = ulps * 2.0 ** -34 - RC * cut_core
         kappa = jnp.where(trial * cut_inv_r == -cut_core, trial, kappa)
 
-    def radial(dist_sq):
-        inv_r, term, core = powers(dist_sq)
-        tail = kappa * inv_r
-        return core + tail, term * term, tail * dist_sq
-
-    def quad_energy(a, h):
-        return ((a[0] + a[1]) + (a[2] + a[3])) - 12.0 * ((h[0] + h[1]) + (h[2] + h[3]))
-
-    cut_f, cut_a, cut_h = radial(rc2)
-    del cut_f
-    cut_energy = quad_energy([cut_a] * QUAD, [cut_h] * QUAD)
+    def quad_energy(dist_sqs):
+        terms, tails = [], []
+        for dist_sq in dist_sqs:
+            inv_r = lax.rsqrt(dist_sq)
+            inv_2 = inv_r * inv_r
+            term = inv_2 * inv_2 * inv_2 - 0.5
+            terms.append(term * term)
+            tails.append(kappa * inv_r * dist_sq)
+        return ((terms[0] + terms[1]) + (terms[2] + terms[3])) - 12.0 * ((tails[0] + tails[1]) + (tails[2] + tails[3]))
+
+    cut_energy = quad_energy([rc2] * QUAD)
     own_minus_lane = lax.broadcasted_iota(jnp.int32, (8, LANES), 0) - lax.broadcasted_iota(jnp.int32, (8, LANES), 1)
 
     def load_own(first):
         return [[mine[axis, first + k] for axis in range(3)] for k in range(QUAD)]
 
-    def one_row(own, first, row, sums, with_self, react=None, weight=None):
+    def gaps(own, first, row, with_self):
         other = [others[axis, row] for axis in range(3)]
-        force, energy, parts_a, parts_h, pulls = list(sums[:-1]), sums[-1], [], [], []
+        deltas, dist_sqs = [], []
         for k in range(QUAD):
             delta = [own[k][axis] - other[axis] for axis in range(3)]
             for axis, box, inv_box in wrap_box:
@@ -209,21 +209,29 @@
             dist_sq = delta[0] * delta[0] + delta[1] * delta[1] + delta[2] * delta[2]
             if with_self:
                 dist_sq = jnp.where(own_minus_lane == row * LANES - (first + k) * 8, rc2, dist_sq)
-            dist_sq = jnp.minimum(dist_sq, rc2)
-            scale, a, h = radial(dist_sq)
-            pulls.append([scale * delta[axis] for axis in range(3)])
+            deltas.append(delta)
+            dist_sqs.append(jnp.minimum(dist_sq, rc2))
+        return deltas, dist_sqs
+
+    def energy_row(own, first, row, total, with_self, weight=None):
+        gain = quad_energy(gaps(own, first, row, with_self)[1]) - cut_energy
+        return total + (gain if weight is None else gain * weight)
+
+    def force_row(own, first, row, force, with_self, react=None):
+        force, pulls = list(force), []
+        deltas, dist_sqs = gaps(own, first, row, with_self)
+        for k in range(QUAD):
+            inv_r, term, core = powers(dist_sqs[k])
+            scale = core + kappa * inv_r
+            pulls.append([scale * deltas[k][axis] for axis in range(3)])
             for axis in range(3):
                 force[3 * k + axis] = force[3 * k + axis] + pulls[k][axis]
-            parts_a.append(a)
-            parts_h.append(h)
-        gain = quad_energy(parts_a, parts_h) - cut_energy
         if react is not None:
-            gain = gain * weight
             for axis in range(3):
                 react[axis, row] = react[axis, row] + ((pulls[0][axis] + pulls[1][axis]) + (pulls[2][axis] + pulls[3][axis]))
-        return tuple(force) + (energy + gain,)
-
-    return load_own, one_row
+        return tuple(force)
+
+    return load_own, energy_row, force_row
 
 
 def prepare_kernel(gat_ref, pkt_ref, own_ref, sorted_ref, mine, others, acc, eng_ref):
@@ -346,13 +354,13 @@
             return carry
 
         def excess(first_quad, last_quad, first_row, wrap_box, energy):
-            load_own, one_row = pair_tools(mine, others, rc2, wrap_box)
+            load_own, energy_row, force_row = pair_tools(mine, others, rc2, wrap_box)
 
             def quad(index, total):
                 first = index * QUAD
                 own = load_own(first)
                 sums = (zero,) * (3 * QUAD) + (total,)
-                sums = lax.fori_loop(first_row, rows, lambda row, part: one_row(own, first, row, part, True), sums)
+                sums = lax.fori_loop(first_row, rows, lambda row, part: force_row(own, first, row, part[:-1], True) + (energy_row(own, first, row, part[-1], True),), sums)
                 for k in range(QUAD):
                     for axis in range(3):
                         acc[axis, first + k] = sums[3 * k + axis]
@@ -385,30 +393,22 @@
     mz, my, mx = coords
     barrier = entry_signals(coords)
     rc2 = RC * RC + 0.0 * mine[0, 0]
-    load_own, one_row = pair_tools(mine, others, rc2, [])
+    load_own, energy_row, force_row = pair_tools(mine, others, rc2, [])
 
     lane_8 = lax.broadcasted_iota(jnp.int32, (8, LANES), 1).astype(jnp.float32)
-    weights = [jnp.where(lane_8 + float(row * LANES) < eng_ref[1], 2.0, 1.0) for row in range(FIXED_BLOCKS)]
-    react[...] = jnp.zeros_like(react)
     energy = eng_ref[0]
     for block in range(FIXED_BLOCKS):
 
-        def quad(index, total, block=block):
+        def energy_quad(index, total, block=block):
             first = block * 16 + index * QUAD
             own = load_own(first)
-            sums = tuple(part[axis, first + k] for k in range(QUAD) for axis in range(3)) + (total,)
-            sums = one_row(own, first, block, sums, True)
+            total = energy_row(own, first, block, total, True)
             for row in range(block + 1, FIXED_ROWS):
-                if row < FIXED_BLOCKS:
-                    sums = one_row(own, first, row, sums, False, react, weights[row])
-                else:
-                    sums = one_row(own, first, row, sums, False)
-            for k in range(QUAD):
-                for axis in range(3):
-                    acc[axis, first + k] = sums[3 * k + axis]
-            return sums[-1]
-
-        energy = lax.fori_loop(0, 16 // QUAD, quad, energy)
+                weight = jnp.where(lane_8 + float(row * LANES) < eng_ref[1], 2.0, 1.0) if row < FIXED_BLOCKS else None
+                total = energy_row(own, first, row, total, False, weight)
+            return total
+
+        energy = lax.fori_loop(0, 16 // QUAD, energy_quad, energy)
     eng[...] = jnp.full((1, LANES), 2.0 * jnp.sum(energy), jnp.float32)
     pl.semaphore_wait(barrier, len(PEERS))
     place = (mz * NY + my) * NX + mx
@@ -417,6 +417,21 @@
         copies.append(pltpu.make_async_remote_copy(src_ref=eng, dst_ref=slots.at[place], send_sem=send_sem.at[index], recv_sem=recv_sem.at[index], device_id=peer_id(coords, offset), device_id_type=MESH))
         copies[-1].start()
     slots[place] = eng[...]
+    react[...] = jnp.zeros_like(react)
+    for block in range(FIXED_BLOCKS):
+
+        def force_quad(index, carry, block=block):
+            first = block * 16 + index * QUAD
+            own = load_own(first)
+            force = force_row(own, first, block, [part[axis, first + k] for k in range(QUAD) for axis in range(3)], True)
+            for row in range(block + 1, FIXED_ROWS):
+                force = force_row(own, first, row, force, False, react if row < FIXED_BLOCKS else None)
+            for k in range(QUAD):
+                for axis in range(3):
+                    acc[axis, first + k] = force[3 * k + axis]
+            return carry
+
+        lax.fori_loop(0, 16 // QUAD, force_quad, 0)
     for block in range(BLOCKS):
         held = acc if block < FIXED_BLOCKS else part
         for axis in range(3):

time: 20.5 us -> 19.6 us (0.956)
  Pallas kernels: 19 us -> 18.1 us
    pallas_call x1, Pallas kernels: 7.04 us -> 6.17 us  [local_step(): pl.pallas_call(tile_kernel, out_shape=(jax.ShapeDtypeStruct((8, WIDE), f3...]
where the time goes in v5:
time: 19.6 us; the launch traced here: 19.4 us
  Pallas kernels  18.1 us (92%)
  between operations  1.3 us (7%)
    pallas_call x1, Pallas kernels, local_step(): pl.pallas_call(exchange_kernel, out_shape=(jax.ShapeDtypeStruct((N_GROUPS...  9.49 us
    pallas_call x1, Pallas kernels, local_step(): pl.pallas_call(tile_kernel, out_shape=(jax.ShapeDtypeStruct((8, WIDE), f3...  6.17 us
    pallas_call x1, Pallas kernels, local_step(): pl.pallas_call(prepare_kernel, out_shape=(jax.ShapeDtypeStruct((BLOCKS, 8...  1.78 us
    pallas_call x1, Pallas kernels, local_step(): pl.pallas_call(finish_kernel, out_shape=(jax.ShapeDtypeStruct((3, CAP), f...  0.65 us

profile of v5, /device:TPU:0, one launch (start us, length us, event | category | flops | bytes accessed | tf_op | source)
XLA Modules:
  0.0 19.4 jit_solution(4970423948094392220)
XLA Ops:
  1.3 9.5 %exchange.1 = (f32[12,3,6,128]{3,2,1,0:T(8,128)S(1)}, f32[15,8,128]{2,1,0:T(8,128)S(1)}, f32[16,768]{1,0:T(8,128)S(1)}) custom-call(f32[]{:T(128)S(6)} %copy.12.brick_ref, f32[3,729]{1,0:T(4,128)} %bitcast.6, f32[3,729]{1,0:T(4,128)} %bitcast.7, f32[3,729]{1,0:T(4,128)} %bitcast.8, s32[729]{0:T(1024)} %id_ref.1, s32[729]{0:T(1024)} %ok_ref.1), custom_call_target="tpu_custom_call" | custom-call | tf_op jit(solution)/shard_map/exchange/pallas_call | solution.py:478
  10.8 1.8 %prepare.1 = (f32[6,8,128]{2,1,0:T(8,128)S(1)}, f32[3,96,8,128]{3,2,1,0:T(8,128)S(1)}, f32[3,110,8,128]{3,2,1,0:T(8,128)S(1)}, f32[3,96,8,128]{3,2,1,0:T(8,128)S(1)}, f32[2,8,128]{2,1,0:T(8,128)S(1)}) custom-call(f32[12,3,6,128]{3,2,1,0:T(8,128)S(1)} %get-tuple-element.22.gat_ref, f32[15,8,128]{2,1,0:T(8,128)S(1)} %get-tuple-element.23.pkt_ref, ...), custom_call_target="tpu_custom_call" | custom-call | tf_op jit(solution)/shard_map/prepare/pallas_call | solution.py:501
  12.6 6.2 %tile.1 = (f32[8,768]{1,0:T(8,128)S(1)}, f32[1,128]{1,0:T(1,128)S(1)}) custom-call(f32[3,96,8,128]{3,2,1,0:T(8,128)S(1)} %get-tuple-element.26.mine, f32[3,110,8,128]{3,2,1,0:T(8,128)S(1)} %get-tuple-element.27.others, f32[3,96,8,128]{3,2,1,0:T(8,128)S(1)} %get-tuple-element.28.part, f32[2,8,128]{2,1,0:T(8,128)S(1)} %get-tuple-element.29.eng_ref), custom_call_target="tpu_custom_call" | custom-call | tf_op jit(solution)/shard_map/tile/pallas_call | solution.py:509
  18.8 0.6 %finish.1 = (f32[3,729]{1,0:T(4,128)}, f32[3,729]{1,0:T(4,128)}, f32[3,729]{1,0:T(4,128)}, s32[729]{0:T(1024)}, s32[729]{0:T(1024)}, /*index=5*/f32[]{:T(128)}) custom-call(f32[6,8,128]{2,1,0:T(8,128)S(1)} %get-tuple-element.25.sorted_ref, f32[8,768]{1,0:T(8,128)S(1)} %get-tuple-element.30.frc_ref, f32[1,128]{1,0:T(1,128)S(1)} %get-tuple-element.31.total_ref), custom_call_target="tpu_custom_call" | custom-call | tf_op jit(solution)/shard_map/finish/pallas_call | solution.py:518

commit v6 on v5

--- a/solution.py
+++ b/solution.py
@@ -6,6 +6,7 @@
 from jax.sharding import PartitionSpec as P
 
 DT = 0.005
+HALF_DT = 0.5 * DT
 RC = 2.5
 UPC = -48.0 * RC ** -13 + 24.0 * RC ** -7
 MESH_AXES = ("z", "y", "x")
@@ -13,6 +14,7 @@
 NZ, NY, NX = 2, 2, 4
 CAP = 729
 LANES = 128
+TILE = (8, LANES)
 BLOCKS = 6
 WIDE = BLOCKS * LANES
 MOVE_CAP = CAP // 100
@@ -46,6 +48,7 @@
 STAY = 13
 NT_DIMS = (((1,), (1,)), ((), ()))
 NN_DIMS = (((1,), (0,)), ((), ()))
+TN_DIMS = (((0,), (0,)), ((), ()))
 
 
 def split3(values):
@@ -66,6 +69,26 @@
 
 def dot_nn(a, b):
     return lax.dot_general(a, b, NN_DIMS, preferred_element_type=jnp.float32)
+
+
+def down(values):
+    return jnp.sum(values, axis=0, keepdims=True)
+
+
+def across(values):
+    return jnp.sum(values, axis=1, keepdims=True)
+
+
+def stack(values):
+    return jnp.concatenate(values, axis=0)
+
+
+def beside(values):
+    return jnp.concatenate(values, axis=1)
+
+
+def iota(shape, axis):
+    return lax.broadcasted_iota(jnp.int32, shape, axis)
 
 
 def my_coords():
@@ -106,7 +129,7 @@
         box = brick * float(size)
         low = mine.astype(jnp.float32) * brick
         high = (mine + 1).astype(jnp.float32) * brick
-        half_v = pad_ref[1, axis:axis + 1, :] + (0.5 * DT) * pad_ref[2, axis:axis + 1, :]
+        half_v = pad_ref[1, axis:axis + 1, :] + HALF_DT * pad_ref[2, axis:axis + 1, :]
         drift = pad_ref[0, axis:axis + 1, :] + DT * half_v
         step = jnp.where(drift >= high, 2, jnp.where(drift < low, 0, 1))
         code = code + step * weight
@@ -121,10 +144,10 @@
     ids = int_ref[0:1, :]
     id_hi = (lax.shift_right_logical(ids, 16) + 1).astype(jnp.float32)
     id_lo = (ids & 65535).astype(jnp.float32)
-    data = jnp.concatenate(moved + [id_hi] + half + [id_lo], axis=0)
-    member = (jnp.broadcast_to(code, (32, WIDE)) == lax.broadcasted_iota(jnp.int32, (32, WIDE), 0)).astype(jnp.float32)
-    tri = (lax.broadcasted_iota(jnp.int32, (LANES, LANES), 0) < lax.broadcasted_iota(jnp.int32, (LANES, LANES), 1)).astype(jnp.bfloat16)
-    codes = lax.broadcasted_iota(jnp.int32, (32, LANES), 0)
+    data = stack(moved + [id_hi] + half + [id_lo])
+    member = (jnp.broadcast_to(code, (32, WIDE)) == iota((32, WIDE), 0)).astype(jnp.float32)
+    tri = (iota((LANES, LANES), 0) < iota((LANES, LANES), 1)).astype(jnp.bfloat16)
+    codes = iota((32, LANES), 0)
     running = jnp.zeros((32, LANES), jnp.float32)
     for move, first in LANE_BASE.items():
         running = jnp.where(codes == move, float(first), running)
@@ -132,17 +155,17 @@
     for block in range(BLOCKS):
         part = member[:, block * LANES:(block + 1) * LANES]
         before = dot_nn(part.astype(jnp.bfloat16), tri)
-        slots.append(jnp.sum(part * (before + running), axis=0, keepdims=True))
-        running = running + jnp.sum(part, axis=1, keepdims=True)
-    slot = jnp.concatenate(slots, axis=1)
+        slots.append(down(part * (before + running)))
+        running = running + across(part)
+    slot = beside(slots)
     stay = code == STAY
     mover_slot = jnp.where(owned & jnp.logical_not(stay), slot, -1.0).astype(jnp.int32)
-    pick = (lax.broadcasted_iota(jnp.int32, (2 * LANES, WIDE), 0) == mover_slot).astype(jnp.float32).astype(jnp.bfloat16)
+    pick = (iota((2 * LANES, WIDE), 0) == mover_slot).astype(jnp.float32).astype(jnp.bfloat16)
     packet = join3(dot_nt(split3(data), pick))
     send_pkt[0] = packet[:, 0:LANES]
     send_pkt[1] = packet[:, LANES:2 * LANES]
     own_ref[0:8, :] = data
-    own_ref[8:16, :] = jnp.concatenate([jnp.where(stay, slot, -1.0), jnp.full((7, WIDE), brick, jnp.float32)], axis=0)
+    own_ref[8:16, :] = stack([jnp.where(stay, slot, -1.0), jnp.full((7, WIDE), brick, jnp.float32)])
     pl.semaphore_wait(barrier, len(PEERS))
     copies = []
     for index, (gx, gy, gz) in enumerate(GROUPS + DISTANT):
@@ -165,8 +188,10 @@
 GROUPS_OWN = BLOCKS * 16
 QUAD = 4
 FIXED_BLOCKS = 4
-FIXED_QUADS = FIXED_BLOCKS * 16 // QUAD
+PER_BLOCK = 16
+FIXED_QUADS = FIXED_BLOCKS * PER_BLOCK // QUAD
 FIXED_ROWS = 11
+ENERGY_ROWS = 8
 
 
 def pair_tools(mine, others, rc2, wrap_box):
@@ -194,7 +219,7 @@
         return ((terms[0] + terms[1]) + (terms[2] + terms[3])) - 12.0 * ((tails[0] + tails[1]) + (tails[2] + tails[3]))
 
     cut_energy = quad_energy([rc2] * QUAD)
-    own_minus_lane = lax.broadcasted_iota(jnp.int32, (8, LANES), 0) - lax.broadcasted_iota(jnp.int32, (8, LANES), 1)
+    own_minus_lane = iota(TILE, 0) - iota(TILE, 1)
 
     def load_own(first):
         return [[mine[axis, first + k] for axis in range(3)] for k in range(QUAD)]
@@ -241,21 +266,21 @@
     sizes = (NX, NY, NZ)
     centre = [(index.astype(jnp.float32) + 0.5) * brick for index in (mx, my, mz)]
     box = [brick * float(size) for size in sizes]
-    lane_1 = lax.broadcasted_iota(jnp.int32, (1, LANES), 1)
+    lane_1 = iota((1, LANES), 1)
     acc[:, pl.ds(0, FIXED_QUADS * QUAD)] = jnp.zeros((3, FIXED_QUADS * QUAD, 8, LANES), jnp.float32)
 
     arrived = []
     for block in range(2):
-        total = jnp.zeros((8, LANES), jnp.float32)
+        total = jnp.zeros(TILE, jnp.float32)
         for index in range(N_GROUPS):
             where_block, first, last = LANE_STARTS[index]
             if where_block == block:
                 total = total + jnp.where((lane_1 >= first) & (lane_1 < last), pkt_ref[index], 0.0)
         arrived.append(total)
-    arr = jnp.concatenate(arrived, axis=1)
+    arr = beside(arrived)
     arr_ok = arr[3:4] > 0.5
     stay_all = own_ref[8:9, :] >= 0.0
-    n_vec = jnp.sum(stay_all.astype(jnp.float32), axis=1, keepdims=True) + jnp.sum(arr_ok.astype(jnp.float32), axis=1, keepdims=True)
+    n_vec = across(stay_all.astype(jnp.float32)) + across(arr_ok.astype(jnp.float32))
     n_own = jnp.max(n_vec).astype(jnp.int32)
     n_int = n_vec.astype(jnp.int32)
     quads = lax.div(n_own + (8 * QUAD - 1), 8 * QUAD)
@@ -264,16 +289,16 @@
     for slot in range(1, N_GROUPS + 1):
         beyond = jnp.minimum(beyond, gat_ref[slot, 0, 4:6, :])
     small = (jnp.min(beyond) > 0.5 * NOWHERE) & (n_own <= FIXED_BLOCKS * LANES)
-    eng_ref[1] = jnp.broadcast_to(n_vec, (8, LANES))
+    eng_ref[1] = jnp.broadcast_to(n_vec, TILE)
     wide = jnp.max(brick) >= 2.0 * RC
     int_max = 2147483647
     rc2 = RC * RC + 0.0 * own_ref[8:16, 0:LANES]
-    zero = jnp.zeros((8, LANES), jnp.float32)
-    far = jnp.full((8, LANES), FAR_OTHER, jnp.float32)
+    zero = jnp.zeros(TILE, jnp.float32)
+    far = jnp.full(TILE, FAR_OTHER, jnp.float32)
 
     def build(blocks, tile_rows):
         span = blocks * LANES
-        data = jnp.concatenate([own_ref[0:8, 0:span], arr], axis=1)
+        data = beside([own_ref[0:8, 0:span], arr])
         ids = lax.shift_left(data[3:4].astype(jnp.int32) - 1, 16) + data[7:8].astype(jnp.int32)
         stay_rank = own_ref[8:9, 0:span]
         stay = stay_rank >= 0.0
@@ -286,67 +311,99 @@
         for axis in range(3):
             near = [gat_ref[slot, axis, 0:tile_rows, :] for slot in range(N_GROUPS + 1)]
             distant = [jnp.where(pkt_ref[N_GROUPS + k, 3:4, :] > 0.5, pkt_ref[N_GROUPS + k, axis:axis + 1, :], NOWHERE) for k in range(len(DISTANT))]
-            values = jnp.concatenate(near + distant + [jnp.full((cand - count_rows - len(DISTANT), LANES), NOWHERE, jnp.float32)], axis=0) - centre[axis]
+            values = stack(near + distant + [jnp.full((cand - count_rows - len(DISTANT), LANES), NOWHERE, jnp.float32)]) - centre[axis]
             rel.append(jnp.where(values > 0.5 * box[axis], values - box[axis], jnp.where(values < -0.5 * box[axis], values + box[axis], values)))
         over = [jnp.maximum(jnp.abs(values) - half_l, 0.0) for values in rel]
         gap_sq = over[0] * over[0] + over[1] * over[1] + over[2] * over[2]
-        ghost = ((gap_sq > 0.0) & (gap_sq < GHOST_SQ)).astype(jnp.float32).astype(jnp.bfloat16)
-        row_i = lax.broadcasted_iota(jnp.int32, (LANES, LANES), 0)
-        col_i = lax.broadcasted_iota(jnp.int32, (LANES, LANES), 1)
-        cum = dot_nn(ghost, (row_i <= col_i).astype(jnp.bfloat16)).astype(jnp.int32)
-        count = dot_nn(ghost, jnp.ones((LANES, LANES), jnp.bfloat16))
-        arr_col = jnp.transpose(jnp.broadcast_to(arr_id, (8, 2 * LANES)), (1, 0))[:, 0:1]
-        own_col = jnp.transpose(jnp.broadcast_to(own_id, (8, span)), (1, 0))[:, 0:1]
-        all_id = jnp.concatenate([own_id, arr_id], axis=1)
-        arr_before = jnp.sum((arr_col < all_id).astype(jnp.float32), axis=0, keepdims=True)
-        stay_before = jnp.sum((own_col < arr_id).astype(jnp.float32), axis=0, keepdims=True)
-        rank = jnp.concatenate([jnp.where(stay, stay_rank + arr_before[:, :span], -1.0), jnp.where(arr_ok, stay_before + arr_before[:, span:], -1.0)], axis=1).astype(jnp.int32)
-        base = dot_nn((col_i < row_i).astype(jnp.bfloat16)[:cand, :cand], count.astype(jnp.bfloat16)).astype(jnp.int32) + n_int
-        count = count.astype(jnp.int32)
-        n_all = jnp.max(base[cand - 8:] + count[cand - 8:])
-        place = (lax.broadcasted_iota(jnp.int32, (cand, LANES), 1) - base) & (LANES - 1)
+        side = jnp.zeros((cand, LANES), jnp.float32)
+        for axis in range(3):
+            side = 3.0 * side + jnp.where(over[2 - axis] > 0.0, jnp.where(rel[2 - axis] > 0.0, 1.0, -1.0), 0.0)
+        near = gap_sq < GHOST_SQ
+        mixed = jnp.where(near & (side > 0.0), 256.0, jnp.where(near & (side < 0.0), 1.0, 0.0)).astype(jnp.bfloat16)
+        row_l, col_l = iota((LANES, LANES), 0), iota((LANES, LANES), 1)
+
+        def counts(chosen):
+            return dot_nn(mixed, chosen.astype(jnp.bfloat16)).astype(jnp.int32)
+
+        cum = counts(row_l <= col_l)
+        total = counts(row_l >= 0)
+        marks = [counts(row_l < 16 * k) for k in range(1, 8)]
+        arr_col = jnp.broadcast_to(arr_id, (8, 2 * LANES)).T[:, 0:1]
+        arr_first = (arr_col < beside([own_id, arr_id])).astype(jnp.float32)
+        arr_before = down(arr_first)
+        stay_after = dot_nt(jnp.broadcast_to(stay.astype(jnp.float32), (8, span)).astype(jnp.bfloat16), arr_first[:, :span].astype(jnp.bfloat16))[0:1]
+        stay_before = across(stay.astype(jnp.float32)) - stay_after
+        rank = beside([jnp.where(stay, stay_rank + arr_before[:, :span], -1.0), jnp.where(arr_ok, stay_before + arr_before[:, span:], -1.0)]).astype(jnp.int32)
+        earlier = (iota((cand, cand), 1) < iota((cand, cand), 0)).astype(jnp.bfloat16)
+        uppers, lowers = lax.shift_right_logical(total, 8), total & 255
+
+        def starts(each, first):
+            base = dot_nn(earlier, each.astype(jnp.float32).astype(jnp.bfloat16)).astype(jnp.int32) + first
+            return base, base[cand - 1:] + each[cand - 1:]
+
+        upper_base, upper_end = starts(uppers, n_int)
+        lower_base, all_end = starts(lowers, upper_end)
+        n_upper, n_all = jnp.max(upper_end), jnp.max(all_end)
+        eng_ref[2] = jnp.broadcast_to(upper_end.astype(jnp.float32), TILE)
+        fits = n_upper <= ENERGY_ROWS * LANES
         parts = split3(data)
+        spread = ((iota((24, 3 * LANES), 0) & 7) == lax.shift_right_logical(iota((24, 3 * LANES), 1), 7)).astype(jnp.bfloat16)
 
         def place_block(block):
-            pick = (lax.broadcasted_iota(jnp.int32, (LANES, span + 2 * LANES), 0) + block * LANES == rank).astype(jnp.float32).astype(jnp.bfloat16)
-            rows_s = join3(jnp.transpose(dot_nt(pick, parts), (1, 0)))
+            pick = (iota((LANES, span + 2 * LANES), 0) + block * LANES == rank).astype(jnp.float32).astype(jnp.bfloat16)
+            rows_s = join3((dot_nt(pick, parts)).T)
             sorted_ref[block] = rows_s
             valid = lane_1 + block * LANES < n_int
-            own_rel = jnp.concatenate([rows_s[axis:axis + 1] - centre[axis] for axis in range(3)] + [rows_s[3:8]], axis=0)
-            columns = jnp.transpose(jnp.where(valid, own_rel, FAR_OWN), (1, 0))
+            own_rel = stack([rows_s[axis:axis + 1] - centre[axis] for axis in range(3)] + [rows_s[3:8]])
+            tiles = lax.dot_general(split3(jnp.where(valid, own_rel, FAR_OWN)), spread, TN_DIMS, preferred_element_type=jnp.float32)
             for axis in range(3):
-                others[axis, block] = jnp.broadcast_to(jnp.where(valid, own_rel[axis:axis + 1], 0.0), (8, LANES))
-                mine[axis, pl.ds(block * 16, 16)] = jnp.broadcast_to(columns[:, axis:axis + 1], (LANES, LANES)).reshape(16, 8, LANES)
-
-        wanted = lax.broadcasted_iota(jnp.int32, (cand, LANES), 1)
-        source = jnp.zeros((cand, LANES), jnp.int32)
-        waiting = list(range(blocks))
-        for stride, probes in ((16, 7), (2, 7), (1, 1)):
-            below = jnp.zeros((cand, LANES), jnp.int32)
-            for k in range(1, probes + 1):
-                probe = jnp.take_along_axis(cum, source + (stride * k - 1), axis=1)
-                below = below + (probe <= wanted).astype(jnp.int32)
-            source = source + stride * below
-            for block in waiting[:2]:
-                place_block(block)
-            waiting = waiting[2:]
-        source = jnp.take_along_axis(source & (LANES - 1), place, axis=1)
+                others[axis, block] = jnp.broadcast_to(jnp.where(valid, own_rel[axis:axis + 1], 0.0), TILE)
+                mine[axis, pl.ds(block * PER_BLOCK, PER_BLOCK)] = tiles[:, axis * LANES:(axis + 1) * LANES].reshape(16, 8, LANES)
+
+        lane_c = iota((cand, LANES), 1)
+        is_upper = lane_c < uppers
+        keep = jnp.where(is_upper, -1, 255)
+        bound = jnp.where(is_upper, lane_c * 256 + 255, lane_c - uppers)
+
+        def passed(probes):
+            return sum(((probe & keep) <= bound).astype(jnp.int32) for probe in probes)
+
+        def probe_at(source, stride, number):
+            return [jnp.take_along_axis(cum, source + (stride * k - 1), axis=1) for k in range(1, number + 1)]
+
+        source = 16 * passed(marks)
+        place_block(0)
+        place_block(1)
+        source = source + 2 * passed(probe_at(source, 2, 7))
+        for block in range(2, blocks):
+            place_block(block)
+        source = source + passed(probe_at(source, 1, 1))
         for block in range(blocks, BLOCKS):
             sorted_ref[block] = zero
-        target = jnp.where(place < count, lax.shift_right_logical(base + place, 7), -1)
-        packed = [jnp.take_along_axis(values, source, axis=1) for values in rel]
+
+        def turned(base, each, first):
+            place = (lane_c - base) & (LANES - 1)
+            lane = jnp.take_along_axis(source, (first + place) & (LANES - 1), axis=1)
+            target = jnp.where(place < each, lax.shift_right_logical(base + place, 7), -1)
+            return target, [jnp.take_along_axis(values, lane, axis=1) for values in rel]
+
+        def pack(target, packed, start, stop, held_rows, empty):
+            def pack_row(row, carry):
+                hit = target == row
+                filled = lane_1 + row * LANES < n_all
+                for axis in range(3):
+                    held = jnp.where(row < held_rows, others[axis, row], 0.0)
+                    values = held + down(jnp.where(hit, packed[axis], 0.0))
+                    others[axis, row] = jnp.where(filled, values, empty)
+                return carry
+
+            lax.fori_loop(lax.div(start, LANES), lax.div(stop + (LANES - 1), LANES), pack_row, 0)
+
+        upper_rows = lax.div(n_upper + (LANES - 1), LANES)
         rows = lax.div(n_all + (LANES - 1), LANES)
-
-        def pack_row(row, carry):
-            hit = target == row
-            filled = lane_1 + row * LANES < n_all
-            for axis in range(3):
-                own_part = jnp.where(row < own_rows, others[axis, row], 0.0)
-                values = jnp.sum(jnp.where(hit, packed[axis], 0.0), axis=0, keepdims=True)
-                others[axis, row] = jnp.where(filled, own_part + values, FAR_OTHER)
-            return carry
-
-        lax.fori_loop(lax.div(n_own, LANES), rows, pack_row, 0)
+        upper_set, lower_set = turned(upper_base, uppers, 0), turned(lower_base, lowers, uppers)
+        pack(*upper_set, n_own, n_upper, own_rows, 0.0)
+        pack(*lower_set, n_upper, n_all, upper_rows, FAR_OTHER)
 
         def set_far(row, carry):
             for axis in range(3):
@@ -354,13 +411,20 @@
             return carry
 
         def excess(first_quad, last_quad, first_row, wrap_box, energy):
+            slot_8 = iota(TILE, 1)
             load_own, energy_row, force_row = pair_tools(mine, others, rc2, wrap_box)
 
             def quad(index, total):
                 first = index * QUAD
                 own = load_own(first)
                 sums = (zero,) * (3 * QUAD) + (total,)
-                sums = lax.fori_loop(first_row, rows, lambda row, part: force_row(own, first, row, part[:-1], True) + (energy_row(own, first, row, part[-1], True),), sums)
+
+                def both(row, part):
+                    slot = slot_8 + row * LANES
+                    weight = 1.0 if wrap_box else jnp.where(slot < n_int, 1.0, jnp.where(slot < upper_end, 2.0, 0.0))
+                    return force_row(own, first, row, part[:-1], True) + (energy_row(own, first, row, part[-1], True, weight),)
+
+                sums = lax.fori_loop(first_row, rows, both, sums)
                 for k in range(QUAD):
                     for axis in range(3):
                         acc[axis, first + k] = sums[3 * k + axis]
@@ -376,13 +440,13 @@
             eng_ref[0] = energy
             lax.fori_loop(rows, FIXED_ROWS, set_far, 0)
 
-        def wrapped():
-            wrap_box = [(axis, box[axis], 1.0 / box[axis]) for axis in (1, 2)]
+        def alone(wrap_box):
             eng_ref[0] = excess(0, quads, 0, wrap_box, zero)
             lax.fori_loop(0, FIXED_ROWS, set_far, 0)
 
-        pl.when(wide)(plain)
-        pl.when(jnp.logical_not(wide))(wrapped)
+        pl.when(wide & fits)(plain)
+        pl.when(wide & jnp.logical_not(fits))(lambda: alone([]))
+        pl.when(jnp.logical_not(wide))(lambda: alone([(axis, box[axis], 1.0 / box[axis]) for axis in (1, 2)]))
 
     pl.when(small)(lambda: build(FIXED_BLOCKS, 4))
     pl.when(jnp.logical_not(small))(lambda: build(BLOCKS, BLOCKS))
@@ -395,20 +459,24 @@
     rc2 = RC * RC + 0.0 * mine[0, 0]
     load_own, energy_row, force_row = pair_tools(mine, others, rc2, [])
 
-    lane_8 = lax.broadcasted_iota(jnp.int32, (8, LANES), 1).astype(jnp.float32)
+    lane_8 = iota(TILE, 1).astype(jnp.float32)
     energy = eng_ref[0]
+
+    def weight_of(row, own_weight):
+        slot = lane_8 + float(row * LANES)
+        return jnp.where(slot < eng_ref[1], own_weight, jnp.where(slot < eng_ref[2], 2.0, 0.0))
+
     for block in range(FIXED_BLOCKS):
 
         def energy_quad(index, total, block=block):
-            first = block * 16 + index * QUAD
+            first = block * PER_BLOCK + index * QUAD
             own = load_own(first)
-            total = energy_row(own, first, block, total, True)
-            for row in range(block + 1, FIXED_ROWS):
-                weight = jnp.where(lane_8 + float(row * LANES) < eng_ref[1], 2.0, 1.0) if row < FIXED_BLOCKS else None
-                total = energy_row(own, first, row, total, False, weight)
+            for row in range(block, ENERGY_ROWS):
+                weight = weight_of(row, 2.0 if block < row < FIXED_BLOCKS else 1.0)
+                total = energy_row(own, first, row, total, row == block, weight)
             return total
 
-        energy = lax.fori_loop(0, 16 // QUAD, energy_quad, energy)
+        energy = lax.fori_loop(0, PER_BLOCK // QUAD, energy_quad, energy)
     eng[...] = jnp.full((1, LANES), 2.0 * jnp.sum(energy), jnp.float32)
     pl.semaphore_wait(barrier, len(PEERS))
     place = (mz * NY + my) * NX + mx
@@ -421,7 +489,7 @@
     for block in range(FIXED_BLOCKS):
 
         def force_quad(index, carry, block=block):
-            first = block * 16 + index * QUAD
+            first = block * PER_BLOCK + index * QUAD
             own = load_own(first)
             force = force_row(own, first, block, [part[axis, first + k] for k in range(QUAD) for axis in range(3)], True)
             for row in range(block + 1, FIXED_ROWS):
@@ -431,14 +499,14 @@
                     acc[axis, first + k] = force[3 * k + axis]
             return carry
 
-        lax.fori_loop(0, 16 // QUAD, force_quad, 0)
+        lax.fori_loop(0, PER_BLOCK // QUAD, force_quad, 0)
     for block in range(BLOCKS):
         held = acc if block < FIXED_BLOCKS else part
         for axis in range(3):
-            turned = jnp.transpose(held[axis, pl.ds(block * 16, 16)].reshape(LANES, LANES), (1, 0))
-            force = jnp.sum(turned, axis=0, keepdims=True)
+            turned = (held[axis, pl.ds(block * PER_BLOCK, PER_BLOCK)].reshape(LANES, LANES)).T
+            force = down(turned)
             if 0 < block < FIXED_BLOCKS:
-                force = force - jnp.sum(react[axis, block], axis=0, keepdims=True)
+                force = force - down(react[axis, block])
             frc_ref[axis:axis + 1, block * LANES:(block + 1) * LANES] = 48.0 * force
     for copy in copies:
         copy.wait()
@@ -458,7 +526,7 @@
         for axis in range(3):
             force = jnp.where(valid, frc_ref[axis:axis + 1, block * LANES:(block + 1) * LANES], 0.0)
             frc_out[axis:axis + 1, lanes] = force[:, :width]
-            vel_out[axis:axis + 1, lanes] = (rows_s[4 + axis:5 + axis] + (0.5 * DT) * force)[:, :width]
+            vel_out[axis:axis + 1, lanes] = (rows_s[4 + axis:5 + axis] + HALF_DT * force)[:, :width]
             pos_out[axis:axis + 1, lanes] = rows_s[axis:axis + 1, :width]
         new_id = lax.shift_left(rows_s[3:4].astype(jnp.int32) - 1, 16) + rows_s[7:8].astype(jnp.int32)
         id_out[lanes] = jnp.where(valid, new_id, 0)[:, :width].reshape(width)
@@ -500,7 +568,7 @@
         own_tiles = jax.ShapeDtypeStruct((3, GROUPS_OWN, 8, LANES), f32)
         placed, mine, others, part, eng = pl.pallas_call(
             prepare_kernel,
-            out_shape=(jax.ShapeDtypeStruct((BLOCKS, 8, LANES), f32), own_tiles, jax.ShapeDtypeStruct((3, MAX_ROWS, 8, LANES), f32), own_tiles, jax.ShapeDtypeStruct((2, 8, LANES), f32)),
+            out_shape=(jax.ShapeDtypeStruct((BLOCKS, 8, LANES), f32), own_tiles, jax.ShapeDtypeStruct((3, MAX_ROWS, 8, LANES), f32), own_tiles, jax.ShapeDtypeStruct((3, 8, LANES), f32)),
             in_specs=[VMEM_SPEC] * 3,
             out_specs=(VMEM_SPEC,) * 5,
             compiler_params=pltpu.CompilerParams(vmem_limit_bytes=VMEM_LIMIT),

time: 19.6 us -> 20 us (1.020)
  Pallas kernels: 18.1 us -> 18.5 us
    pallas_call x1, Pallas kernels: 1.78 us -> 2.63 us  [local_step(): pl.pallas_call(prepare_kernel, out_shape=(jax.ShapeDtypeStruct((BLOCKS, 8...]
    pallas_call x1, Pallas kernels: 6.17 us -> 5.74 us  [local_step(): pl.pallas_call(tile_kernel, out_shape=(jax.ShapeDtypeStruct((8, WIDE), f3...]
where the time goes in v6:
time: 20 us; the launch traced here: 19.8 us
  Pallas kernels  18.5 us (92%)
  between operations  1.3 us (6%)
    pallas_call x1, Pallas kernels, local_step(): pl.pallas_call(exchange_kernel, out_shape=(jax.ShapeDtypeStruct((N_GROUPS...  9.49 us
    pallas_call x1, Pallas kernels, local_step(): pl.pallas_call(tile_kernel, out_shape=(jax.ShapeDtypeStruct((8, WIDE), f3...  5.74 us
    pallas_call x1, Pallas kernels, local_step(): pl.pallas_call(prepare_kernel, out_shape=(jax.ShapeDtypeStruct((BLOCKS, 8...  2.63 us
    pallas_call x1, Pallas kernels, local_step(): pl.pallas_call(finish_kernel, out_shape=(jax.ShapeDtypeStruct((3, CAP), f...  0.65 us

profile of v6, /device:TPU:0, one launch (start us, length us, event | category | flops | bytes accessed | tf_op | source)
XLA Modules:
  0.0 19.8 jit_solution(2245152152347954646)
XLA Ops:
  1.3 9.5 %exchange.1 = (f32[12,3,6,128]{3,2,1,0:T(8,128)S(1)}, f32[15,8,128]{2,1,0:T(8,128)S(1)}, f32[16,768]{1,0:T(8,128)S(1)}) custom-call(f32[]{:T(128)S(6)} %copy.12.brick_ref, f32[3,729]{1,0:T(4,128)} %bitcast.6, f32[3,729]{1,0:T(4,128)} %bitcast.7, f32[3,729]{1,0:T(4,128)} %bitcast.8, s32[729]{0:T(1024)} %id_ref.1, s32[729]{0:T(1024)} %ok_ref.1), custom_call_target="tpu_custom_call" | custom-call | tf_op jit(solution)/shard_map/exchange/pallas_call | solution.py:546
  10.8 2.6 %prepare.1 = (f32[6,8,128]{2,1,0:T(8,128)S(1)}, f32[3,96,8,128]{3,2,1,0:T(8,128)S(1)}, f32[3,110,8,128]{3,2,1,0:T(8,128)S(1)}, f32[3,96,8,128]{3,2,1,0:T(8,128)S(1)}, f32[3,8,128]{2,1,0:T(8,128)S(1)}) custom-call(f32[12,3,6,128]{3,2,1,0:T(8,128)S(1)} %get-tuple-element.22.gat_ref, f32[15,8,128]{2,1,0:T(8,128)S(1)} %get-tuple-element.23.pkt_ref, ...), custom_call_target="tpu_custom_call" | custom-call | tf_op jit(solution)/shard_map/prepare/pallas_call | solution.py:569
  13.4 5.7 %tile.1 = (f32[8,768]{1,0:T(8,128)S(1)}, f32[1,128]{1,0:T(1,128)S(1)}) custom-call(f32[3,96,8,128]{3,2,1,0:T(8,128)S(1)} %get-tuple-element.26.mine, f32[3,110,8,128]{3,2,1,0:T(8,128)S(1)} %get-tuple-element.27.others, f32[3,96,8,128]{3,2,1,0:T(8,128)S(1)} %get-tuple-element.28.part, f32[3,8,128]{2,1,0:T(8,128)S(1)} %get-tuple-element.29.eng_ref), custom_call_target="tpu_custom_call" | custom-call | tf_op jit(solution)/shard_map/tile/pallas_call | solution.py:577
  19.2 0.6 %finish.1 = (f32[3,729]{1,0:T(4,128)}, f32[3,729]{1,0:T(4,128)}, f32[3,729]{1,0:T(4,128)}, s32[729]{0:T(1024)}, s32[729]{0:T(1024)}, /*index=5*/f32[]{:T(128)}) custom-call(f32[6,8,128]{2,1,0:T(8,128)S(1)} %get-tuple-element.25.sorted_ref, f32[8,768]{1,0:T(8,128)S(1)} %get-tuple-element.30.frc_ref, f32[1,128]{1,0:T(1,128)S(1)} %get-tuple-element.31.total_ref), custom_call_target="tpu_custom_call" | custom-call | tf_op jit(solution)/shard_map/finish/pallas_call | solution.py:586

commit v7 on v6

--- a/solution.py
+++ b/solution.py
@@ -48,7 +48,6 @@
 STAY = 13
 NT_DIMS = (((1,), (1,)), ((), ()))
 NN_DIMS = (((1,), (0,)), ((), ()))
-TN_DIMS = (((0,), (0,)), ((), ()))
 
 
 def split3(values):
@@ -347,7 +346,6 @@
         eng_ref[2] = jnp.broadcast_to(upper_end.astype(jnp.float32), TILE)
         fits = n_upper <= ENERGY_ROWS * LANES
         parts = split3(data)
-        spread = ((iota((24, 3 * LANES), 0) & 7) == lax.shift_right_logical(iota((24, 3 * LANES), 1), 7)).astype(jnp.bfloat16)
 
         def place_block(block):
             pick = (iota((LANES, span + 2 * LANES), 0) + block * LANES == rank).astype(jnp.float32).astype(jnp.bfloat16)
@@ -355,10 +353,10 @@
             sorted_ref[block] = rows_s
             valid = lane_1 + block * LANES < n_int
             own_rel = stack([rows_s[axis:axis + 1] - centre[axis] for axis in range(3)] + [rows_s[3:8]])
-            tiles = lax.dot_general(split3(jnp.where(valid, own_rel, FAR_OWN)), spread, TN_DIMS, preferred_element_type=jnp.float32)
+            columns = jnp.where(valid, own_rel, FAR_OWN).T
             for axis in range(3):
                 others[axis, block] = jnp.broadcast_to(jnp.where(valid, own_rel[axis:axis + 1], 0.0), TILE)
-                mine[axis, pl.ds(block * PER_BLOCK, PER_BLOCK)] = tiles[:, axis * LANES:(axis + 1) * LANES].reshape(16, 8, LANES)
+                mine[axis, pl.ds(block * PER_BLOCK, PER_BLOCK)] = jnp.broadcast_to(columns[:, axis:axis + 1], (LANES, LANES)).reshape(16, 8, LANES)
 
         lane_c = iota((cand, LANES), 1)
         is_upper = lane_c < uppers
@@ -477,7 +475,7 @@
             return total
 
         energy = lax.fori_loop(0, PER_BLOCK // QUAD, energy_quad, energy)
-    eng[...] = jnp.full((1, LANES), 2.0 * jnp.sum(energy), jnp.float32)
+    eng[...] = 2.0 * down(energy)
     pl.semaphore_wait(barrier, len(PEERS))
     place = (mz * NY + my) * NX + mx
     copies = []
@@ -517,7 +515,7 @@
 
 
 def finish_kernel(sorted_ref, frc_ref, total_ref, pos_out, vel_out, frc_out, id_out, ok_out, eng_out):
-    eng_out[...] = jnp.max(total_ref[...])
+    eng_out[...] = jnp.sum(total_ref[...])
     for block in range(BLOCKS):
         width = min(LANES, CAP - block * LANES)
         lanes = slice(block * LANES, block * LANES + width)

time: 20 us -> 19.3 us (0.965)
  Pallas kernels: 18.5 us -> 17.8 us
    pallas_call x1, Pallas kernels: 2.63 us -> 1.9 us  [local_step(): pl.pallas_call(prepare_kernel, out_shape=(jax.ShapeDtypeStruct((BLOCKS, 8...]
where the time goes in v7:
time: 19.3 us; the launch traced here: 19.1 us
  Pallas kernels  17.8 us (92%)
  between operations  1.3 us (7%)
    pallas_call x1, Pallas kernels, local_step(): pl.pallas_call(exchange_kernel, out_shape=(jax.ShapeDtypeStruct((N_GROUPS...  9.49 us
    pallas_call x1, Pallas kernels, local_step(): pl.pallas_call(tile_kernel, out_shape=(jax.ShapeDtypeStruct((8, WIDE), f3...  5.74 us
    pallas_call x1, Pallas kernels, local_step(): pl.pallas_call(prepare_kernel, out_shape=(jax.ShapeDtypeStruct((BLOCKS, 8...  1.9 us
    pallas_call x1, Pallas kernels, local_step(): pl.pallas_call(finish_kernel, out_shape=(jax.ShapeDtypeStruct((3, CAP), f...  0.65 us

profile of v7, /device:TPU:0, one launch (start us, length us, event | category | flops | bytes accessed | tf_op | source)
XLA Modules:
  0.0 19.1 jit_solution(16253575807634805768)
XLA Ops:
  1.3 9.5 %exchange.1 = (f32[12,3,6,128]{3,2,1,0:T(8,128)S(1)}, f32[15,8,128]{2,1,0:T(8,128)S(1)}, f32[16,768]{1,0:T(8,128)S(1)}) custom-call(f32[]{:T(128)S(6)} %copy.12.brick_ref, f32[3,729]{1,0:T(4,128)} %bitcast.6, f32[3,729]{1,0:T(4,128)} %bitcast.7, f32[3,729]{1,0:T(4,128)} %bitcast.8, s32[729]{0:T(1024)} %id_ref.1, s32[729]{0:T(1024)} %ok_ref.1), custom_call_target="tpu_custom_call" | custom-call | tf_op jit(solution)/shard_map/exchange/pallas_call | solution.py:544
  10.8 1.9 %prepare.1 = (f32[6,8,128]{2,1,0:T(8,128)S(1)}, f32[3,96,8,128]{3,2,1,0:T(8,128)S(1)}, f32[3,110,8,128]{3,2,1,0:T(8,128)S(1)}, f32[3,96,8,128]{3,2,1,0:T(8,128)S(1)}, f32[3,8,128]{2,1,0:T(8,128)S(1)}) custom-call(f32[12,3,6,128]{3,2,1,0:T(8,128)S(1)} %get-tuple-element.22.gat_ref, f32[15,8,128]{2,1,0:T(8,128)S(1)} %get-tuple-element.23.pkt_ref, ...), custom_call_target="tpu_custom_call" | custom-call | tf_op jit(solution)/shard_map/prepare/pallas_call | solution.py:567
  12.7 5.7 %tile.1 = (f32[8,768]{1,0:T(8,128)S(1)}, f32[1,128]{1,0:T(1,128)S(1)}) custom-call(f32[3,96,8,128]{3,2,1,0:T(8,128)S(1)} %get-tuple-element.26.mine, f32[3,110,8,128]{3,2,1,0:T(8,128)S(1)} %get-tuple-element.27.others, f32[3,96,8,128]{3,2,1,0:T(8,128)S(1)} %get-tuple-element.28.part, f32[3,8,128]{2,1,0:T(8,128)S(1)} %get-tuple-element.29.eng_ref), custom_call_target="tpu_custom_call" | custom-call | tf_op jit(solution)/shard_map/tile/pallas_call | solution.py:575
  18.4 0.6 %finish.1 = (f32[3,729]{1,0:T(4,128)}, f32[3,729]{1,0:T(4,128)}, f32[3,729]{1,0:T(4,128)}, s32[729]{0:T(1024)}, s32[729]{0:T(1024)}, /*index=5*/f32[]{:T(128)}) custom-call(f32[6,8,128]{2,1,0:T(8,128)S(1)} %get-tuple-element.25.sorted_ref, f32[8,768]{1,0:T(8,128)S(1)} %get-tuple-element.30.frc_ref, f32[1,128]{1,0:T(1,128)S(1)} %get-tuple-element.31.total_ref), custom_call_target="tpu_custom_call" | custom-call | tf_op jit(solution)/shard_map/finish/pallas_call | solution.py:584

commit v8 on v7

--- a/solution.py
+++ b/solution.py
@@ -54,7 +54,7 @@
     hi = values.astype(jnp.bfloat16).astype(jnp.float32)
     rest = values - hi
     mid = rest.astype(jnp.bfloat16).astype(jnp.float32)
-    return jnp.concatenate([hi, mid, rest - mid], axis=0).astype(jnp.bfloat16)
+    return jnp.concatenate([hi, mid, rest - mid], axis=0)
 
 
 def join3(parts):
@@ -160,7 +160,7 @@
     stay = code == STAY
     mover_slot = jnp.where(owned & jnp.logical_not(stay), slot, -1.0).astype(jnp.int32)
     pick = (iota((2 * LANES, WIDE), 0) == mover_slot).astype(jnp.float32).astype(jnp.bfloat16)
-    packet = join3(dot_nt(split3(data), pick))
+    packet = join3(dot_nt(split3(data).astype(jnp.bfloat16), pick))
     send_pkt[0] = packet[:, 0:LANES]
     send_pkt[1] = packet[:, LANES:2 * LANES]
     own_ref[0:8, :] = data
@@ -345,7 +345,8 @@
         n_upper, n_all = jnp.max(upper_end), jnp.max(all_end)
         eng_ref[2] = jnp.broadcast_to(upper_end.astype(jnp.float32), TILE)
         fits = n_upper <= ENERGY_ROWS * LANES
-        parts = split3(data)
+        parts = split3(data).astype(jnp.bfloat16)
+        spread = ((iota((24, 3 * LANES), 0) & 7) == lax.shift_right_logical(iota((24, 3 * LANES), 1), 7)).astype(jnp.bfloat16)
 
         def place_block(block):
             pick = (iota((LANES, span + 2 * LANES), 0) + block * LANES == rank).astype(jnp.float32).astype(jnp.bfloat16)
@@ -353,10 +354,10 @@
             sorted_ref[block] = rows_s
             valid = lane_1 + block * LANES < n_int
             own_rel = stack([rows_s[axis:axis + 1] - centre[axis] for axis in range(3)] + [rows_s[3:8]])
-            columns = jnp.where(valid, own_rel, FAR_OWN).T
+            tiles = dot_nn(split3(jnp.where(valid, own_rel, FAR_OWN)).T.astype(jnp.bfloat16), spread)
             for axis in range(3):
                 others[axis, block] = jnp.broadcast_to(jnp.where(valid, own_rel[axis:axis + 1], 0.0), TILE)
-                mine[axis, pl.ds(block * PER_BLOCK, PER_BLOCK)] = jnp.broadcast_to(columns[:, axis:axis + 1], (LANES, LANES)).reshape(16, 8, LANES)
+                mine[axis, pl.ds(block * PER_BLOCK, PER_BLOCK)] = tiles[:, axis * LANES:(axis + 1) * LANES].reshape(16, 8, LANES)
 
         lane_c = iota((cand, LANES), 1)
         is_upper = lane_c < uppers

time: 19.3 us -> 20.1 us (1.041)
  Pallas kernels: 17.8 us -> 18.6 us
    pallas_call x1, Pallas kernels: 1.9 us -> 2.74 us  [local_step(): pl.pallas_call(prepare_kernel, out_shape=(jax.ShapeDtypeStruct((BLOCKS, 8...]
where the time goes in v8:
time: 20.1 us; the launch traced here: 19.9 us
  Pallas kernels  18.6 us (93%)
  between operations  1.3 us (6%)
    pallas_call x1, Pallas kernels, local_step(): pl.pallas_call(exchange_kernel, out_shape=(jax.ShapeDtypeStruct((N_GROUPS...  9.49 us
    pallas_call x1, Pallas kernels, local_step(): pl.pallas_call(tile_kernel, out_shape=(jax.ShapeDtypeStruct((8, WIDE), f3...  5.74 us
    pallas_call x1, Pallas kernels, local_step(): pl.pallas_call(prepare_kernel, out_shape=(jax.ShapeDtypeStruct((BLOCKS, 8...  2.74 us
    pallas_call x1, Pallas kernels, local_step(): pl.pallas_call(finish_kernel, out_shape=(jax.ShapeDtypeStruct((3, CAP), f...  0.65 us

profile of v8, /device:TPU:0, one launch (start us, length us, event | category | flops | bytes accessed | tf_op | source)
XLA Modules:
  0.0 19.9 jit_solution(9245034888420673470)
XLA Ops:
  1.3 9.5 %exchange.1 = (f32[12,3,6,128]{3,2,1,0:T(8,128)S(1)}, f32[15,8,128]{2,1,0:T(8,128)S(1)}, f32[16,768]{1,0:T(8,128)S(1)}) custom-call(f32[]{:T(128)S(6)} %copy.12.brick_ref, f32[3,729]{1,0:T(4,128)} %bitcast.6, f32[3,729]{1,0:T(4,128)} %bitcast.7, f32[3,729]{1,0:T(4,128)} %bitcast.8, s32[729]{0:T(1024)} %id_ref.1, s32[729]{0:T(1024)} %ok_ref.1), custom_call_target="tpu_custom_call" | custom-call | tf_op jit(solution)/shard_map/exchange/pallas_call | solution.py:545
  10.8 2.7 %prepare.1 = (f32[6,8,128]{2,1,0:T(8,128)S(1)}, f32[3,96,8,128]{3,2,1,0:T(8,128)S(1)}, f32[3,110,8,128]{3,2,1,0:T(8,128)S(1)}, f32[3,96,8,128]{3,2,1,0:T(8,128)S(1)}, f32[3,8,128]{2,1,0:T(8,128)S(1)}) custom-call(f32[12,3,6,128]{3,2,1,0:T(8,128)S(1)} %get-tuple-element.22.gat_ref, f32[15,8,128]{2,1,0:T(8,128)S(1)} %get-tuple-element.23.pkt_ref, ...), custom_call_target="tpu_custom_call" | custom-call | tf_op jit(solution)/shard_map/prepare/pallas_call | solution.py:568
  13.5 5.7 %tile.1 = (f32[8,768]{1,0:T(8,128)S(1)}, f32[1,128]{1,0:T(1,128)S(1)}) custom-call(f32[3,96,8,128]{3,2,1,0:T(8,128)S(1)} %get-tuple-element.26.mine, f32[3,110,8,128]{3,2,1,0:T(8,128)S(1)} %get-tuple-element.27.others, f32[3,96,8,128]{3,2,1,0:T(8,128)S(1)} %get-tuple-element.28.part, f32[3,8,128]{2,1,0:T(8,128)S(1)} %get-tuple-element.29.eng_ref), custom_call_target="tpu_custom_call" | custom-call | tf_op jit(solution)/shard_map/tile/pallas_call | solution.py:576
  19.3 0.6 %finish.1 = (f32[3,729]{1,0:T(4,128)}, f32[3,729]{1,0:T(4,128)}, f32[3,729]{1,0:T(4,128)}, s32[729]{0:T(1024)}, s32[729]{0:T(1024)}, /*index=5*/f32[]{:T(128)}) custom-call(f32[6,8,128]{2,1,0:T(8,128)S(1)} %get-tuple-element.25.sorted_ref, f32[8,768]{1,0:T(8,128)S(1)} %get-tuple-element.30.frc_ref, f32[1,128]{1,0:T(1,128)S(1)} %get-tuple-element.31.total_ref), custom_call_target="tpu_custom_call" | custom-call | tf_op jit(solution)/shard_map/finish/pallas_call | solution.py:585

commit v9 on v7

--- a/solution.py
+++ b/solution.py
@@ -347,9 +347,11 @@
         fits = n_upper <= ENERGY_ROWS * LANES
         parts = split3(data)
 
+        pick = (iota((span, span + 2 * LANES), 0) == rank).astype(jnp.float32).astype(jnp.bfloat16)
+        chosen = dot_nt(pick, parts)
+
         def place_block(block):
-            pick = (iota((LANES, span + 2 * LANES), 0) + block * LANES == rank).astype(jnp.float32).astype(jnp.bfloat16)
-            rows_s = join3((dot_nt(pick, parts)).T)
+            rows_s = join3(chosen[block * LANES:(block + 1) * LANES].T)
             sorted_ref[block] = rows_s
             valid = lane_1 + block * LANES < n_int
             own_rel = stack([rows_s[axis:axis + 1] - centre[axis] for axis in range(3)] + [rows_s[3:8]])

time: 19.3 us -> 19.1 us (0.990)
  Pallas kernels: 17.8 us -> 17.6 us
where the time goes in v9:
time: 19.1 us; the launch traced here: 18.9 us
  Pallas kernels  17.6 us (92%)
  between operations  1.3 us (7%)
    pallas_call x1, Pallas kernels, local_step(): pl.pallas_call(exchange_kernel, out_shape=(jax.ShapeDtypeStruct((N_GROUPS...  9.49 us
    pallas_call x1, Pallas kernels, local_step(): pl.pallas_call(tile_kernel, out_shape=(jax.ShapeDtypeStruct((8, WIDE), f3...  5.74 us
    pallas_call x1, Pallas kernels, local_step(): pl.pallas_call(prepare_kernel, out_shape=(jax.ShapeDtypeStruct((BLOCKS, 8...  1.75 us
    pallas_call x1, Pallas kernels, local_step(): pl.pallas_call(finish_kernel, out_shape=(jax.ShapeDtypeStruct((3, CAP), f...  0.65 us

profile of v9, /device:TPU:0, one launch (start us, length us, event | category | flops | bytes accessed | tf_op | source)
XLA Modules:
  0.0 18.9 jit_solution(15308066902764667443)
XLA Ops:
  1.3 9.5 %exchange.1 = (f32[12,3,6,128]{3,2,1,0:T(8,128)S(1)}, f32[15,8,128]{2,1,0:T(8,128)S(1)}, f32[16,768]{1,0:T(8,128)S(1)}) custom-call(f32[]{:T(128)S(6)} %copy.12.brick_ref, f32[3,729]{1,0:T(4,128)} %bitcast.6, f32[3,729]{1,0:T(4,128)} %bitcast.7, f32[3,729]{1,0:T(4,128)} %bitcast.8, s32[729]{0:T(1024)} %id_ref.1, s32[729]{0:T(1024)} %ok_ref.1), custom_call_target="tpu_custom_call" | custom-call | tf_op jit(solution)/shard_map/exchange/pallas_call | solution.py:546
  10.8 1.7 %prepare.1 = (f32[6,8,128]{2,1,0:T(8,128)S(1)}, f32[3,96,8,128]{3,2,1,0:T(8,128)S(1)}, f32[3,110,8,128]{3,2,1,0:T(8,128)S(1)}, f32[3,96,8,128]{3,2,1,0:T(8,128)S(1)}, f32[3,8,128]{2,1,0:T(8,128)S(1)}) custom-call(f32[12,3,6,128]{3,2,1,0:T(8,128)S(1)} %get-tuple-element.22.gat_ref, f32[15,8,128]{2,1,0:T(8,128)S(1)} %get-tuple-element.23.pkt_ref, ...), custom_call_target="tpu_custom_call" | custom-call | tf_op jit(solution)/shard_map/prepare/pallas_call | solution.py:569
  12.5 5.7 %tile.1 = (f32[8,768]{1,0:T(8,128)S(1)}, f32[1,128]{1,0:T(1,128)S(1)}) custom-call(f32[3,96,8,128]{3,2,1,0:T(8,128)S(1)} %get-tuple-element.26.mine, f32[3,110,8,128]{3,2,1,0:T(8,128)S(1)} %get-tuple-element.27.others, f32[3,96,8,128]{3,2,1,0:T(8,128)S(1)} %get-tuple-element.28.part, f32[3,8,128]{2,1,0:T(8,128)S(1)} %get-tuple-element.29.eng_ref), custom_call_target="tpu_custom_call" | custom-call | tf_op jit(solution)/shard_map/tile/pallas_call | solution.py:577
  18.3 0.6 %finish.1 = (f32[3,729]{1,0:T(4,128)}, f32[3,729]{1,0:T(4,128)}, f32[3,729]{1,0:T(4,128)}, s32[729]{0:T(1024)}, s32[729]{0:T(1024)}, /*index=5*/f32[]{:T(128)}) custom-call(f32[6,8,128]{2,1,0:T(8,128)S(1)} %get-tuple-element.25.sorted_ref, f32[8,768]{1,0:T(8,128)S(1)} %get-tuple-element.30.frc_ref, f32[1,128]{1,0:T(1,128)S(1)} %get-tuple-element.31.total_ref), custom_call_target="tpu_custom_call" | custom-call | tf_op jit(solution)/shard_map/finish/pallas_call | solution.py:586

commit v10 on v9

--- a/solution.py
+++ b/solution.py
@@ -321,12 +321,9 @@
         mixed = jnp.where(near & (side > 0.0), 256.0, jnp.where(near & (side < 0.0), 1.0, 0.0)).astype(jnp.bfloat16)
         row_l, col_l = iota((LANES, LANES), 0), iota((LANES, LANES), 1)
 
-        def counts(chosen):
-            return dot_nn(mixed, chosen.astype(jnp.bfloat16)).astype(jnp.int32)
-
-        cum = counts(row_l <= col_l)
-        total = counts(row_l >= 0)
-        marks = [counts(row_l < 16 * k) for k in range(1, 8)]
+        levels = beside([(row_l <= col_l)] + [row_l < 16 * k for k in range(1, 9)]).astype(jnp.float32).astype(jnp.bfloat16)
+        counts = dot_nn(mixed, levels).astype(jnp.int32)
+        cum, *marks, total = [counts[:, k * LANES:(k + 1) * LANES] for k in range(9)]
         arr_col = jnp.broadcast_to(arr_id, (8, 2 * LANES)).T[:, 0:1]
         arr_first = (arr_col < beside([own_id, arr_id])).astype(jnp.float32)
         arr_before = down(arr_first)
@@ -336,12 +333,11 @@
         earlier = (iota((cand, cand), 1) < iota((cand, cand), 0)).astype(jnp.bfloat16)
         uppers, lowers = lax.shift_right_logical(total, 8), total & 255
 
-        def starts(each, first):
-            base = dot_nn(earlier, each.astype(jnp.float32).astype(jnp.bfloat16)).astype(jnp.int32) + first
-            return base, base[cand - 1:] + each[cand - 1:]
-
-        upper_base, upper_end = starts(uppers, n_int)
-        lower_base, all_end = starts(lowers, upper_end)
+        bases = dot_nn(earlier, beside([uppers, lowers]).astype(jnp.float32).astype(jnp.bfloat16)).astype(jnp.int32)
+        upper_base = bases[:, :LANES] + n_int
+        upper_end = upper_base[cand - 1:] + uppers[cand - 1:]
+        lower_base = bases[:, LANES:] + upper_end
+        all_end = lower_base[cand - 1:] + lowers[cand - 1:]
         n_upper, n_all = jnp.max(upper_end), jnp.max(all_end)
         eng_ref[2] = jnp.broadcast_to(upper_end.astype(jnp.float32), TILE)
         fits = n_upper <= ENERGY_ROWS * LANES

time: 19.1 us -> 19.2 us (level)
  no operation moved by 1% of the time
where the time goes in v10:
time: 19.2 us; the launch traced here: 19 us
  Pallas kernels  17.7 us (92%)
  between operations  1.3 us (7%)
    pallas_call x1, Pallas kernels, local_step(): pl.pallas_call(exchange_kernel, out_shape=(jax.ShapeDtypeStruct((N_GROUPS...  9.49 us
    pallas_call x1, Pallas kernels, local_step(): pl.pallas_call(tile_kernel, out_shape=(jax.ShapeDtypeStruct((8, WIDE), f3...  5.74 us
    pallas_call x1, Pallas kernels, local_step(): pl.pallas_call(prepare_kernel, out_shape=(jax.ShapeDtypeStruct((BLOCKS, 8...  1.83 us
    pallas_call x1, Pallas kernels, local_step(): pl.pallas_call(finish_kernel, out_shape=(jax.ShapeDtypeStruct((3, CAP), f...  0.65 us

profile of v10, /device:TPU:0, one launch (start us, length us, event | category | flops | bytes accessed | tf_op | source)
XLA Modules:
  0.0 19.0 jit_solution(5323150651344908551)
XLA Ops:
  1.3 9.5 %exchange.1 = (f32[12,3,6,128]{3,2,1,0:T(8,128)S(1)}, f32[15,8,128]{2,1,0:T(8,128)S(1)}, f32[16,768]{1,0:T(8,128)S(1)}) custom-call(f32[]{:T(128)S(6)} %copy.12.brick_ref, f32[3,729]{1,0:T(4,128)} %bitcast.6, f32[3,729]{1,0:T(4,128)} %bitcast.7, f32[3,729]{1,0:T(4,128)} %bitcast.8, s32[729]{0:T(1024)} %id_ref.1, s32[729]{0:T(1024)} %ok_ref.1), custom_call_target="tpu_custom_call" | custom-call | tf_op jit(solution)/shard_map/exchange/pallas_call | solution.py:542
  10.8 1.8 %prepare.1 = (f32[6,8,128]{2,1,0:T(8,128)S(1)}, f32[3,96,8,128]{3,2,1,0:T(8,128)S(1)}, f32[3,110,8,128]{3,2,1,0:T(8,128)S(1)}, f32[3,96,8,128]{3,2,1,0:T(8,128)S(1)}, f32[3,8,128]{2,1,0:T(8,128)S(1)}) custom-call(f32[12,3,6,128]{3,2,1,0:T(8,128)S(1)} %get-tuple-element.22.gat_ref, f32[15,8,128]{2,1,0:T(8,128)S(1)} %get-tuple-element.23.pkt_ref, ...), custom_call_target="tpu_custom_call" | custom-call | tf_op jit(solution)/shard_map/prepare/pallas_call | solution.py:565
  12.6 5.7 %tile.1 = (f32[8,768]{1,0:T(8,128)S(1)}, f32[1,128]{1,0:T(1,128)S(1)}) custom-call(f32[3,96,8,128]{3,2,1,0:T(8,128)S(1)} %get-tuple-element.26.mine, f32[3,110,8,128]{3,2,1,0:T(8,128)S(1)} %get-tuple-element.27.others, f32[3,96,8,128]{3,2,1,0:T(8,128)S(1)} %get-tuple-element.28.part, f32[3,8,128]{2,1,0:T(8,128)S(1)} %get-tuple-element.29.eng_ref), custom_call_target="tpu_custom_call" | custom-call | tf_op jit(solution)/shard_map/tile/pallas_call | solution.py:573
  18.4 0.6 %finish.1 = (f32[3,729]{1,0:T(4,128)}, f32[3,729]{1,0:T(4,128)}, f32[3,729]{1,0:T(4,128)}, s32[729]{0:T(1024)}, s32[729]{0:T(1024)}, /*index=5*/f32[]{:T(128)}) custom-call(f32[6,8,128]{2,1,0:T(8,128)S(1)} %get-tuple-element.25.sorted_ref, f32[8,768]{1,0:T(8,128)S(1)} %get-tuple-element.30.frc_ref, f32[1,128]{1,0:T(1,128)S(1)} %get-tuple-element.31.total_ref), custom_call_target="tpu_custom_call" | custom-call | tf_op jit(solution)/shard_map/finish/pallas_call | solution.py:582

commit v11 on v9

--- a/solution.py
+++ b/solution.py
@@ -258,7 +258,14 @@
     return load_own, energy_row, force_row
 
 
-def prepare_kernel(gat_ref, pkt_ref, own_ref, sorted_ref, mine, others, acc, eng_ref):
+def spread_own(rel_ref, mine, blocks):
+    for block in range(blocks):
+        columns = rel_ref[block].T
+        for axis in range(3):
+            mine[axis, pl.ds(block * PER_BLOCK, PER_BLOCK)] = jnp.broadcast_to(columns[:, axis:axis + 1], (LANES, LANES)).reshape(PER_BLOCK, *TILE)
+
+
+def prepare_kernel(gat_ref, pkt_ref, own_ref, sorted_ref, rel_ref, others, acc, eng_ref, mine):
     mz, my, mx = my_coords()
     brick = own_ref[9:10, 0:LANES]
     half_l = 0.5 * brick
@@ -355,10 +362,9 @@
             sorted_ref[block] = rows_s
             valid = lane_1 + block * LANES < n_int
             own_rel = stack([rows_s[axis:axis + 1] - centre[axis] for axis in range(3)] + [rows_s[3:8]])
-            columns = jnp.where(valid, own_rel, FAR_OWN).T
+            rel_ref[block] = jnp.where(valid, own_rel, FAR_OWN)
             for axis in range(3):
                 others[axis, block] = jnp.broadcast_to(jnp.where(valid, own_rel[axis:axis + 1], 0.0), TILE)
-                mine[axis, pl.ds(block * PER_BLOCK, PER_BLOCK)] = jnp.broadcast_to(columns[:, axis:axis + 1], (LANES, LANES)).reshape(16, 8, LANES)
 
         lane_c = iota((cand, LANES), 1)
         is_upper = lane_c < uppers
@@ -432,15 +438,21 @@
 
             return lax.fori_loop(first_quad, last_quad, quad, energy)
 
-        def plain():
+        def leftover():
+            spread_own(rel_ref, mine, blocks)
             short = jnp.where(rows > FIXED_ROWS, jnp.minimum(quads, FIXED_QUADS), 0)
             energy = excess(0, short, FIXED_ROWS, [], zero)
             if blocks > FIXED_BLOCKS:
                 energy = excess(FIXED_QUADS, quads, 0, [], energy)
             eng_ref[0] = energy
+
+        def plain():
+            eng_ref[0] = zero
+            pl.when((rows > FIXED_ROWS) | (quads > FIXED_QUADS))(leftover)
             lax.fori_loop(rows, FIXED_ROWS, set_far, 0)
 
         def alone(wrap_box):
+            spread_own(rel_ref, mine, blocks)
             eng_ref[0] = excess(0, quads, 0, wrap_box, zero)
             lax.fori_loop(0, FIXED_ROWS, set_far, 0)
 
@@ -452,11 +464,12 @@
     pl.when(jnp.logical_not(small))(lambda: build(BLOCKS, BLOCKS))
 
 
-def tile_kernel(mine, others, part, eng_ref, frc_ref, out_ref, acc, react, eng, slots, send_sem, recv_sem):
+def tile_kernel(rel_ref, others, part, eng_ref, frc_ref, out_ref, mine, acc, react, eng, slots, send_sem, recv_sem):
     coords = my_coords()
     mz, my, mx = coords
     barrier = entry_signals(coords)
-    rc2 = RC * RC + 0.0 * mine[0, 0]
+    rc2 = RC * RC + 0.0 * rel_ref[0]
+    spread_own(rel_ref, mine, FIXED_BLOCKS)
     load_own, energy_row, force_row = pair_tools(mine, others, rc2, [])
 
     lane_8 = iota(TILE, 1).astype(jnp.float32)
@@ -566,11 +579,13 @@
             name="exchange",
         )(brick_side, *(pltpu.with_memory_space_constraint(value, pltpu.HBM) for value in (atom_pos.T, atom_vel.T, atom_frc.T, atom_id, atom_ok)))
         own_tiles = jax.ShapeDtypeStruct((3, GROUPS_OWN, 8, LANES), f32)
-        placed, mine, others, part, eng = pl.pallas_call(
+        block_rows = jax.ShapeDtypeStruct((BLOCKS, 8, LANES), f32)
+        placed, rel, others, part, eng = pl.pallas_call(
             prepare_kernel,
-            out_shape=(jax.ShapeDtypeStruct((BLOCKS, 8, LANES), f32), own_tiles, jax.ShapeDtypeStruct((3, MAX_ROWS, 8, LANES), f32), own_tiles, jax.ShapeDtypeStruct((3, 8, LANES), f32)),
+            out_shape=(block_rows, block_rows, jax.ShapeDtypeStruct((3, MAX_ROWS, 8, LANES), f32), own_tiles, jax.ShapeDtypeStruct((3, 8, LANES), f32)),
             in_specs=[VMEM_SPEC] * 3,
             out_specs=(VMEM_SPEC,) * 5,
+            scratch_shapes=[pltpu.VMEM(own_tiles.shape, f32)],
             compiler_params=pltpu.CompilerParams(vmem_limit_bytes=VMEM_LIMIT),
             name="prepare",
         )(gat, pkt, own)
@@ -579,10 +594,10 @@
             out_shape=(jax.ShapeDtypeStruct((8, WIDE), f32), jax.ShapeDtypeStruct((1, LANES), f32)),
             in_specs=[VMEM_SPEC] * 4,
             out_specs=(VMEM_SPEC,) * 2,
-            scratch_shapes=[pltpu.VMEM((3, FIXED_BLOCKS * 16, 8, LANES), f32), pltpu.VMEM((3, FIXED_BLOCKS, 8, LANES), f32), pltpu.VMEM((1, LANES), f32), pltpu.VMEM((n_dev, 1, LANES), f32), pltpu.SemaphoreType.DMA((n_dev - 1,)), pltpu.SemaphoreType.DMA((n_dev - 1,))],
+            scratch_shapes=[pltpu.VMEM((3, FIXED_BLOCKS * PER_BLOCK, 8, LANES), f32)] * 2 + [pltpu.VMEM((3, FIXED_BLOCKS, 8, LANES), f32), pltpu.VMEM((1, LANES), f32), pltpu.VMEM((n_dev, 1, LANES), f32), pltpu.SemaphoreType.DMA((n_dev - 1,)), pltpu.SemaphoreType.DMA((n_dev - 1,))],
             compiler_params=pltpu.CompilerParams(collective_id=1, has_side_effects=True, vmem_limit_bytes=VMEM_LIMIT),
             name="tile",
-        )(mine, others, part, eng)
+        )(rel, others, part, eng)
         pos, vel, frc, ids, oks, energy = pl.pallas_call(
             finish_kernel,
             out_shape=(jax.ShapeDtypeStruct((3, CAP), f32),) * 3 + (jax.ShapeDtypeStruct((CAP,), jnp.int32),) * 2 + (jax.ShapeDtypeStruct((), f32),),

time: 19.1 us -> 19 us (level)
    pallas_call x1, Pallas kernels: 1.75 us -> 1.26 us  [local_step(): pl.pallas_call(prepare_kernel, out_shape=(block_rows, block_rows, jax.Sha...]
    pallas_call x1, Pallas kernels: 5.74 us -> 6.08 us  [local_step(): pl.pallas_call(tile_kernel, out_shape=(jax.ShapeDtypeStruct((8, WIDE), f3...]
where the time goes in v11:
time: 19 us; the launch traced here: 18.8 us
  Pallas kernels  17.5 us (92%)
  between operations  1.3 us (7%)
    pallas_call x1, Pallas kernels, local_step(): pl.pallas_call(exchange_kernel, out_shape=(jax.ShapeDtypeStruct((N_GROUPS...  9.49 us
    pallas_call x1, Pallas kernels, local_step(): pl.pallas_call(tile_kernel, out_shape=(jax.ShapeDtypeStruct((8, WIDE), f3...  6.08 us
    pallas_call x1, Pallas kernels, local_step(): pl.pallas_call(prepare_kernel, out_shape=(block_rows, block_rows, jax.Sha...  1.26 us
    pallas_call x1, Pallas kernels, local_step(): pl.pallas_call(finish_kernel, out_shape=(jax.ShapeDtypeStruct((3, CAP), f...  0.65 us

profile of v11, /device:TPU:0, one launch (start us, length us, event | category | flops | bytes accessed | tf_op | source)
XLA Modules:
  0.0 18.8 jit_solution(8329950514840236756)
XLA Ops:
  1.3 9.5 %exchange.1 = (f32[12,3,6,128]{3,2,1,0:T(8,128)S(1)}, f32[15,8,128]{2,1,0:T(8,128)S(1)}, f32[16,768]{1,0:T(8,128)S(1)}) custom-call(f32[]{:T(128)S(6)} %copy.12.brick_ref, f32[3,729]{1,0:T(4,128)} %bitcast.6, f32[3,729]{1,0:T(4,128)} %bitcast.7, f32[3,729]{1,0:T(4,128)} %bitcast.8, s32[729]{0:T(1024)} %id_ref.1, s32[729]{0:T(1024)} %ok_ref.1), custom_call_target="tpu_custom_call" | custom-call | tf_op jit(solution)/shard_map/exchange/pallas_call | solution.py:559
  10.8 1.3 %prepare.1 = (f32[6,8,128]{2,1,0:T(8,128)S(1)}, f32[6,8,128]{2,1,0:T(8,128)S(1)}, f32[3,110,8,128]{3,2,1,0:T(8,128)S(1)}, f32[3,96,8,128]{3,2,1,0:T(8,128)S(1)}, f32[3,8,128]{2,1,0:T(8,128)S(1)}) custom-call(f32[12,3,6,128]{3,2,1,0:T(8,128)S(1)} %get-tuple-element.22.gat_ref, f32[15,8,128]{2,1,0:T(8,128)S(1)} %get-tuple-element.23.pkt_ref, ...), custom_call_target="tpu_custom_call" | custom-call | tf_op jit(solution)/shard_map/prepare/pallas_call | solution.py:583
  12.0 6.1 %tile.1 = (f32[8,768]{1,0:T(8,128)S(1)}, f32[1,128]{1,0:T(1,128)S(1)}) custom-call(f32[6,8,128]{2,1,0:T(8,128)S(1)} %get-tuple-element.26.rel_ref, f32[3,110,8,128]{3,2,1,0:T(8,128)S(1)} %get-tuple-element.27.others, f32[3,96,8,128]{3,2,1,0:T(8,128)S(1)} %get-tuple-element.28.part, f32[3,8,128]{2,1,0:T(8,128)S(1)} %get-tuple-element.29.eng_ref), custom_call_target="tpu_custom_call" | custom-call | tf_op jit(solution)/shard_map/tile/pallas_call | solution.py:592
  18.1 0.6 %finish.1 = (f32[3,729]{1,0:T(4,128)}, f32[3,729]{1,0:T(4,128)}, f32[3,729]{1,0:T(4,128)}, s32[729]{0:T(1024)}, s32[729]{0:T(1024)}, /*index=5*/f32[]{:T(128)}) custom-call(f32[6,8,128]{2,1,0:T(8,128)S(1)} %get-tuple-element.25.sorted_ref, f32[8,768]{1,0:T(8,128)S(1)} %get-tuple-element.30.frc_ref, f32[1,128]{1,0:T(1,128)S(1)} %get-tuple-element.31.total_ref), custom_call_target="tpu_custom_call" | custom-call | tf_op jit(solution)/shard_map/finish/pallas_call | solution.py:601

commit v12 on v11

--- a/solution.py
+++ b/solution.py
@@ -150,11 +150,11 @@
     running = jnp.zeros((32, LANES), jnp.float32)
     for move, first in LANE_BASE.items():
         running = jnp.where(codes == move, float(first), running)
+    pieces = [member[:, block * LANES:(block + 1) * LANES] for block in range(BLOCKS)]
+    before = dot_nn(stack(pieces).astype(jnp.bfloat16), tri)
     slots = []
-    for block in range(BLOCKS):
-        part = member[:, block * LANES:(block + 1) * LANES]
-        before = dot_nn(part.astype(jnp.bfloat16), tri)
-        slots.append(down(part * (before + running)))
+    for block, part in enumerate(pieces):
+        slots.append(down(part * (before[32 * block:32 * block + 32] + running)))
         running = running + across(part)
     slot = beside(slots)
     stay = code == STAY

time: 19 us -> 19 us (level)
  no operation moved by 1% of the time
where the time goes in v12:
time: 19 us; the launch traced here: 18.8 us
  Pallas kernels  17.5 us (92%)
  between operations  1.3 us (7%)
    pallas_call x1, Pallas kernels, local_step(): pl.pallas_call(exchange_kernel, out_shape=(jax.ShapeDtypeStruct((N_GROUPS...  9.49 us
    pallas_call x1, Pallas kernels, local_step(): pl.pallas_call(tile_kernel, out_shape=(jax.ShapeDtypeStruct((8, WIDE), f3...  6.06 us
    pallas_call x1, Pallas kernels, local_step(): pl.pallas_call(prepare_kernel, out_shape=(block_rows, block_rows, jax.Sha...  1.27 us
    pallas_call x1, Pallas kernels, local_step(): pl.pallas_call(finish_kernel, out_shape=(jax.ShapeDtypeStruct((3, CAP), f...  0.65 us

profile of v12, /device:TPU:0, one launch (start us, length us, event | category | flops | bytes accessed | tf_op | source)
XLA Modules:
  0.0 18.8 jit_solution(12471969347823799089)
XLA Ops:
  1.3 9.5 %exchange.1 = (f32[12,3,6,128]{3,2,1,0:T(8,128)S(1)}, f32[15,8,128]{2,1,0:T(8,128)S(1)}, f32[16,768]{1,0:T(8,128)S(1)}) custom-call(f32[]{:T(128)S(6)} %copy.12.brick_ref, f32[3,729]{1,0:T(4,128)} %bitcast.6, f32[3,729]{1,0:T(4,128)} %bitcast.7, f32[3,729]{1,0:T(4,128)} %bitcast.8, s32[729]{0:T(1024)} %id_ref.1, s32[729]{0:T(1024)} %ok_ref.1), custom_call_target="tpu_custom_call" | custom-call | tf_op jit(solution)/shard_map/exchange/pallas_call | solution.py:559
  10.8 1.3 %prepare.1 = (f32[6,8,128]{2,1,0:T(8,128)S(1)}, f32[6,8,128]{2,1,0:T(8,128)S(1)}, f32[3,110,8,128]{3,2,1,0:T(8,128)S(1)}, f32[3,96,8,128]{3,2,1,0:T(8,128)S(1)}, f32[3,8,128]{2,1,0:T(8,128)S(1)}) custom-call(f32[12,3,6,128]{3,2,1,0:T(8,128)S(1)} %get-tuple-element.22.gat_ref, f32[15,8,128]{2,1,0:T(8,128)S(1)} %get-tuple-element.23.pkt_ref, ...), custom_call_target="tpu_custom_call" | custom-call | tf_op jit(solution)/shard_map/prepare/pallas_call | solution.py:583
  12.0 6.1 %tile.1 = (f32[8,768]{1,0:T(8,128)S(1)}, f32[1,128]{1,0:T(1,128)S(1)}) custom-call(f32[6,8,128]{2,1,0:T(8,128)S(1)} %get-tuple-element.26.rel_ref, f32[3,110,8,128]{3,2,1,0:T(8,128)S(1)} %get-tuple-element.27.others, f32[3,96,8,128]{3,2,1,0:T(8,128)S(1)} %get-tuple-element.28.part, f32[3,8,128]{2,1,0:T(8,128)S(1)} %get-tuple-element.29.eng_ref), custom_call_target="tpu_custom_call" | custom-call | tf_op jit(solution)/shard_map/tile/pallas_call | solution.py:592
  18.1 0.6 %finish.1 = (f32[3,729]{1,0:T(4,128)}, f32[3,729]{1,0:T(4,128)}, f32[3,729]{1,0:T(4,128)}, s32[729]{0:T(1024)}, s32[729]{0:T(1024)}, /*index=5*/f32[]{:T(128)}) custom-call(f32[6,8,128]{2,1,0:T(8,128)S(1)} %get-tuple-element.25.sorted_ref, f32[8,768]{1,0:T(8,128)S(1)} %get-tuple-element.30.frc_ref, f32[1,128]{1,0:T(1,128)S(1)} %get-tuple-element.31.total_ref), custom_call_target="tpu_custom_call" | custom-call | tf_op jit(solution)/shard_map/finish/pallas_call | solution.py:601

commit v13 on v12

--- a/solution.py
+++ b/solution.py
@@ -167,7 +167,8 @@
     own_ref[8:16, :] = stack([jnp.where(stay, slot, -1.0), jnp.full((7, WIDE), brick, jnp.float32)])
     pl.semaphore_wait(barrier, len(PEERS))
     copies = []
-    for index, (gx, gy, gz) in enumerate(GROUPS + DISTANT):
+    order = list(enumerate(GROUPS + DISTANT))
+    for index, (gx, gy, gz) in order[N_GROUPS:] + order[:N_GROUPS]:
         peer = peer_id(coords, (gz, gy, gx))
         if index < N_GROUPS:
             copies.append(pltpu.make_async_remote_copy(src_ref=send_pos, dst_ref=gat_ref.at[index], send_sem=pos_send_sem.at[index], recv_sem=pos_recv_sem.at[index], device_id=peer, device_id_type=MESH))
@@ -207,6 +208,8 @@
         trial = ulps * 2.0 ** -34 - RC * cut_core
         kappa = jnp.where(trial * cut_inv_r == -cut_core, trial, kappa)
 
+    kappa_12 = 12.0 * kappa
+
     def quad_energy(dist_sqs):
         terms, tails = [], []
         for dist_sq in dist_sqs:
@@ -214,8 +217,8 @@
             inv_2 = inv_r * inv_r
             term = inv_2 * inv_2 * inv_2 - 0.5
             terms.append(term * term)
-            tails.append(kappa * inv_r * dist_sq)
-        return ((terms[0] + terms[1]) + (terms[2] + terms[3])) - 12.0 * ((tails[0] + tails[1]) + (tails[2] + tails[3]))
+            tails.append(kappa_12 * inv_r * dist_sq)
+        return ((terms[0] + terms[1]) + (terms[2] + terms[3])) - ((tails[0] + tails[1]) + (tails[2] + tails[3]))
 
     cut_energy = quad_energy([rc2] * QUAD)
     own_minus_lane = iota(TILE, 0) - iota(TILE, 1)

time: 19 us -> 18.5 us (0.974)
  Pallas kernels: 17.5 us -> 17 us
    pallas_call x1, Pallas kernels: 9.49 us -> 9.17 us  [local_step(): pl.pallas_call(exchange_kernel, out_shape=(jax.ShapeDtypeStruct((N_GROUPS...]
where the time goes in v13:
time: 18.5 us; the launch traced here: 18.3 us
  Pallas kernels  17 us (92%)
  between operations  1.3 us (7%)
    pallas_call x1, Pallas kernels, local_step(): pl.pallas_call(exchange_kernel, out_shape=(jax.ShapeDtypeStruct((N_GROUPS...  9.17 us
    pallas_call x1, Pallas kernels, local_step(): pl.pallas_call(tile_kernel, out_shape=(jax.ShapeDtypeStruct((8, WIDE), f3...  5.92 us
    pallas_call x1, Pallas kernels, local_step(): pl.pallas_call(prepare_kernel, out_shape=(block_rows, block_rows, jax.Sha...  1.27 us
    pallas_call x1, Pallas kernels, local_step(): pl.pallas_call(finish_kernel, out_shape=(jax.ShapeDtypeStruct((3, CAP), f...  0.65 us

profile of v13, /device:TPU:0, one launch (start us, length us, event | category | flops | bytes accessed | tf_op | source)
XLA Modules:
  0.0 18.3 jit_solution(8998840222285525462)
XLA Ops:
  1.3 9.2 %exchange.1 = (f32[12,3,6,128]{3,2,1,0:T(8,128)S(1)}, f32[15,8,128]{2,1,0:T(8,128)S(1)}, f32[16,768]{1,0:T(8,128)S(1)}) custom-call(f32[]{:T(128)S(6)} %copy.12.brick_ref, f32[3,729]{1,0:T(4,128)} %bitcast.6, f32[3,729]{1,0:T(4,128)} %bitcast.7, f32[3,729]{1,0:T(4,128)} %bitcast.8, s32[729]{0:T(1024)} %id_ref.1, s32[729]{0:T(1024)} %ok_ref.1), custom_call_target="tpu_custom_call" | custom-call | tf_op jit(solution)/shard_map/exchange/pallas_call | solution.py:562
  10.5 1.3 %prepare.1 = (f32[6,8,128]{2,1,0:T(8,128)S(1)}, f32[6,8,128]{2,1,0:T(8,128)S(1)}, f32[3,110,8,128]{3,2,1,0:T(8,128)S(1)}, f32[3,96,8,128]{3,2,1,0:T(8,128)S(1)}, f32[3,8,128]{2,1,0:T(8,128)S(1)}) custom-call(f32[12,3,6,128]{3,2,1,0:T(8,128)S(1)} %get-tuple-element.22.gat_ref, f32[15,8,128]{2,1,0:T(8,128)S(1)} %get-tuple-element.23.pkt_ref, ...), custom_call_target="tpu_custom_call" | custom-call | tf_op jit(solution)/shard_map/prepare/pallas_call | solution.py:586
  11.7 5.9 %tile.1 = (f32[8,768]{1,0:T(8,128)S(1)}, f32[1,128]{1,0:T(1,128)S(1)}) custom-call(f32[6,8,128]{2,1,0:T(8,128)S(1)} %get-tuple-element.26.rel_ref, f32[3,110,8,128]{3,2,1,0:T(8,128)S(1)} %get-tuple-element.27.others, f32[3,96,8,128]{3,2,1,0:T(8,128)S(1)} %get-tuple-element.28.part, f32[3,8,128]{2,1,0:T(8,128)S(1)} %get-tuple-element.29.eng_ref), custom_call_target="tpu_custom_call" | custom-call | tf_op jit(solution)/shard_map/tile/pallas_call | solution.py:595
  17.7 0.6 %finish.1 = (f32[3,729]{1,0:T(4,128)}, f32[3,729]{1,0:T(4,128)}, f32[3,729]{1,0:T(4,128)}, s32[729]{0:T(1024)}, s32[729]{0:T(1024)}, /*index=5*/f32[]{:T(128)}) custom-call(f32[6,8,128]{2,1,0:T(8,128)S(1)} %get-tuple-element.25.sorted_ref, f32[8,768]{1,0:T(8,128)S(1)} %get-tuple-element.30.frc_ref, f32[1,128]{1,0:T(1,128)S(1)} %get-tuple-element.31.total_ref), custom_call_target="tpu_custom_call" | custom-call | tf_op jit(solution)/shard_map/finish/pallas_call | solution.py:604

commit v14 on v13

--- a/solution.py
+++ b/solution.py
@@ -22,7 +22,8 @@
 FAR_OTHER = -1.0e4
 NOWHERE = 1.0e9
 GHOST_SQ = RC * RC + 0.01
-PEERS = [(dz, dy, dx) for dz in range(NZ) for dy in range(NY) for dx in range(NX)][:0:-1]
+PEERS = [(dz, dy, dx) for dz in range(NZ) for dy in range(NY) for dx in range(NX)][1:]
+PEERS.sort(key=lambda offset: -2 * (offset[0] + offset[1]) - (1, 2, 3, 2)[offset[2]])
 SIDES = [(1, 1), (1, 0), (0, 1), (0, 0)]
 GROUPS = [(gx, *side) for side in SIDES for gx in (1, -1)] + [(0, *side) for side in SIDES[:3]]
 N_GROUPS = len(GROUPS)
@@ -167,8 +168,8 @@
     own_ref[8:16, :] = stack([jnp.where(stay, slot, -1.0), jnp.full((7, WIDE), brick, jnp.float32)])
     pl.semaphore_wait(barrier, len(PEERS))
     copies = []
-    order = list(enumerate(GROUPS + DISTANT))
-    for index, (gx, gy, gz) in order[N_GROUPS:] + order[:N_GROUPS]:
+    order = sorted(enumerate(GROUPS + DISTANT), key=lambda item: (item[0] < N_GROUPS, -2 * (item[1][1] + item[1][2]) - abs(item[1][0])))
+    for index, (gx, gy, gz) in order:
         peer = peer_id(coords, (gz, gy, gx))
         if index < N_GROUPS:
             copies.append(pltpu.make_async_remote_copy(src_ref=send_pos, dst_ref=gat_ref.at[index], send_sem=pos_send_sem.at[index], recv_sem=pos_recv_sem.at[index], device_id=peer, device_id_type=MESH))

time: 18.5 us -> 18.5 us (level)
    pallas_call x1, Pallas kernels: 5.92 us -> 5.72 us  [local_step(): pl.pallas_call(tile_kernel, out_shape=(jax.ShapeDtypeStruct((8, WIDE), f3...]
where the time goes in v14:
time: 18.5 us; the launch traced here: 18.3 us
  Pallas kernels  17 us (92%)
  between operations  1.3 us (7%)
    pallas_call x1, Pallas kernels, local_step(): pl.pallas_call(exchange_kernel, out_shape=(jax.ShapeDtypeStruct((N_GROUPS...  9.35 us
    pallas_call x1, Pallas kernels, local_step(): pl.pallas_call(tile_kernel, out_shape=(jax.ShapeDtypeStruct((8, WIDE), f3...  5.72 us
    pallas_call x1, Pallas kernels, local_step(): pl.pallas_call(prepare_kernel, out_shape=(block_rows, block_rows, jax.Sha...  1.27 us
    pallas_call x1, Pallas kernels, local_step(): pl.pallas_call(finish_kernel, out_shape=(jax.ShapeDtypeStruct((3, CAP), f...  0.65 us

profile of v14, /device:TPU:0, one launch (start us, length us, event | category | flops | bytes accessed | tf_op | source)
XLA Modules:
  0.0 18.3 jit_solution(263855681810016195)
XLA Ops:
  1.3 9.3 %exchange.1 = (f32[12,3,6,128]{3,2,1,0:T(8,128)S(1)}, f32[15,8,128]{2,1,0:T(8,128)S(1)}, f32[16,768]{1,0:T(8,128)S(1)}) custom-call(f32[]{:T(128)S(6)} %copy.12.brick_ref, f32[3,729]{1,0:T(4,128)} %bitcast.6, f32[3,729]{1,0:T(4,128)} %bitcast.7, f32[3,729]{1,0:T(4,128)} %bitcast.8, s32[729]{0:T(1024)} %id_ref.1, s32[729]{0:T(1024)} %ok_ref.1), custom_call_target="tpu_custom_call" | custom-call | tf_op jit(solution)/shard_map/exchange/pallas_call | solution.py:563
  10.6 1.3 %prepare.1 = (f32[6,8,128]{2,1,0:T(8,128)S(1)}, f32[6,8,128]{2,1,0:T(8,128)S(1)}, f32[3,110,8,128]{3,2,1,0:T(8,128)S(1)}, f32[3,96,8,128]{3,2,1,0:T(8,128)S(1)}, f32[3,8,128]{2,1,0:T(8,128)S(1)}) custom-call(f32[12,3,6,128]{3,2,1,0:T(8,128)S(1)} %get-tuple-element.22.gat_ref, f32[15,8,128]{2,1,0:T(8,128)S(1)} %get-tuple-element.23.pkt_ref, ...), custom_call_target="tpu_custom_call" | custom-call | tf_op jit(solution)/shard_map/prepare/pallas_call | solution.py:587
  11.9 5.7 %tile.1 = (f32[8,768]{1,0:T(8,128)S(1)}, f32[1,128]{1,0:T(1,128)S(1)}) custom-call(f32[6,8,128]{2,1,0:T(8,128)S(1)} %get-tuple-element.26.rel_ref, f32[3,110,8,128]{3,2,1,0:T(8,128)S(1)} %get-tuple-element.27.others, f32[3,96,8,128]{3,2,1,0:T(8,128)S(1)} %get-tuple-element.28.part, f32[3,8,128]{2,1,0:T(8,128)S(1)} %get-tuple-element.29.eng_ref), custom_call_target="tpu_custom_call" | custom-call | tf_op jit(solution)/shard_map/tile/pallas_call | solution.py:596
  17.6 0.6 %finish.1 = (f32[3,729]{1,0:T(4,128)}, f32[3,729]{1,0:T(4,128)}, f32[3,729]{1,0:T(4,128)}, s32[729]{0:T(1024)}, s32[729]{0:T(1024)}, /*index=5*/f32[]{:T(128)}) custom-call(f32[6,8,128]{2,1,0:T(8,128)S(1)} %get-tuple-element.25.sorted_ref, f32[8,768]{1,0:T(8,128)S(1)} %get-tuple-element.30.frc_ref, f32[1,128]{1,0:T(1,128)S(1)} %get-tuple-element.31.total_ref), custom_call_target="tpu_custom_call" | custom-call | tf_op jit(solution)/shard_map/finish/pallas_call | solution.py:605
